TPU v7x, 32 devices: a whole 2x2x4 slice. The times are simulated.
32 devices in a mesh: dp: 8 (over z, x), fsdp: 4 (over y, core).
Axes of the slice: x: 2, y: 2, z: 4, core: 2. Of those that a mesh axis runs over, the one named last changes fastest.
Arguments:
- tokens: bfloat16 [16384, 768], P(('dp', 'fsdp')), may hold values from -6 to 6
- query_weight: bfloat16 [2, 768, 768], P(None, 'fsdp'), may hold values from -0.21875 to 0.21875
- key_weight: bfloat16 [2, 768, 768], P(None, 'fsdp'), may hold values from -0.21875 to 0.21875
- value_weight: bfloat16 [2, 768, 768], P(None, 'fsdp'), may hold values from -0.21875 to 0.21875
- projection: bfloat16 [2, 768, 768], P(None, 'fsdp'), may hold values from -1.75 to 1.75
- router_weight: bfloat16 [2, 768, 8], P(None, 'fsdp'), may hold values from -0.15625 to 0.15625
- attention_gain: bfloat16 [2, 768], P(None, 'fsdp'), may hold values from 0.5 to 1.5
- expert_gain: bfloat16 [2, 768], P(None, 'fsdp'), may hold values from 0.5 to 1.5
- position_bias: bfloat16 [2, 12, 32], P(None, 'fsdp'), may hold values from -4 to 4
- expert_up: bfloat16 [2, 8, 768, 3072], P(None, 'dp'), may hold values from -0.21875 to 0.21875
- expert_down: bfloat16 [2, 8, 3072, 768], P(None, 'dp'), may hold values from -0.15625 to 0.15625
- routes: int32 [16384, 2], P(('dp', 'fsdp')), may hold values from 0 to 7, all different within a row; in each aligned block of 512 rows (0 to 511, 512 to 1023, ...) at most 144 rows name the same one
- cotangent: bfloat16 [16384, 768], P(('dp', 'fsdp')), may hold values from -6 to 6
Outputs:
- output: bfloat16 [16384, 768], P(('dp', 'fsdp'))
- tokens_gradient: float32 [16384, 768], P(('dp', 'fsdp'))
- query_gradient: float32 [2, 768, 768], P(None, 'fsdp')
- key_gradient: float32 [2, 768, 768], P(None, 'fsdp')
- value_gradient: float32 [2, 768, 768], P(None, 'fsdp')
- projection_gradient: float32 [2, 768, 768], P(None, 'fsdp')
- router_gradient: float32 [2, 768, 8], P(None, 'fsdp')
- attention_gain_gradient: float32 [2, 768], P(None, 'fsdp')
- expert_gain_gradient: float32 [2, 768], P(None, 'fsdp')
- position_bias_gradient: float32 [2, 12, 32], P(None, 'fsdp')
- expert_up_gradient: float32 [2, 8, 768, 3072], P(None, 'dp', 'fsdp')
- expert_down_gradient: float32 [2, 8, 3072, 768], P(None, 'dp', 'fsdp')
Inputs may be any that keep to these rules, and one draw needn't show every extreme that they name: `routes`: each row names 2 different experts. Within the rows of one device (aligned blocks of 512 rows) no expert is named by more than 144 rows, a bound that some block reaches.
All inputs are finite; a program needn't handle non-finite values.
Results may differ from a plain program's by a relative error of at most 0.025.
Values may be sent and summed in bfloat16 or wider, within the bound.
A program may use at most 256 MiB of HBM per device.

v0:
```python
import jax
import jax.numpy as jnp
from jax import lax
from jax.sharding import PartitionSpec as P

EXP_DEV = 1
TOP = 2
BLOCK = 256
NB = 32
QBLK = 512


epsilon = 1e-06
edges = (1, 2, 3, 4, 5, 6, 7, 8, 12, 16, 24, 32, 64, 128, 256)
masked = -1000000000.0
highest = lax.Precision.HIGHEST
contract_first = (((0,), (0,)), ((), ()))
contract_last = (((1,), (1,)), ((), ()))


def norm_rows(values, gain):
    scale = lax.rsqrt(jnp.mean(values * values, axis=-1, keepdims=True) + epsilon)
    return values * scale * gain


def smooth_gate(values):
    return jax.nn.gelu(values, approximate=True)


def pair_layout(start, rows, length, block, buckets):
    queries = start + jnp.arange(rows, dtype=jnp.int32)
    places = jnp.arange(length, dtype=jnp.int32)
    offset = places[None, :] - queries[:, None]
    distance = jnp.abs(offset)
    bucket = jnp.zeros((rows, length), jnp.int32)
    for edge in edges:
        bucket = bucket + (distance >= edge).astype(jnp.int32)
    bucket = bucket + buckets // 2 * (offset > 0).astype(jnp.int32)
    allowed = places[None, :] // block <= queries[:, None] // block
    selector = (bucket[:, :, None] == jnp.arange(buckets, dtype=jnp.int32)[None, None, :]).astype(
        jnp.float32
    )
    return (selector, allowed)


def block_scores(rows, keys, bias, selector, allowed, scale):
    raw = jnp.einsum("qhe,khe->hqk", rows, keys, preferred_element_type=jnp.float32)
    table = jnp.einsum("hb,qkb->hqk", bias, selector, precision=highest)
    return jnp.where(allowed[None, :, :], scale * raw + table, masked)


def attention_forward(query, key, value, bias):
    length = query.shape[0]
    scale = query.shape[-1] ** (-0.5)
    starts = jnp.arange(length // QBLK, dtype=jnp.int32) * QBLK

    def one_block(carry, start):
        selector, allowed = pair_layout(start, QBLK, length, BLOCK, NB)
        scores = block_scores(query, key, bias, selector, allowed, scale)
        peak = jnp.max(scores, axis=-1, keepdims=True)
        lifted = jnp.exp(scores - peak)
        total = jnp.sum(lifted, axis=-1, keepdims=True)
        shares = (lifted / total).astype(jnp.bfloat16)
        mixed = jnp.einsum("hqk,khe->qhe", shares, value, preferred_element_type=jnp.float32)
        return (carry, (mixed.astype(jnp.bfloat16), peak + jnp.log(total)))

    unused, (mixed, log_total) = lax.scan(one_block, jnp.zeros((), jnp.int32), starts)
    return (mixed.reshape(length, -1), log_total)


def attention_backward(query, key, value, bias, log_total, back_mixed):
    length, heads, size = query.shape
    scale = size ** (-0.5)
    blocks = length // QBLK
    starts = jnp.arange(blocks, dtype=jnp.int32) * QBLK

    def one_block(carry, inputs):
        back_key, back_value, back_bias = carry
        start, log_part, back_part = inputs
        selector, allowed = pair_layout(start, QBLK, length, BLOCK, NB)
        scores = block_scores(query, key, bias, selector, allowed, scale)
        shares = jnp.exp(scores - log_part)
        low_shares = shares.astype(jnp.bfloat16)
        mixed = jnp.einsum("hqk,khe->qhe", low_shares, value, preferred_element_type=jnp.float32)
        back_shares = jnp.einsum(
            "qhe,khe->hqk", back_part, value, preferred_element_type=jnp.float32
        )
        back_scores = shares * (back_shares - jnp.sum(shares * back_shares, axis=-1, keepdims=True))
        back_bias = back_bias + jnp.einsum("hqk,qkb->hb", back_scores, selector, precision=highest)
        back_raw = (scale * back_scores).astype(jnp.bfloat16)
        back_rows = jnp.einsum("hqk,khe->qhe", back_raw, key, preferred_element_type=jnp.float32)
        back_key = back_key + jnp.einsum(
            "hqk,qhe->khe", back_raw, query, preferred_element_type=jnp.float32
        )
        back_value = back_value + jnp.einsum(
            "hqk,qhe->khe", low_shares, back_part, preferred_element_type=jnp.float32
        )
        return (
            (back_key, back_value, back_bias),
            (back_rows.astype(jnp.bfloat16), mixed.astype(jnp.bfloat16)),
        )

    start_carry = (
        jnp.zeros((length, heads, size), jnp.float32),
        jnp.zeros((length, heads, size), jnp.float32),
        jnp.zeros(bias.shape, jnp.float32),
    )
    back_blocks = back_mixed.reshape(blocks, QBLK, heads, size)
    (back_key, back_value, back_bias), (back_query, mixed) = lax.scan(
        one_block, start_carry, (starts, log_total, back_blocks)
    )
    return (
        back_query.reshape(length, heads * size),
        back_key.astype(jnp.bfloat16).reshape(length, heads * size),
        back_value.astype(jnp.bfloat16).reshape(length, heads * size),
        back_bias,
        mixed.reshape(length, heads * size),
    )


def plan_routes(routes, experts, capacity):
    count = routes.shape[0] * routes.shape[1]
    flat_expert = routes.reshape(count)
    selector = flat_expert[:, None] == jnp.arange(experts, dtype=jnp.int32)[None, :]
    running = jnp.cumsum(selector.astype(jnp.int32), axis=0)
    rank = jnp.sum(jnp.where(selector, running, 0), axis=1) - 1
    slot = flat_expert * capacity + rank
    anchor = (
        jnp.zeros((experts * capacity,), jnp.int32).at[slot].set(jnp.arange(count, dtype=jnp.int32))
    )
    filled = jnp.zeros((experts * capacity,), jnp.bool_).at[slot].set(True)
    route_select = routes[:, :, None] == jnp.arange(experts, dtype=jnp.int32)[None, None, :]
    return (slot, anchor, filled, route_select)


def fetch_mixer(
    layer,
    query_weight,
    key_weight,
    value_weight,
    projection,
    router_weight,
    attention_gain,
    expert_gain,
    position_bias,
):
    return (
        lax.all_gather(query_weight[layer], "fsdp", axis=0, tiled=True),
        lax.all_gather(key_weight[layer], "fsdp", axis=0, tiled=True),
        lax.all_gather(value_weight[layer], "fsdp", axis=0, tiled=True),
        lax.all_gather(projection[layer], "fsdp", axis=0, tiled=True),
        lax.all_gather(router_weight[layer], "fsdp", axis=0, tiled=True),
        lax.all_gather(attention_gain[layer], "fsdp", axis=0, tiled=True),
        lax.all_gather(expert_gain[layer], "fsdp", axis=0, tiled=True),
        lax.all_gather(position_bias[layer], "fsdp", axis=0, tiled=True),
    )


def send_rows(send, up_matrix, down_matrix):
    received = lax.all_to_all(send, "dp", split_axis=0, concat_axis=0, tiled=True)
    flat_rows = received.reshape(-1, received.shape[-1])
    inner = jnp.dot(flat_rows, up_matrix, preferred_element_type=jnp.float32)
    activity = smooth_gate(inner).astype(jnp.bfloat16)
    result = jnp.dot(activity, down_matrix, preferred_element_type=jnp.float32).astype(jnp.bfloat16)
    result, received = (result.reshape(received.shape), received)
    returned = lax.all_to_all(result, "dp", split_axis=0, concat_axis=0, tiled=True)
    return (returned, received)


def expert_inputs(middle, gain, router_full, plan, experts, capacity):
    slot, anchor, filled, route_select = plan
    width = middle.shape[1]
    normed = norm_rows(middle, gain.astype(jnp.float32)).astype(jnp.bfloat16)
    logits = jnp.dot(normed, router_full, preferred_element_type=jnp.float32)
    picked = jnp.sum(jnp.where(route_select, logits[:, None, :], 0.0), axis=-1)
    send = jnp.where(filled[:, None], normed[anchor // TOP], jnp.zeros((), jnp.bfloat16))
    return (normed, picked, send.reshape(experts, capacity, width))


def pick_routed(returned, slot, length):
    width = returned.shape[-1]
    return returned.reshape(-1, width)[slot].reshape(length, TOP, width)


def projections(hidden, mixer):
    (
        query_full,
        key_full,
        value_full,
        projection_full,
        router_full,
        gain_attention,
        gain_expert,
        bias_full,
    ) = mixer
    length = hidden.shape[0]
    heads = bias_full.shape[0]
    normed = norm_rows(hidden, gain_attention.astype(jnp.float32)).astype(jnp.bfloat16)
    query = jnp.dot(normed, query_full, preferred_element_type=jnp.float32).astype(jnp.bfloat16)
    key = jnp.dot(normed, key_full, preferred_element_type=jnp.float32).astype(jnp.bfloat16)
    value = jnp.dot(normed, value_full, preferred_element_type=jnp.float32).astype(jnp.bfloat16)
    return (
        normed,
        query.reshape(length, heads, -1),
        key.reshape(length, heads, -1),
        value.reshape(length, heads, -1),
    )


def layer_forward(hidden, mixer, up_matrix, down_matrix, plan, experts, capacity):
    (
        query_full,
        key_full,
        value_full,
        projection_full,
        router_full,
        gain_attention,
        gain_expert,
        bias_full,
    ) = mixer
    length = hidden.shape[0]
    normed, query, key, value = projections(hidden, mixer)
    mixed, log_total = attention_forward(query, key, value, bias_full.astype(jnp.float32))
    middle = hidden + jnp.dot(mixed, projection_full, preferred_element_type=jnp.float32)
    normed_expert, picked, send = expert_inputs(
        middle, gain_expert, router_full, plan, experts, capacity
    )
    returned, received = send_rows(send, up_matrix, down_matrix)
    routed = pick_routed(returned, plan[0], length)
    gates = jax.nn.softmax(picked, axis=-1)
    update = jnp.sum(gates[:, :, None] * routed.astype(jnp.float32), axis=1)
    return (middle + update, (middle, log_total, routed, received))


def layer_backward(hidden, mixer, up_matrix, down_matrix, plan, experts, capacity, kept, back_out):
    (
        query_full,
        key_full,
        value_full,
        projection_full,
        router_full,
        gain_attention,
        gain_expert,
        bias_full,
    ) = mixer
    slot, anchor, filled, route_select = plan
    length, width = hidden.shape
    middle, log_total, routed, received = kept
    normed_expert, picked, send = expert_inputs(
        middle, gain_expert, router_full, plan, experts, capacity
    )
    returned, received = send_rows(send, up_matrix, down_matrix)
    routed = pick_routed(returned, slot, length)
    gates, gate_back = jax.vjp(lambda values: jax.nn.softmax(values, axis=-1), picked)
    back_gates = jnp.sum(back_out[:, None, :] * routed.astype(jnp.float32), axis=-1)
    back_routed = (gates[:, :, None] * back_out[:, None, :]).astype(jnp.bfloat16).reshape(-1, width)
    back_slots = jnp.where(filled[:, None], back_routed[anchor], jnp.zeros((), jnp.bfloat16))
    back_received = lax.all_to_all(
        back_slots.reshape(experts, capacity, width), "dp", split_axis=0, concat_axis=0, tiled=True
    )
    flat_rows = received.reshape(-1, width)
    flat_back = back_received.reshape(-1, width)
    inner = jnp.dot(flat_rows, up_matrix, preferred_element_type=jnp.float32)
    activity, smooth_back = jax.vjp(smooth_gate, inner)
    low_activity = activity.astype(jnp.bfloat16)
    back_activity = lax.dot_general(
        flat_back, down_matrix, contract_last, preferred_element_type=jnp.float32
    )
    back_inner = smooth_back(back_activity)[0].astype(jnp.bfloat16)
    down_change = lax.dot_general(
        low_activity, flat_back, contract_first, preferred_element_type=jnp.float32
    )
    up_change = lax.dot_general(
        flat_rows, back_inner, contract_first, preferred_element_type=jnp.float32
    )
    back_rows = lax.dot_general(
        back_inner, up_matrix, contract_last, preferred_element_type=jnp.float32
    )
    back_returned = lax.all_to_all(
        back_rows.astype(jnp.bfloat16).reshape(received.shape),
        "dp",
        split_axis=0,
        concat_axis=0,
        tiled=True,
    )
    back_expert = jnp.sum(pick_routed(back_returned, slot, length).astype(jnp.float32), axis=1)
    back_picked = gate_back(back_gates)[0]
    back_logits = jnp.sum(jnp.where(route_select, back_picked[:, :, None], 0.0), axis=1).astype(
        jnp.bfloat16
    )
    router_change = lax.dot_general(
        normed_expert, back_logits, contract_first, preferred_element_type=jnp.float32
    )
    back_expert = back_expert + lax.dot_general(
        back_logits, router_full, contract_last, preferred_element_type=jnp.float32
    )
    unused, expert_norm_back = jax.vjp(norm_rows, middle, gain_expert.astype(jnp.float32))
    back_middle, expert_gain_change = expert_norm_back(back_expert)
    back_middle = back_middle + back_out
    normed, query, key, value = projections(hidden, mixer)
    back_attended = back_middle.astype(jnp.bfloat16)
    back_mixed = lax.dot_general(
        back_attended, projection_full, contract_last, preferred_element_type=jnp.float32
    ).astype(jnp.bfloat16)
    back_query, back_key, back_value, bias_change, mixed = attention_backward(
        query, key, value, bias_full.astype(jnp.float32), log_total, back_mixed
    )
    projection_change = lax.dot_general(
        mixed, back_attended, contract_first, preferred_element_type=jnp.float32
    )
    query_change = lax.dot_general(
        normed, back_query, contract_first, preferred_element_type=jnp.float32
    )
    key_change = lax.dot_general(
        normed, back_key, contract_first, preferred_element_type=jnp.float32
    )
    value_change = lax.dot_general(
        normed, back_value, contract_first, preferred_element_type=jnp.float32
    )
    back_normed = lax.dot_general(
        back_query, query_full, contract_last, preferred_element_type=jnp.float32
    )
    back_normed = back_normed + lax.dot_general(
        back_key, key_full, contract_last, preferred_element_type=jnp.float32
    )
    back_normed = back_normed + lax.dot_general(
        back_value, value_full, contract_last, preferred_element_type=jnp.float32
    )
    unused, attention_norm_back = jax.vjp(norm_rows, hidden, gain_attention.astype(jnp.float32))
    back_hidden, attention_gain_change = attention_norm_back(back_normed)
    back_hidden = back_hidden + back_middle
    mixer_changes = (
        query_change,
        key_change,
        value_change,
        projection_change,
        router_change,
        attention_gain_change,
        expert_gain_change,
        bias_change,
    )
    return (back_hidden, mixer_changes, (up_change, down_change))


def per_device(
    tokens,
    query_weight,
    key_weight,
    value_weight,
    projection,
    router_weight,
    attention_gain,
    expert_gain,
    position_bias,
    expert_up,
    expert_down,
    routes,
    cotangent,
):
    layers = query_weight.shape[0]
    length = tokens.shape[0]
    experts = lax.axis_size("dp") * EXP_DEV
    capacity = max(2, 9 * length * TOP // (8 * experts))
    plan = plan_routes(routes, experts, capacity)
    weights = (
        query_weight,
        key_weight,
        value_weight,
        projection,
        router_weight,
        attention_gain,
        expert_gain,
        position_bias,
    )
    hidden = tokens.astype(jnp.float32)
    inputs = []
    saved = []
    copies = []
    for layer in range(layers):
        mixer = fetch_mixer(layer, *weights)
        inputs.append(hidden)
        copies.append(mixer)
        hidden, kept = layer_forward(
            hidden, mixer, expert_up[layer, 0], expert_down[layer, 0], plan, experts, capacity
        )
        saved.append(kept)
    output = hidden.astype(jnp.bfloat16)
    back = cotangent.astype(jnp.float32)
    mixer_results = [None] * layers
    expert_results = [None] * layers
    for layer in range(layers - 1, -1, -1):
        mixer = fetch_mixer(layer, *weights)
        back, mixer_changes, expert_changes = layer_backward(
            inputs[layer],
            mixer,
            expert_up[layer, 0],
            expert_down[layer, 0],
            plan,
            experts,
            capacity,
            saved[layer],
            back,
        )
        (
            query_change,
            key_change,
            value_change,
            projection_change,
            router_change,
            attention_gain_change,
            expert_gain_change,
            bias_change,
        ) = mixer_changes
        shards = (
            lax.psum_scatter(
                query_change.astype(jnp.bfloat16), "fsdp", scatter_dimension=0, tiled=True
            ).astype(jnp.float32),
            lax.psum_scatter(
                key_change.astype(jnp.bfloat16), "fsdp", scatter_dimension=0, tiled=True
            ).astype(jnp.float32),
            lax.psum_scatter(
                value_change.astype(jnp.bfloat16), "fsdp", scatter_dimension=0, tiled=True
            ).astype(jnp.float32),
            lax.psum_scatter(
                projection_change.astype(jnp.bfloat16), "fsdp", scatter_dimension=0, tiled=True
            ).astype(jnp.float32),
            lax.psum_scatter(
                router_change.astype(jnp.bfloat16), "fsdp", scatter_dimension=0, tiled=True
            ).astype(jnp.float32),
            lax.psum_scatter(
                attention_gain_change.astype(jnp.bfloat16), "fsdp", scatter_dimension=0, tiled=True
            ).astype(jnp.float32),
            lax.psum_scatter(
                expert_gain_change.astype(jnp.bfloat16), "fsdp", scatter_dimension=0, tiled=True
            ).astype(jnp.float32),
            lax.psum_scatter(
                bias_change.astype(jnp.bfloat16), "fsdp", scatter_dimension=0, tiled=True
            ).astype(jnp.float32),
        )
        (
            query_shard,
            key_shard,
            value_shard,
            projection_shard,
            router_shard,
            attention_gain_shard,
            expert_gain_shard,
            bias_shard,
        ) = shards
        mixer_results[layer] = lax.psum(
            (
                query_shard,
                key_shard,
                value_shard,
                projection_shard,
                router_shard,
                attention_gain_shard,
                expert_gain_shard,
                bias_shard,
            ),
            "dp",
        )
        up_change, down_change = expert_changes
        expert_results[layer] = (
            lax.psum_scatter(
                up_change.astype(jnp.bfloat16), "fsdp", scatter_dimension=0, tiled=True
            ).astype(jnp.float32),
            lax.psum_scatter(
                down_change.astype(jnp.bfloat16), "fsdp", scatter_dimension=0, tiled=True
            ).astype(jnp.float32),
        )
    stacked = [
        jnp.stack([mixer_results[layer][member] for layer in range(layers)]) for member in range(8)
    ]
    up_stack = jnp.stack([expert_results[layer][0] for layer in range(layers)])[:, None]
    down_stack = jnp.stack([expert_results[layer][1] for layer in range(layers)])[:, None]
    return (
        output,
        back,
        stacked[0],
        stacked[1],
        stacked[2],
        stacked[3],
        stacked[4],
        stacked[5],
        stacked[6],
        stacked[7],
        up_stack,
        down_stack,
    )


def solution(mesh):
    return jax.shard_map(
        per_device,
        mesh=mesh,
        in_specs=(
            P(("dp", "fsdp"), None),
            P(None, "fsdp", None),
            P(None, "fsdp", None),
            P(None, "fsdp", None),
            P(None, "fsdp", None),
            P(None, "fsdp", None),
            P(None, "fsdp"),
            P(None, "fsdp"),
            P(None, "fsdp", None),
            P(None, "dp", None, None),
            P(None, "dp", None, None),
            P(("dp", "fsdp"), None),
            P(("dp", "fsdp"), None),
        ),
        out_specs=(
            P(("dp", "fsdp"), None),
            P(("dp", "fsdp"), None),
            P(None, "fsdp", None),
            P(None, "fsdp", None),
            P(None, "fsdp", None),
            P(None, "fsdp", None),
            P(None, "fsdp", None),
            P(None, "fsdp"),
            P(None, "fsdp"),
            P(None, "fsdp", None),
            P(None, "dp", "fsdp", None),
            P(None, "dp", "fsdp", None),
        ),
        check_vma=False,
    )
```

profile of v0, /device:TPU:0, one launch (start us, length us, event | category | flops | bytes accessed | tf_op | source)
XLA Modules:
  0.0 1242.0 jit_solution(1515575596061935497)
XLA Ops:
  57.4 12.4 all-gather.27.cloned.1.call-done
  74.2 15.3 %fusion.210 = (f32[12,512]{1,0:T(8,128)S(1)}, f32[12,512,512]{1,2,0:T(8,128)S(1)}) fusion(f32[512,512,12]{0,2,1:T(8,128)} %fusion.3, bf16[512,12,64]{0,2,1:T(8,128)(2,1)S(1)} %bitcast.320, bf16[512,12,64]{0,2,1:T(8,128)(2,1)S(1)} %bitcast.315, pred[512,512]{0,1:T(8,128)(4,1)S(1)} %broadcast_compare_fusion), kind=kOutput, calls=%fused_computation.346 | convolution fusion | flops 415229952 | bytes 27025408 | tf_op jit(solution)/shard_map/while/body/eval_jaxpr/qhe,khe->hqk/dot_general | solution.py:47
  113.1 40.3 %all-to-all-done = bf16[8,144,768]{2,1,0:T(8,128)(2,1)S(1)} async-done(((bf16[8,144,768]{2,1,0:T(8,128)(2,1)}), bf16[8,144,768]{2,1,0:T(8,128)(2,1)S(1)}, u32[]{:S(2)}, u32[]{:S(2)}) %all-to-all-start) | async-done | bytes 1769504 | tf_op jit(solution)/shard_map/all_to_all | solution.py:160
  161.6 15.4 %fusion.57 = bf16[1152,768]{1,0:T(8,128)(2,1)} fusion(bf16[2,1,3072,768]{3,2,1,0:T(8,128)(2,1)} %param.23, f32[1152,3072]{1,0:T(8,128)S(1)} %fusion.44), kind=kOutput, calls=%fused_computation.90 | convolution fusion | flops 5468553216 | bytes 20643840 | tf_op jit(solution)/shard_map/dot_general | solution.py:164
  191.4 9.6 all-gather.15
  215.0 9.8 fusion.2
  236.2 14.9 %multiply_reduce_fusion.5 = f32[512,768]{1,0:T(8,128)S(1)} fusion(f32[512,2,768]{2,1,0:T(2,128)S(1)} %reshape.753, f32[512,2]{1,0:T(8,128)S(1)} %copy.213), kind=kLoop, calls=%fused_computation.98 | loop fusion | flops 1179648 | bytes 4722688 | tf_op jit(solution)/shard_map/reduce_sum | solution.py:231
  260.0 15.1 %fusion.211 = (f32[12,512]{1,0:T(8,128)S(1)}, f32[12,512,512]{1,2,0:T(8,128)S(1)}) fusion(f32[512,512,12]{0,2,1:T(8,128)} %fusion.2, bf16[512,12,64]{0,2,1:T(8,128)(2,1)S(1)} %bitcast.324, bf16[512,12,64]{0,2,1:T(8,128)(2,1)S(1)} %bitcast.322, pred[512,512]{0,1:T(8,128)(4,1)S(1)} %copy-done.44), kind=kOutput, calls=%fused_computation.347 | convolution fusion | flops 415229952 | bytes 27025408 | tf_op jit(solution)/shard_map/while/body/eval_jaxpr/qhe,khe->hqk/dot_general | solution.py:47
  311.2 47.8 %all_to_all.44 = bf16[8,144,768]{2,1,0:T(8,128)(2,1)} all-to-all(bf16[8,144,768]{2,1,0:T(8,128)(2,1)S(1)} %get-tuple-element.255), channel_id=1, replica_groups=mesh['dp'=8,'fsdp'=4] {'dp'}, dimensions={0} | all-to-all | bytes 3538944 | tf_op jit(solution)/shard_map/all_to_all | solution.py:160
  376.0 11.8 fusion.63
  387.8 16.2 %all-to-all-done.4 = bf16[8,144,768]{2,1,0:T(8,128)(2,1)} async-done(((bf16[8,144,768]{2,1,0:T(8,128)(2,1)}), bf16[8,144,768]{2,1,0:T(8,128)(2,1)}, u32[]{:S(2)}, u32[]{:S(2)}) %all-to-all-start.4) | async-done | bytes 1769504 | tf_op jit(solution)/shard_map/all_to_all | solution.py:258
  408.1 16.6 %fusion.23 = bf16[1152,3072]{1,0:T(8,128)(2,1)S(1)} fusion(f32[1152,3072]{1,0:T(8,128)} %copy-done.123, bf16[1152,768]{1,0:T(8,128)(2,1)} %bitcast.39, bf16[2,1,3072,768]{3,2,1,0:T(8,128)(2,1)} %param.23), kind=kOutput, calls=%fused_computation.38 | convolution fusion | flops 5506596864 | bytes 27721728 | tf_op jit(solution)/shard_map/dot_general | solution.py:266
  427.6 9.3 fusion.60
  436.9 12.2 all-to-all-done.3
  477.3 9.6 multiply_reduce_fusion.3
  526.6 9.0 multiply_reduce_fusion.1
  588.6 34.5 %all-to-all-done.6 = bf16[8,144,768]{2,1,0:T(8,128)(2,1)} async-done(((bf16[8,144,768]{2,1,0:T(8,128)(2,1)}), bf16[8,144,768]{2,1,0:T(8,128)(2,1)}, u32[]{:S(2)}, u32[]{:S(2)}) %all-to-all-start.6) | async-done | bytes 1769504 | tf_op jit(solution)/shard_map/all_to_all | solution.py:258
  623.0 16.6 %fusion.16 = bf16[1152,3072]{1,0:T(8,128)(2,1)S(1)} fusion(f32[1152,3072]{1,0:T(8,128)} %copy-done.122, bf16[1152,768]{1,0:T(8,128)(2,1)} %bitcast.50, bf16[2,1,3072,768]{3,2,1,0:T(8,128)(2,1)} %param.23), kind=kOutput, calls=%fused_computation.31 | convolution fusion | flops 5506596864 | bytes 27721728 | tf_op jit(solution)/shard_map/dot_general | solution.py:266
  639.6 12.0 fusion.54
  670.5 26.1 %all-to-all-done.7 = bf16[8,144,768]{2,1,0:T(8,128)(2,1)S(1)} async-done(((bf16[8,144,768]{2,1,0:T(8,128)(2,1)}), bf16[8,144,768]{2,1,0:T(8,128)(2,1)S(1)}, u32[]{:S(2)}, u32[]{:S(2)}) %all-to-all-start.7) | async-done | bytes 1769504 | tf_op jit(solution)/shard_map/all_to_all | solution.py:279
  762.4 13.2 %convolution_convert_fusion = bf16[3072,768]{1,0:T(8,128)(2,1)} fusion(bf16[1152,768]{1,0:T(8,128)(2,1)} %bitcast.39, f32[1152,3072]{1,0:T(8,128)} %copy-done.123), kind=kOutput, calls=%fused_computation.63 | convolution fusion | flops 5470027776 | bytes 20643840 | tf_op jit(solution)/shard_map/dot_general | solution.py:270
  775.7 13.3 %convolution_convert_fusion.1 = bf16[3072,768]{1,0:T(8,128)(2,1)} fusion(bf16[1152,768]{1,0:T(8,128)(2,1)} %bitcast.50, f32[1152,3072]{1,0:T(8,128)} %copy-done.122), kind=kOutput, calls=%fused_computation.64 | convolution fusion | flops 5470027776 | bytes 20643840 | tf_op jit(solution)/shard_map/dot_general | solution.py:270
  790.5 10.9 convolution_convert_fusion.2
  802.9 10.9 convolution_convert_fusion.3
  815.1 24.5 %fusion.134 = bf16[12,32]{1,0:T(8,128)(2,1)S(1)} fusion(s32[512,512]{0,1:T(8,128)S(1)} %copy-done.8, f32[12,512,512]{1,2,0:T(8,128)} %copy-done.2), kind=kOutput, calls=%fused_computation.206 | convolution fusion | flops 1216348544 | bytes 13632256 | tf_op jit(solution)/shard_map/while/body/eval_jaxpr/hqk,qkb->hb/dot_general | solution.py:89
  862.8 25.4 %fusion.137 = bf16[12,32]{1,0:T(8,128)(2,1)S(1)} fusion(s32[512,512]{0,1:T(8,128)S(1)} %copy-done.8, f32[12,512,512]{1,2,0:T(8,128)} %copy-done.3), kind=kOutput, calls=%fused_computation.207 | convolution fusion | flops 1216348544 | bytes 13632256 | tf_op jit(solution)/shard_map/while/body/eval_jaxpr/hqk,qkb->hb/dot_general | solution.py:89
  888.3 11.8 all-reduce.12
  900.4 35.7 %all-reduce.10 = (f32[1,192,8]{1,2,0:T(8,128)S(1)}, f32[1,192,8]{1,2,0:T(8,128)S(1)}, f32[1,192]{1,0:T(1,128)S(1)}, f32[1,192]{1,0:T(1,128)S(1)}, f32[1,192]{1,0...) all-reduce(f32[1,192,8]{1,2,0:T(8,128)S(1)} %bitcast_convert_fusion, ...), channel_id=1, replica_groups=mesh['dp'=8,'fsdp'=4] {'dp'}, use_global_device_ids=true, to_apply=%region_54.55 | all-reduce | flops 4032 | bytes 32256 | tf_op jit(solution)/shard_map/psum | solution.py:450
  941.5 11.0 reduce-scatter.39.cloned.1.call-done
  956.6 47.0 %reduce-scatter.37.cloned.1.call-done = bf16[192,3072]{1,0:T(8,128)(2,1)} async-done(((bf16[768,3072]{1,0:T(8,128)(2,1)}), bf16[192,3072]{1,0:T(8,128)(2,1)}) %reduce-scatter.37.cloned.1.call-update) | async-done | bytes 1179664 | tf_op jit(solution)/shard_map/reduce_scatter | solution.py:465
  1003.6 50.5 %reduce-scatter.35.cloned.1.call-done = bf16[192,3072]{1,0:T(8,128)(2,1)} async-done(((bf16[768,3072]{1,0:T(8,128)(2,1)}), bf16[192,3072]{1,0:T(8,128)(2,1)}) %reduce-scatter.35.cloned.1.call-update) | async-done | bytes 1179664 | tf_op jit(solution)/shard_map/reduce_scatter | solution.py:465
  1058.2 170.8 %all-reduce.16.cloned.1.call-done = (f32[1,192,768]{2,1,0:T(8,128)}, f32[1,192,768]{2,1,0:T(8,128)}, f32[1,192,768]{2,1,0:T(8,128)}, f32[1,192,768]{2,1,0:T(8,12...) async-done(((f32[1,192,768]{2,1,0:T(8,128)}, f32[1,192,768]{2,1,0:T(8,128)}, f32[1,192,768]{2,1,0:T(8,128)}, ...) | async-done | bytes 4718608 | tf_op jit(solution)/shard_map/psum | solution.py:450
  (537 shorter events, 444.8 us)
Async XLA Ops:
  7.2 45.1 %all-gather.25.cloned.1.call-start = ((), (), s32[]{:S(2)}) async-start(), calls=%async_computation.34 | async-start | bytes 1474560 | tf_op jit(solution)/shard_map/all_gather | solution.py:150
  9.3 45.5 %all-gather.29.cloned.1.call-start = ((), (), s32[]{:S(2)}) async-start(), calls=%async_computation.36 | async-start | bytes 1474560 | tf_op jit(solution)/shard_map/all_gather | solution.py:149
  10.2 59.6 %all-gather.27.cloned.1.call-start = ((), (), s32[]{:S(2)}) async-start(), calls=%async_computation.35 | async-start | bytes 1474560 | tf_op jit(solution)/shard_map/all_gather | solution.py:148
  11.2 85.5 %all-gather.31.cloned.1.call-start = ((), (), s32[]{:S(2)}) async-start(), calls=%async_computation.37 | async-start | bytes 1474560 | tf_op jit(solution)/shard_map/all_gather | solution.py:151
  12.1 239.5 %all-gather.37.cloned.1.call-start = ((), (), s32[]{:S(2)}) async-start(), calls=%async_computation.40 | async-start | bytes 1474560 | tf_op jit(solution)/shard_map/all_gather | solution.py:149
  100.3 124.5 %copy-start.4 = (bf16[512,768]{1,0:T(8,128)(2,1)}, bf16[512,768]{1,0:T(8,128)(2,1)S(1)}, u32[]{:S(2)}) copy-start(bf16[512,768]{1,0:T(8,128)(2,1)S(1)} %multiply_convert_fusion.12) | copy-start | bytes 2359300
  106.3 47.1 %all-to-all-start = ((bf16[8,144,768]{2,1,0:T(8,128)(2,1)}), bf16[8,144,768]{2,1,0:T(8,128)(2,1)S(1)}, u32[]{:S(2)}, u32[]{:S(2)}) async-start(bf16[8,144,768]{2,1,0:T(8,128)(2,1)} %broadcast_select_fusion.3), calls=%async_computation | async-start | bytes 3538944 | tf_op jit(solution)/shard_map/all_to_all | solution.py:160
  111.8 143.3 %all-gather.35.cloned.1.call-start = ((), (), s32[]{:S(2)}) async-start(), calls=%async_computation.39 | async-start | bytes 1474560 | tf_op jit(solution)/shard_map/all_gather | solution.py:148
  112.4 169.0 %all-gather.33.cloned.1.call-start = ((), (), s32[]{:S(2)}) async-start(), calls=%async_computation.38 | async-start | bytes 1474560 | tf_op jit(solution)/shard_map/all_gather | solution.py:150
  177.0 48.4 %all-to-all-start.1 = ((bf16[8,144,768]{2,1,0:T(8,128)(2,1)}), bf16[8,144,768]{2,1,0:T(8,128)(2,1)S(1)}, u32[]{:S(2)}, u32[]{:S(2)}) async-start(bf16[8,144,768]{2,1,0:T(8,128)(2,1)} %bitcast.347), calls=%async_computation.1 | async-start | bytes 3538944 | tf_op jit(solution)/shard_map/all_to_all | solution.py:166
  180.8 109.8 %all-gather.39.cloned.1.call-start = ((), (), s32[]{:S(2)}) async-start(), calls=%async_computation.41 | async-start | bytes 1474560 | tf_op jit(solution)/shard_map/all_gather | solution.py:151
  358.9 45.1 %all-to-all-start.4 = ((bf16[8,144,768]{2,1,0:T(8,128)(2,1)}), bf16[8,144,768]{2,1,0:T(8,128)(2,1)}, u32[]{:S(2)}, u32[]{:S(2)}) async-start(bf16[8,144,768]{2,1,0:T(8,128)(2,1)} %get-tuple-element.254), calls=%async_computation.4 | async-start | bytes 3538944 | tf_op jit(solution)/shard_map/all_to_all | solution.py:258
  404.0 45.0 %all-to-all-start.3 = ((bf16[8,144,768]{2,1,0:T(8,128)(2,1)}), bf16[8,144,768]{2,1,0:T(8,128)(2,1)S(1)}, u32[]{:S(2)}, u32[]{:S(2)}) async-start(bf16[8,144,768]{2,1,0:T(8,128)(2,1)} %bitcast.350), calls=%async_computation.3 | async-start | bytes 3538944 | tf_op jit(solution)/shard_map/all_to_all | solution.py:166
  450.3 45.0 %all-to-all-start.5 = ((bf16[8,144,768]{2,1,0:T(8,128)(2,1)}), bf16[8,144,768]{2,1,0:T(8,128)(2,1)S(1)}, u32[]{:S(2)}, u32[]{:S(2)}) async-start(bf16[8,144,768]{2,1,0:T(8,128)(2,1)} %bitcast.348), calls=%async_computation.5 | async-start | bytes 3538944 | tf_op jit(solution)/shard_map/all_to_all | solution.py:279
  453.9 385.7 %reduce-scatter.45.cloned.1.call-start = ((), (), s32[]{:S(2)}) async-start(), calls=%async_computation.43 | async-start | bytes 245760
  550.5 290.0 %reduce-scatter.33.cloned.1.call-start = ((), (), s32[]{:S(2)}) async-start(), calls=%async_computation.29 | async-start | bytes 1474560 | tf_op jit(solution)/shard_map/reduce_scatter | solution.py:424
  577.7 45.3 %all-to-all-start.6 = ((bf16[8,144,768]{2,1,0:T(8,128)(2,1)}), bf16[8,144,768]{2,1,0:T(8,128)(2,1)}, u32[]{:S(2)}, u32[]{:S(2)}) async-start(bf16[8,144,768]{2,1,0:T(8,128)(2,1)} %broadcast_select_fusion), calls=%async_computation.6 | async-start | bytes 3538944 | tf_op jit(solution)/shard_map/all_to_all | solution.py:258
  582.2 260.1 %reduce-scatter.29.cloned.1.call-start = ((), (), s32[]{:S(2)}) async-start(), calls=%async_computation.27 | async-start | bytes 1474560 | tf_op jit(solution)/shard_map/reduce_scatter | solution.py:421
  585.3 258.8 %reduce-scatter.21.cloned.1.call-start = ((), (), s32[]{:S(2)}) async-start(), calls=%async_computation.23 | async-start | bytes 1474560 | tf_op jit(solution)/shard_map/reduce_scatter | solution.py:415
  651.6 45.0 %all-to-all-start.7 = ((bf16[8,144,768]{2,1,0:T(8,128)(2,1)}), bf16[8,144,768]{2,1,0:T(8,128)(2,1)S(1)}, u32[]{:S(2)}, u32[]{:S(2)}) async-start(bf16[8,144,768]{2,1,0:T(8,128)(2,1)} %bitcast.349), calls=%async_computation.7 | async-start | bytes 3538944 | tf_op jit(solution)/shard_map/all_to_all | solution.py:279
  655.4 190.6 %reduce-scatter.25.cloned.1.call-start = ((), (), s32[]{:S(2)}) async-start(), calls=%async_computation.25 | async-start | bytes 1474560 | tf_op jit(solution)/shard_map/reduce_scatter | solution.py:418
  658.7 189.1 %reduce-scatter.31.cloned.1.call-start = ((), (), s32[]{:S(2)}) async-start(), calls=%async_computation.28 | async-start | bytes 1474560 | tf_op jit(solution)/shard_map/reduce_scatter | solution.py:424
  719.2 130.4 %reduce-scatter.27.cloned.1.call-start = ((), (), s32[]{:S(2)}) async-start(), calls=%async_computation.26 | async-start | bytes 1474560 | tf_op jit(solution)/shard_map/reduce_scatter | solution.py:421
  732.3 119.1 %reduce-scatter.23.cloned.1.call-start = ((), (), s32[]{:S(2)}) async-start(), calls=%async_computation.24 | async-start | bytes 1474560 | tf_op jit(solution)/shard_map/reduce_scatter | solution.py:418
  753.0 100.2 %reduce-scatter.19.cloned.1.call-start = ((), (), s32[]{:S(2)}) async-start(), calls=%async_computation.22 | async-start | bytes 1474560 | tf_op jit(solution)/shard_map/reduce_scatter | solution.py:415
  761.0 94.1 %reduce-scatter.43.cloned.1.call-start = ((), (), s32[]{:S(2)}) async-start(), calls=%async_computation.42 | async-start | bytes 245760
  762.2 179.3 %reduce-scatter.41.cloned.1.call-start = ((), (), s32[]{:S(2)}) async-start(), calls=%async_computation.33 | async-start | bytes 5898240 | tf_op jit(solution)/shard_map/reduce_scatter | solution.py:468
  775.7 176.8 %reduce-scatter.39.cloned.1.call-start = ((), (), s32[]{:S(2)}) async-start(), calls=%async_computation.32 | async-start | bytes 5898240 | tf_op jit(solution)/shard_map/reduce_scatter | solution.py:468
  789.0 214.5 %reduce-scatter.37.cloned.1.call-start = ((), (), s32[]{:S(2)}) async-start(), calls=%async_computation.31 | async-start | bytes 5898240 | tf_op jit(solution)/shard_map/reduce_scatter | solution.py:465
  801.4 252.7 %reduce-scatter.35.cloned.1.call-start = ((), (), s32[]{:S(2)}) async-start(), calls=%async_computation.30 | async-start | bytes 5898240 | tf_op jit(solution)/shard_map/reduce_scatter | solution.py:465
  813.8 415.2 %all-reduce.16.cloned.1.call-start = ((), (), s32[]{:S(2)}) async-start(), calls=%async_computation.44 | async-start | bytes 9437184 | tf_op jit(solution)/shard_map/psum | solution.py:450
  862.8 75.7 %copy-start.19 = (f32[512,768]{1,0:T(8,128)S(1)}, f32[512,768]{1,0:T(8,128)}, u32[]{:S(2)}) copy-start(f32[512,768]{1,0:T(8,128)} %copy-done.18) | copy-start | bytes 4718596
  (125 other events, 1232.7 us)
Sparse Core Ops, SparseCore 0:
  10.1 20.2 all-gather.24
  32.6 17.5 all-gather.28
  52.4 17.4 all-gather.26
  71.8 17.4 all-gather.30
  91.3 17.4 all-gather.36
  114.4 17.8 all-gather.34
  134.5 17.4 all-gather.32
  183.1 19.9 all-gather.38
  550.6 18.1 reduce-scatter.44
  571.2 25.5 reduce-scatter.32
  599.4 25.5 reduce-scatter.28
  628.0 25.5 reduce-scatter.20
  659.3 26.1 reduce-scatter.24
  719.3 23.9 reduce-scatter.30
  745.7 25.6 reduce-scatter.26
  774.3 25.6 reduce-scatter.22
  803.0 25.6 reduce-scatter.18
  830.9 19.7 reduce-scatter.42
  853.8 48.2 reduce-scatter.40
  904.5 47.9 reduce-scatter.38
  955.6 47.9 reduce-scatter.36
  1006.1 47.9 reduce-scatter.34
  1059.2 169.8 all-reduce.15
where the time goes:
time: 1250 us; the launch traced here: 1240 us
  waiting for transfers between devices  431 us (34%)
  matrix products  370 us (30%)
  local copies, waits for them, and re-layouts  146 us (12%)
  blocking collectives  131 us (10%)
  other arithmetic  114 us (9%)
  starting transfers between devices  32 us (3%)
  between operations  18.1 us (1%)
    psum x1, waiting for transfers between devices, per_device(): lax.psum((query_shard, key_shard, value_shard, projection_shard, router_s...  171 us
    reduce_scatter x2, waiting for transfers between devices, per_device(): lax.psum_scatter(up_change.astype(jnp.bfloat16), 'fsdp', scatter_dimensio...  97.5 us
    all_to_all x2, waiting for transfers between devices, layer_backward(): lax.all_to_all(back_slots.reshape(experts, capacity, width), 'dp', split_...  50.6 us
    dot_general x2, matrix products, one_block(): jnp.einsum('hqk,qkb->hb', back_scores, selector, precision=highest)  49.9 us
    all_to_all x1, blocking collectives, send_rows(): lax.all_to_all(send, 'dp', split_axis=0, concat_axis=0, tiled=True)  47.8 us
    unnamed x271, local copies, waits for them, and re-layouts  43.4 us
    all_to_all x1, waiting for transfers between devices, send_rows(): lax.all_to_all(send, 'dp', split_axis=0, concat_axis=0, tiled=True)  40.3 us
    psum x1, blocking collectives, per_device(): lax.psum((query_shard, key_shard, value_shard, projection_shard, router_s...  35.7 us
  transfers between devices with their start and end apart: 30, of which 11 were waited for; matrix products, arithmetic and copies ran while one was open for 41% of the time, Pallas kernels for 0%

commit v1 on v0

v1 whole, which is shorter than its diff:
```python
import functools

import jax
import jax.numpy as jnp
from jax import lax
from jax.experimental import pallas as pl
from jax.experimental.pallas import tpu as pltpu
from jax.sharding import PartitionSpec as P

EXP_DEV = 1
TOP = 2
BLOCK = 256
NB = 32
LANES = 128


epsilon = 1e-06
edges = (1, 2, 3, 4, 5, 6, 7, 8, 12, 16, 24, 32, 64, 128, 256)
highest = lax.Precision.HIGHEST
contract_first = (((0,), (0,)), ((), ()))
contract_last = (((1,), (1,)), ((), ()))
root = 0.7978845608028654
cubic = 0.044715


def dot(left, right):
    return jnp.dot(left, right, preferred_element_type=jnp.float32)


def dot_last(left, right):
    return lax.dot_general(left, right, contract_last, preferred_element_type=jnp.float32)


def dot_first(left, right):
    return lax.dot_general(left, right, contract_first, preferred_element_type=jnp.float32)


def low(values):
    return values.astype(jnp.bfloat16)


def row_scale(values):
    return lax.rsqrt(jnp.mean(values * values, axis=-1, keepdims=True) + epsilon)


def norm_back(values, scale, gain, back):
    lifted = back * gain
    inner = jnp.mean(lifted * values, axis=-1, keepdims=True)
    rows = scale * lifted - scale * scale * scale * values * inner
    return rows, jnp.sum(back * values * scale, axis=0)


def smooth_pair(values):
    tail = jnp.tanh(root * (values + cubic * values * values * values))
    half = 0.5 * (1.0 + tail)
    slope = half + 0.5 * values * (1.0 - tail * tail) * root * (1.0 + 3.0 * cubic * values * values)
    return values * half, slope


def offset_selector(length):
    offset = jnp.arange(2 * length, dtype=jnp.int32) - (length - 1)
    distance = jnp.abs(offset)
    bucket = jnp.zeros_like(offset)
    for edge in edges:
        bucket = bucket + (distance >= edge).astype(jnp.int32)
    bucket = bucket + NB // 2 * (offset > 0).astype(jnp.int32)
    return (bucket[:, None] == jnp.arange(NB, dtype=jnp.int32)[None, :]).astype(jnp.float32)


def lane_of(half, heads):
    lanes = lax.broadcasted_iota(jnp.int32, (1, LANES), 1)
    size = LANES // heads
    return (lanes >= half * size) & (lanes < (half + 1) * size)


def bias_tile(table, start, block, keys):
    span = table.shape[1]
    length = span // 2
    spread = jnp.broadcast_to(table, (block, span))
    shift = (start - (length - 1)) % span
    return pltpu.roll(spread, shift, 1, stride=1, stride_axis=0)[:, :keys]


def attend(pair, scale, q_ref, k_ref, v_ref, table_ref, mixed_ref, log_ref):
    length = q_ref.shape[0]
    for start in range(0, length, BLOCK):
        keys = start + BLOCK
        rows = pl.ds(start, BLOCK)
        query = q_ref[rows, :]
        key = k_ref[pl.ds(0, keys), :]
        value = v_ref[pl.ds(0, keys), :]
        mixed = None
        for half in range(pair):
            lane = lane_of(half, pair)
            table = table_ref[0, half : half + 1, :]
            raw = dot_last(jnp.where(lane, query, jnp.zeros_like(query)), key)
            scores = scale * raw + bias_tile(table, start, BLOCK, keys)
            peak = jnp.max(scores, axis=-1, keepdims=True)
            lifted = jnp.exp(scores - peak)
            total = jnp.sum(lifted, axis=-1, keepdims=True)
            shares = low(lifted * (1.0 / total))
            part = dot(shares, value)
            tops = jnp.broadcast_to(peak + jnp.log(total), part.shape)
            mixed = part if mixed is None else jnp.where(lane, part, mixed)
            logs = tops if half == 0 else jnp.where(lane, tops, logs)
        mixed_ref[rows, :] = low(mixed)
        log_ref[rows, :] = logs


def attend_back(
    pair,
    scale,
    q_ref,
    k_ref,
    v_ref,
    table_ref,
    log_ref,
    back_ref,
    dq_ref,
    dk_ref,
    dv_ref,
    sums_ref,
    key_sum,
    value_sum,
):
    length = q_ref.shape[0]
    size = LANES // pair
    span = 2 * length
    order = list(range(0, length, BLOCK))[::-1]
    for turn, start in enumerate(order):
        keys = start + BLOCK
        rows = pl.ds(start, BLOCK)
        query = q_ref[rows, :]
        back = back_ref[rows, :]
        key = k_ref[pl.ds(0, keys), :]
        value = v_ref[pl.ds(0, keys), :]
        back_query = None
        for half in range(pair):
            lane = lane_of(half, pair)
            table = table_ref[0, half : half + 1, :]
            query_half = jnp.where(lane, query, jnp.zeros_like(query))
            back_half = jnp.where(lane, back, jnp.zeros_like(back))
            raw = dot_last(query_half, key)
            scores = scale * raw + bias_tile(table, start, BLOCK, keys)
            shares = jnp.exp(scores - log_ref[rows, half * size : half * size + 1])
            back_shares = dot_last(back_half, value)
            weighted = shares * back_shares
            back_scores = weighted - shares * jnp.sum(weighted, axis=-1, keepdims=True)
            back_raw = low(scale * back_scores)
            part = dot(back_raw, key)
            back_query = part if back_query is None else jnp.where(lane, part, back_query)
            key_part = dot_first(back_raw, query_half)
            value_part = dot_first(low(shares), back_half)
            if turn == 0 and half == 0:
                key_sum[pl.ds(0, keys), :] = key_part
                value_sum[pl.ds(0, keys), :] = value_part
            else:
                key_sum[pl.ds(0, keys), :] += key_part
                value_sum[pl.ds(0, keys), :] += value_part
            first = length - 1 - start
            lines = jnp.zeros((8, span), jnp.float32)
            wide = jnp.concatenate(
                [back_scores, jnp.zeros((BLOCK, span - keys), jnp.float32)], axis=1
            )
            for tile in range(BLOCK // 8):
                piece = wide[tile * 8 : tile * 8 + 8, :]
                lines = lines + pltpu.roll(piece, (first - tile * 8) % span, 1)
            line = lines[0:1, :]
            for step in range(1, 8):
                line = line + pltpu.roll(lines[step : step + 1, :], span - step, 1)
            if turn == 0:
                sums_ref[0, half : half + 1, :] = line
            else:
                sums_ref[0, half : half + 1, :] += line
        dq_ref[rows, :] = low(back_query)
    dk_ref[...] = low(key_sum[...])
    dv_ref[...] = low(value_sum[...])


def attention_specs(length, heads, size):
    pair = LANES // size
    groups = heads // pair

    def column(offset):
        return pl.BlockSpec((length, LANES), lambda g: (0, g + offset))

    table = pl.BlockSpec((1, pair, 2 * length), lambda g: (g, 0, 0))
    return pair, groups, column, table


def attention_forward(joined, table, heads):
    length, width = joined.shape[0], joined.shape[1] // 3
    size = width // heads
    pair, groups, column, table_spec = attention_specs(length, heads, size)
    return pl.pallas_call(
        functools.partial(attend, pair, size**-0.5),
        grid=(groups,),
        out_shape=(
            jax.ShapeDtypeStruct((length, width), jnp.bfloat16),
            jax.ShapeDtypeStruct((length, width), jnp.float32),
        ),
        in_specs=[column(0), column(groups), column(2 * groups), table_spec],
        out_specs=(column(0), column(0)),
        compiler_params=pltpu.CompilerParams(vmem_limit_bytes=32 << 20),
        cost_estimate=pl.CostEstimate(
            flops=4 * length * length * width,
            bytes_accessed=length * width * 12,
            transcendentals=length * length * heads,
        ),
        name="attend",
    )(joined, joined, joined, table.reshape(groups, pair, 2 * length))


def attention_backward(joined, table, log_total, back_mixed, heads):
    length, width = back_mixed.shape
    size = width // heads
    pair, groups, column, table_spec = attention_specs(length, heads, size)
    rows = jax.ShapeDtypeStruct((length, width), jnp.bfloat16)
    back_query, back_key, back_value, sums = pl.pallas_call(
        functools.partial(attend_back, pair, size**-0.5),
        grid=(groups,),
        out_shape=(
            rows,
            rows,
            rows,
            jax.ShapeDtypeStruct((groups, pair, 2 * length), jnp.float32),
        ),
        in_specs=[
            column(0),
            column(groups),
            column(2 * groups),
            table_spec,
            column(0),
            column(0),
        ],
        out_specs=(column(0), column(0), column(0), table_spec),
        scratch_shapes=[pltpu.VMEM((length, LANES), jnp.float32)] * 2,
        compiler_params=pltpu.CompilerParams(vmem_limit_bytes=32 << 20),
        cost_estimate=pl.CostEstimate(
            flops=10 * length * length * width,
            bytes_accessed=length * width * 20,
            transcendentals=length * length * heads,
        ),
        name="attend_back",
    )(joined, joined, joined, table.reshape(groups, pair, 2 * length), log_total, back_mixed)
    return back_query, back_key, back_value, sums.reshape(heads, 2 * length)


def plan_routes(routes, experts, capacity):
    length = routes.shape[0]
    flat = routes.reshape(-1)
    selector = flat[:, None] == jnp.arange(experts, dtype=jnp.int32)[None, :]
    running = jnp.cumsum(selector.astype(jnp.int32), axis=0)
    rank = jnp.sum(jnp.where(selector, running, 0), axis=1) - 1
    slot = (flat * capacity + rank).reshape(length, TOP).T.reshape(-1)
    place = jnp.arange(experts * capacity, dtype=jnp.int32)
    taken = slot[None, :] == place[:, None]
    pick = low(taken)
    both = sum(pick[:, choice * length : (choice + 1) * length] for choice in range(TOP))
    chosen = routes[:, :, None] == jnp.arange(experts, dtype=jnp.int32)[None, None, :]
    return taken, pick, both, chosen


def exchange(values):
    return lax.all_to_all(values, "dp", split_axis=0, concat_axis=0, tiled=True)


def exchange_rows(values, experts):
    rows, width = values.shape
    return exchange(values.reshape(experts, rows // experts, width)).reshape(rows, width)


def exchange_numbers(values, experts):
    return exchange(values.reshape(experts, 1, -1)).reshape(-1)


def pack_small(router, attention_gain, expert_gain, bias):
    rows = router.shape[0]
    flat = bias.reshape(-1)
    column = jnp.concatenate([flat, jnp.zeros((rows - flat.shape[0],), flat.dtype)])
    block = jnp.concatenate(
        [router, attention_gain[:, None], expert_gain[:, None], column[:, None]], axis=1
    )
    return jnp.pad(block, ((0, 0), (0, -block.shape[1] % LANES)))


def unpack_small(block, experts, shards, heads):
    router = block[:, :experts]
    attention_gain = block[:, experts]
    expert_gain = block[:, experts + 1]
    column = block[:, experts + 2].reshape(shards, -1)
    bias = column[:, : heads // shards * NB].reshape(heads, NB)
    return router, attention_gain, expert_gain, bias


def per_device(
    tokens,
    query_weight,
    key_weight,
    value_weight,
    projection,
    router_weight,
    attention_gain,
    expert_gain,
    position_bias,
    expert_up,
    expert_down,
    routes,
    cotangent,
):
    layers = query_weight.shape[0]
    length, width = tokens.shape
    shards = lax.axis_size("fsdp")
    owners = lax.axis_size("dp")
    experts = owners * EXP_DEV
    heads = position_bias.shape[1] * shards
    capacity = max(2, 9 * length * TOP // (8 * experts))
    taken, pick, both, chosen = plan_routes(routes, experts, capacity)
    offsets = offset_selector(length)

    mixers = []
    for layer in range(layers):
        small = pack_small(
            router_weight[layer], attention_gain[layer], expert_gain[layer], position_bias[layer]
        )
        first = jnp.concatenate(
            [query_weight[layer], key_weight[layer], value_weight[layer], small], axis=1
        )
        first = lax.all_gather(first, "fsdp", axis=0, tiled=True)
        second = lax.all_gather(projection[layer], "fsdp", axis=0, tiled=True)
        router, gain_attention, gain_expert, bias = unpack_small(
            first[:, 3 * width :], experts, shards, heads
        )
        table = lax.dot_general(
            bias.astype(jnp.float32), offsets, contract_last, precision=highest
        )
        mixers.append(
            (
                first[:, : 3 * width],
                second,
                router,
                gain_attention.astype(jnp.float32),
                gain_expert.astype(jnp.float32),
                table,
            )
        )

    early = exchange_rows(low(dot(both, cotangent)), experts)

    hidden = tokens.astype(jnp.float32)
    saved = []
    for layer in range(layers):
        joined_weight, projection_full, router, gain_attention, gain_expert, table = mixers[layer]
        up_matrix, down_matrix = expert_up[layer, 0], expert_down[layer, 0]
        scale = row_scale(hidden)
        normed = low(hidden * scale * gain_attention)
        joined = low(dot(normed, joined_weight))
        mixed, log_total = attention_forward(joined, table, heads)
        middle = hidden + dot(mixed, projection_full)
        scale_expert = row_scale(middle)
        normed_expert = low(middle * scale_expert * gain_expert)
        logits = dot(normed_expert, router)
        picked = jnp.sum(jnp.where(chosen, logits[:, None, :], 0.0), axis=-1)
        gates = jax.nn.softmax(picked, axis=-1)
        gate_line = gates.T.reshape(-1)
        received = exchange_rows(low(dot(both, normed_expert)), experts)
        inner = dot(received, up_matrix)
        activity, slope = smooth_pair(inner)
        activity = low(activity)
        result = low(dot(activity, down_matrix))
        if layer == layers - 1:
            gate_places = exchange_numbers(
                jnp.sum(jnp.where(taken, gate_line[None, :], 0.0), axis=1), experts
            )
            back_places = jnp.sum(early.astype(jnp.float32) * result.astype(jnp.float32), axis=1)
            back_places = exchange_numbers(back_places, experts)
            back_sent = low(gate_places[:, None] * early.astype(jnp.float32))
            back_inner = low(dot_last(back_sent, down_matrix) * slope)
            back_rows = exchange_rows(low(dot_last(back_inner, up_matrix)), experts)
            last = (back_places, back_sent, back_inner, back_rows)
        returned = exchange_rows(result, experts)
        routed = low(dot_first(pick, returned)).reshape(TOP, length, width)
        update = sum(
            gates[:, choice : choice + 1] * routed[choice].astype(jnp.float32)
            for choice in range(TOP)
        )
        saved.append(
            (
                hidden,
                scale,
                normed,
                joined,
                mixed,
                log_total,
                middle,
                scale_expert,
                normed_expert,
                gates,
                received,
                activity,
                slope,
                routed,
            )
        )
        hidden = middle + update
    output = low(hidden)

    back_out = cotangent.astype(jnp.float32)
    mixer_results = [None] * layers
    expert_results = [None] * layers
    for layer in range(layers - 1, -1, -1):
        joined_weight, projection_full, router, gain_attention, gain_expert, table = mixers[layer]
        up_matrix, down_matrix = expert_up[layer, 0], expert_down[layer, 0]
        (
            hidden,
            scale,
            normed,
            joined,
            mixed,
            log_total,
            middle,
            scale_expert,
            normed_expert,
            gates,
            received,
            activity,
            slope,
            routed,
        ) = saved[layer]
        if layer == layers - 1:
            back_places, back_sent, back_inner, back_rows = last
            back_gates = jnp.sum(jnp.where(taken, back_places[:, None], 0.0), axis=0)
            back_gates = back_gates.reshape(TOP, length).T
        else:
            back_gates = jnp.stack(
                [
                    jnp.sum(back_out * routed[choice].astype(jnp.float32), axis=-1)
                    for choice in range(TOP)
                ],
                axis=1,
            )
            gated = jnp.concatenate(
                [low(gates[:, choice : choice + 1] * back_out) for choice in range(TOP)], axis=0
            )
            back_sent = exchange_rows(low(dot(pick, gated)), experts)
            back_inner = low(dot_last(back_sent, down_matrix) * slope)
            back_rows = exchange_rows(low(dot_last(back_inner, up_matrix)), experts)
        down_change = dot_first(activity, back_sent)
        up_change = dot_first(received, back_inner)
        expert_results[layer] = tuple(
            lax.psum_scatter(low(change), "fsdp", scatter_dimension=0, tiled=True).astype(
                jnp.float32
            )
            for change in (up_change, down_change)
        )
        back_picked = gates * (back_gates - jnp.sum(gates * back_gates, axis=-1, keepdims=True))
        back_logits = low(jnp.sum(jnp.where(chosen, back_picked[:, :, None], 0.0), axis=1))
        router_change = dot_first(normed_expert, back_logits)
        back_expert = dot_first(both, back_rows) + dot_last(back_logits, router)
        rows, expert_gain_change = norm_back(middle, scale_expert, gain_expert, back_expert)
        back_middle = back_out + rows
        back_attended = low(back_middle)
        back_mixed = low(dot_last(back_attended, projection_full))
        back_query, back_key, back_value, sums = attention_backward(
            joined, table, log_total, back_mixed, heads
        )
        bias_change = jnp.dot(sums, offsets, precision=highest)
        projection_change = dot_first(mixed, back_attended)
        parts = (back_query, back_key, back_value)
        changes = [low(dot_first(normed, part)) for part in parts]
        back_normed = sum(
            dot_last(part, joined_weight[:, index * width : (index + 1) * width])
            for index, part in enumerate(parts)
        )
        rows, attention_gain_change = norm_back(hidden, scale, gain_attention, back_normed)
        back_out = back_middle + rows
        column = jnp.pad(
            bias_change.reshape(shards, -1), ((0, 0), (0, (width - heads * NB) // shards))
        ).reshape(-1)
        small = jnp.concatenate(
            [
                router_change,
                attention_gain_change[:, None],
                expert_gain_change[:, None],
                column[:, None],
            ],
            axis=1,
        )
        small = jnp.pad(small, ((0, 0), (0, -small.shape[1] % LANES)))
        packed = jnp.concatenate(changes + [low(projection_change), low(small)], axis=1)
        shard = lax.psum_scatter(packed, "fsdp", scatter_dimension=0, tiled=True)
        mixer_results[layer] = lax.psum(shard, "dp").astype(jnp.float32)

    stacked = jnp.stack(mixer_results)
    router_gradient = stacked[:, :, 4 * width : 4 * width + experts]
    tail = 4 * width + experts
    bias_gradient = stacked[:, : position_bias.shape[1] * NB, tail + 2].reshape(
        position_bias.shape
    )
    up_stack = jnp.stack([expert_results[layer][0] for layer in range(layers)])[:, None]
    down_stack = jnp.stack([expert_results[layer][1] for layer in range(layers)])[:, None]
    return (
        output,
        back_out,
        stacked[:, :, :width],
        stacked[:, :, width : 2 * width],
        stacked[:, :, 2 * width : 3 * width],
        stacked[:, :, 3 * width : 4 * width],
        router_gradient,
        stacked[:, :, tail],
        stacked[:, :, tail + 1],
        bias_gradient,
        up_stack,
        down_stack,
    )


def solution(mesh):
    return jax.shard_map(
        per_device,
        mesh=mesh,
        in_specs=(
            P(("dp", "fsdp"), None),
            P(None, "fsdp", None),
            P(None, "fsdp", None),
            P(None, "fsdp", None),
            P(None, "fsdp", None),
            P(None, "fsdp", None),
            P(None, "fsdp"),
            P(None, "fsdp"),
            P(None, "fsdp", None),
            P(None, "dp", None, None),
            P(None, "dp", None, None),
            P(("dp", "fsdp"), None),
            P(("dp", "fsdp"), None),
        ),
        out_specs=(
            P(("dp", "fsdp"), None),
            P(("dp", "fsdp"), None),
            P(None, "fsdp", None),
            P(None, "fsdp", None),
            P(None, "fsdp", None),
            P(None, "fsdp", None),
            P(None, "fsdp", None),
            P(None, "fsdp"),
            P(None, "fsdp"),
            P(None, "fsdp", None),
            P(None, "dp", "fsdp", None),
            P(None, "dp", "fsdp", None),
        ),
        check_vma=False,
    )
```

time: 1250 us -> 1060 us (0.85)
  waiting for transfers between devices: 431 us -> 602 us
  matrix products: 370 us -> 216 us
  blocking collectives: 131 us -> 8.89 us
  local copies, waits for them, and re-layouts: 146 us -> 68.9 us
  other arithmetic: 114 us -> 38.6 us
  Pallas kernels: 0 us -> 60 us
    dot_general x60 -> x50, matrix products: 370 us -> 216 us  [the longest x18 79.4 us: dot_first(): lax.dot_general(left, right, contract_first, preferred_element_type=jnp.f...]
    all_to_all x7 -> x9, waiting for transfers between devices: 136 us -> 257 us  [exchange(): return lax.all_to_all(values, 'dp', split_axis=0, concat_axis=0, tiled=True)]
    reduce_scatter x12 -> x4, waiting for transfers between devices: 108 us -> 186 us  [per_device(): lax.psum_scatter(low(change), 'fsdp', scatter_dimension=0, tiled=True)]
    pallas_call x0 -> x4, Pallas kernels: none -> 60 us  [the longest x2 35 us: attention_backward(): pl.pallas_call(functools.partial(attend_back, pair, size ** (-0.5)), grid...]
    gather x8 -> x0, local copies, waits for them, and re-layouts: 42.1 us -> none  [the longest x4 22.9 us: pick_routed(): return returned.reshape(-1, width)[slot].reshape(length, TOP, width)]
    reduce_sum x17 -> x12, other arithmetic: 45 us -> 3.3 us  [the longest x1 1.23 us: per_device(): back_gates = jnp.sum(jnp.where(taken, back_places[:, None], 0.0), axis=0)]
    all_to_all x1, blocking collectives: 47.8 us -> 8.89 us  [exchange(): return lax.all_to_all(values, 'dp', split_axis=0, concat_axis=0, tiled=True)]
    psum x1, waiting for transfers between devices: 171 us -> 132 us  [per_device(): mixer_results[layer] = lax.psum(shard, 'dp').astype(jnp.float32)]
  transfers between devices with their start and end apart: 30 -> 20, of which waited for: 11 -> 15; matrix products, arithmetic and copies ran while one was open for 41% -> 22% of each run, Pallas kernels for 0% -> 4%
where the time goes in v1:
time: 1060 us; the launch traced here: 1050 us
  waiting for transfers between devices  602 us (57%)
  matrix products  216 us (20%)
  local copies, waits for them, and re-layouts  68.9 us (7%)
  Pallas kernels  60 us (6%)
  starting transfers between devices  40.9 us (4%)
  other arithmetic  38.6 us (4%)
  between operations  15.2 us (1%)
    all_to_all x9, waiting for transfers between devices, exchange(): return lax.all_to_all(values, 'dp', split_axis=0, concat_axis=0, tiled=True)  257 us
    reduce_scatter x4, waiting for transfers between devices, per_device(): lax.psum_scatter(low(change), 'fsdp', scatter_dimension=0, tiled=True)  186 us
    psum x1, waiting for transfers between devices, per_device(): mixer_results[layer] = lax.psum(shard, 'dp').astype(jnp.float32)  132 us
    dot_general x18, matrix products, dot_first(): lax.dot_general(left, right, contract_first, preferred_element_type=jnp.f...  79.4 us
    dot_general x14, matrix products, dot(): return jnp.dot(left, right, preferred_element_type=jnp.float32)  76.5 us
    dot_general x14, matrix products, dot_last(): lax.dot_general(left, right, contract_last, preferred_element_type=jnp.fl...  59.4 us
    unnamed x167, local copies, waits for them, and re-layouts  50.6 us
    all_to_all x9, starting transfers between devices, exchange(): return lax.all_to_all(values, 'dp', split_axis=0, concat_axis=0, tiled=True)  39.7 us
  transfers between devices with their start and end apart: 20, of which 15 were waited for; matrix products, arithmetic and copies ran while one was open for 22% of the time, Pallas kernels for 4%

profile of v1, /device:TPU:0, one launch (start us, length us, event | category | flops | bytes accessed | tf_op | source)
XLA Modules:
  0.0 1050.7 jit_solution(9674718009631099136)
XLA Ops:
  23.3 26.9 %all-gather.7.cloned.1.call-done = bf16[768,2432]{1,0:T(8,128)(2,1)} async-done(((bf16[192,2432]{1,0:T(8,128)(2,1)}), bf16[768,2432]{1,0:T(8,128)(2,1)}) %all-gather.7.cloned.1.call-update) | async-done | bytes 3735568 | tf_op jit(solution)/shard_map/all_gather | solution.py:329
  57.7 12.5 %attend.2 = (bf16[512,768]{1,0:T(8,128)(2,1)S(1)}, f32[512,768]{1,0:T(8,128)S(1)}) custom-call(bf16[512,2304]{1,0:T(8,128)(2,1)S(1)} %convolution_convert_fusion.5.q_ref.k_ref.v_ref, bf16[512,2304]{1,0:T(8,128)(2,1)S(1)} %convolution_convert_fusion.5.q_ref.k_ref.v_ref, bf16[512,2304]{1,0:T(8,128)(2,1)S(1)} %convolution_convert_fusion.5.q_ref.k_ref.v_ref, ...), custom_call_target="tpu_custom_call" | custom-call | flops 805306368 | bytes 4718592 | tf_op jit(solution)/shard_map/attend/pallas_call | solution.py:195
  86.6 40.2 %all-to-all-done = bf16[8,144,768]{2,1,0:T(8,128)(2,1)} async-done(((bf16[8,144,768]{2,1,0:T(8,128)(2,1)}), bf16[8,144,768]{2,1,0:T(8,128)(2,1)}, u32[]{:S(2)}, u32[]{:S(2)}) %all-to-all-start) | async-done | bytes 1769504 | tf_op jit(solution)/shard_map/all_to_all | solution.py:265
  126.8 8.1 fusion.24
  134.8 15.3 %fusion.46 = bf16[1152,768]{1,0:T(8,128)(2,1)} fusion(bf16[2,1,3072,768]{3,2,1,0:T(8,128)(2,1)} %param.23, f32[1152,3072]{1,0:T(8,128)S(1)} %fusion.24), kind=kOutput, calls=%fused_computation.72 | convolution fusion | flops 5468553216 | bytes 20643840 | tf_op jit(solution)/shard_map/dot_general | solution.py:27
  159.4 35.9 %all-to-all-done.1 = bf16[8,144,768]{2,1,0:T(8,128)(2,1)} async-done(((bf16[8,144,768]{2,1,0:T(8,128)(2,1)}), bf16[8,144,768]{2,1,0:T(8,128)(2,1)}, u32[]{:S(2)}, u32[]{:S(2)}) %all-to-all-start.1) | async-done | bytes 1769504 | tf_op jit(solution)/shard_map/all_to_all | solution.py:265
  204.7 12.5 %attend.3 = (bf16[512,768]{1,0:T(8,128)(2,1)S(1)}, f32[512,768]{1,0:T(8,128)S(1)}) custom-call(bf16[512,2304]{1,0:T(8,128)(2,1)S(1)} %convolution_convert_fusion.4.q_ref.k_ref.v_ref, bf16[512,2304]{1,0:T(8,128)(2,1)S(1)} %convolution_convert_fusion.4.q_ref.k_ref.v_ref, bf16[512,2304]{1,0:T(8,128)(2,1)S(1)} %convolution_convert_fusion.4.q_ref.k_ref.v_ref, ...), custom_call_target="tpu_custom_call" | custom-call | flops 805306368 | bytes 4718592 | tf_op jit(solution)/shard_map/attend/pallas_call | solution.py:195
  233.3 37.0 %all-to-all-done.2 = bf16[8,144,768]{2,1,0:T(8,128)(2,1)} async-done(((bf16[8,144,768]{2,1,0:T(8,128)(2,1)}), bf16[8,144,768]{2,1,0:T(8,128)(2,1)}, u32[]{:S(2)}, u32[]{:S(2)}) %all-to-all-start.2) | async-done | bytes 1769504 | tf_op jit(solution)/shard_map/all_to_all | solution.py:265
  276.4 11.0 %fusion.17 = f32[1152,3072]{1,0:T(8,128)} fusion(bf16[1152,768]{1,0:T(8,128)(2,1)} %bitcast.27, bf16[2,1,768,3072]{3,2,1,0:T(8,128)(2,1)} %param.22), kind=kOutput, calls=%fused_computation.31 | convolution fusion | flops 5435817984 | bytes 20643840 | tf_op jit(solution)/shard_map/dot_general | solution.py:27
  287.4 28.2 %all-to-all-done.5 = bf16[8,144,768]{2,1,0:T(8,128)(2,1)} async-done(((bf16[8,144,768]{2,1,0:T(8,128)(2,1)}), bf16[8,144,768]{2,1,0:T(8,128)(2,1)}, u32[]{:S(2)}, u32[]{:S(2)}) %all-to-all-start.5) | async-done | bytes 1769504 | tf_op jit(solution)/shard_map/all_to_all | solution.py:265
  315.6 16.5 %fusion.41 = (f32[1152]{0:T(1024)S(1)}, bf16[1152,768]{1,0:T(8,128)(2,1)}) fusion(bf16[8,144,768]{2,1,0:T(8,128)(2,1)} %all-to-all-done.5, bf16[2,1,3072,768]{3,2,1,0:T(8,128)(2,1)} %param.23, f32[1152,3072]{1,0:T(8,128)} %fusion.17), kind=kOutput, calls=%fused_computation.63 | convolution fusion | flops 5472091136 | bytes 22417920 | tf_op jit(solution)/shard_map/dot_general | solution.py:27
  344.4 8.9 all_to_all.50
  359.6 15.4 %fusion.10 = bf16[1152,3072]{1,0:T(8,128)(2,1)S(1)} fusion(f32[1152,3072]{1,0:T(8,128)} %fusion.17, bf16[1152,768]{1,0:T(8,128)(2,1)S(1)} %bitcast.229, bf16[2,1,3072,768]{3,2,1,0:T(8,128)(2,1)} %param.23), kind=kOutput, calls=%fused_computation.20 | convolution fusion | flops 5503057920 | bytes 27721728 | tf_op jit(solution)/shard_map/dot_general | solution.py:31
  377.9 9.2 fusion.49
  387.1 9.9 all-to-all-done.3
  406.8 35.5 %all-to-all-done.6 = bf16[8,144,768]{2,1,0:T(8,128)(2,1)} async-done(((bf16[8,144,768]{2,1,0:T(8,128)(2,1)}), bf16[8,144,768]{2,1,0:T(8,128)(2,1)}, u32[]{:S(2)}, u32[]{:S(2)}) %all-to-all-start.6) | async-done | bytes 1769504 | tf_op jit(solution)/shard_map/all_to_all | solution.py:265
  451.0 17.6 %attend_back.2 = (bf16[512,768]{1,0:T(8,128)(2,1)S(1)}, bf16[512,768]{1,0:T(8,128)(2,1)S(1)}, bf16[512,768]{1,0:T(8,128)(2,1)S(1)}, f32[6,2,1024]{2,1,0:T(2,128)S(1)}) custom-call(bf16[512,2304]{1,0:T(8,128)(2,1)S(1)} %convolution_convert_fusion.4.q_ref.k_ref.v_ref, bf16[512,2304]{1,0:T(8,128)(2,1)S(1)} %convolution_convert_fusion.4.q_ref.k_ref.v_ref, ...), custom_call_target="tpu_custom_call" | custom-call | flops 2013265920 | bytes 7864320 | tf_op jit(solution)/shard_map/attend_back/pallas_call | solution.py:219
  490.6 7.7 copy.162
  498.3 24.1 %all-to-all-done.8 = bf16[8,144,768]{2,1,0:T(8,128)(2,1)} async-done(((bf16[8,144,768]{2,1,0:T(8,128)(2,1)}), bf16[8,144,768]{2,1,0:T(8,128)(2,1)}, u32[]{:S(2)}, u32[]{:S(2)}) %all-to-all-start.8) | async-done | bytes 1769504 | tf_op jit(solution)/shard_map/all_to_all | solution.py:265
  522.4 15.9 %fusion.11 = bf16[1152,3072]{1,0:T(8,128)(2,1)S(1)} fusion(f32[1152,3072]{1,0:T(8,128)} %copy-done.71, bf16[1152,768]{1,0:T(8,128)(2,1)} %bitcast.41, bf16[2,1,3072,768]{3,2,1,0:T(8,128)(2,1)} %param.23), kind=kOutput, calls=%fused_computation.21 | convolution fusion | flops 5503057920 | bytes 27721728 | tf_op jit(solution)/shard_map/dot_general | solution.py:31
  550.6 40.0 %all-to-all-done.9 = bf16[8,144,768]{2,1,0:T(8,128)(2,1)S(1)} async-done(((bf16[8,144,768]{2,1,0:T(8,128)(2,1)}), bf16[8,144,768]{2,1,0:T(8,128)(2,1)S(1)}, u32[]{:S(2)}, u32[]{:S(2)}) %all-to-all-start.9) | async-done | bytes 1769504 | tf_op jit(solution)/shard_map/all_to_all | solution.py:265
  597.4 17.4 %attend_back.3 = (bf16[512,768]{1,0:T(8,128)(2,1)S(1)}, bf16[512,768]{1,0:T(8,128)(2,1)S(1)}, bf16[512,768]{1,0:T(8,128)(2,1)S(1)}, f32[6,2,1024]{2,1,0:T(2,128)S(1)}) custom-call(bf16[512,2304]{1,0:T(8,128)(2,1)S(1)} %copy-done.1, bf16[512,2304]{1,0:T(8,128)(2,1)S(1)} %copy-done.1, bf16[512,2304]{1,0:T(8,128)(2,1)S(1)} %copy-done.1, ...), custom_call_target="tpu_custom_call" | custom-call | flops 2013265920 | bytes 7864320 | tf_op jit(solution)/shard_map/attend_back/pallas_call | solution.py:219
  627.9 7.4 copy.160
  637.3 14.0 %convolution_convert_fusion = bf16[3072,768]{1,0:T(8,128)(2,1)} fusion(bf16[1152,768]{1,0:T(8,128)(2,1)S(1)} %fusion.42, f32[1152,3072]{1,0:T(8,128)} %fusion.17), kind=kOutput, calls=%fused_computation.22 | convolution fusion | flops 5470027776 | bytes 20643840 | tf_op jit(solution)/shard_map/dot_general | solution.py:35
  651.3 14.1 %convolution_convert_fusion.1 = bf16[3072,768]{1,0:T(8,128)(2,1)} fusion(bf16[1152,768]{1,0:T(8,128)(2,1)} %bitcast.41, f32[1152,3072]{1,0:T(8,128)} %copy-done.71), kind=kOutput, calls=%fused_computation.23 | convolution fusion | flops 5470027776 | bytes 20643840 | tf_op jit(solution)/shard_map/dot_general | solution.py:35
  665.4 10.5 convolution_convert_fusion.2
  676.0 10.8 %convolution_convert_fusion.3 = bf16[768,3072]{1,0:T(8,128)(2,1)} fusion(bf16[1152,768]{1,0:T(8,128)(2,1)} %bitcast.12, bf16[1152,3072]{1,0:T(8,128)(2,1)} %copy-done.70), kind=kOutput, calls=%fused_computation.25 | convolution fusion | flops 5438177280 | bytes 13565952 | tf_op jit(solution)/shard_map/dot_general | solution.py:35
  696.0 37.8 %reduce-scatter.17.cloned.1.call-done = bf16[768,768]{1,0:T(8,128)(2,1)} async-done(((bf16[3072,768]{1,0:T(8,128)(2,1)}), bf16[768,768]{1,0:T(8,128)(2,1)}) %reduce-scatter.17.cloned.1.call-update) | async-done | bytes 1179664 | tf_op jit(solution)/shard_map/reduce_scatter | solution.py:451
  733.8 50.5 %reduce-scatter.15.cloned.1.call-done = bf16[768,768]{1,0:T(8,128)(2,1)} async-done(((bf16[3072,768]{1,0:T(8,128)(2,1)}), bf16[768,768]{1,0:T(8,128)(2,1)}) %reduce-scatter.15.cloned.1.call-update) | async-done | bytes 1179664 | tf_op jit(solution)/shard_map/reduce_scatter | solution.py:451
  788.5 47.0 %reduce-scatter.13.cloned.1.call-done = bf16[192,3072]{1,0:T(8,128)(2,1)} async-done(((bf16[768,3072]{1,0:T(8,128)(2,1)}), bf16[192,3072]{1,0:T(8,128)(2,1)}) %reduce-scatter.13.cloned.1.call-update) | async-done | bytes 1179664 | tf_op jit(solution)/shard_map/reduce_scatter | solution.py:451
  835.5 50.4 %reduce-scatter.11.cloned.1.call-done = bf16[192,3072]{1,0:T(8,128)(2,1)} async-done(((bf16[768,3072]{1,0:T(8,128)(2,1)}), bf16[192,3072]{1,0:T(8,128)(2,1)}) %reduce-scatter.11.cloned.1.call-update) | async-done | bytes 1179664 | tf_op jit(solution)/shard_map/reduce_scatter | solution.py:451
  890.0 132.2 %all-reduce.11.cloned.1.call-done = (bf16[1,192,3200]{1,2,0:T(8,128)(2,1)}, bf16[1,192,3200]{1,2,0:T(8,128)(2,1)}) async-done(((bf16[1,192,3200]{1,2,0:T(8,128)(2,1)}, bf16[1,192,3200]{1,2,0:T(8,128)(2,1)}), (bf16[1,192,3200]{1,2,0:T(8,128)(2,1)}, bf16[1,192,3200]{1,2,0:T(8,128)(2,1)})) %all-reduce.11.cloned.1.call-update) | async-done | bytes 2457616 | tf_op jit(solution)/shard_map/psum | solution.py:492
  (352 shorter events, 215.2 us)
Async XLA Ops:
  7.2 43.0 %all-gather.7.cloned.1.call-start = ((), (), s32[]{:S(2)}) async-start(), calls=%async_computation.16 | async-start | bytes 4669440 | tf_op jit(solution)/shard_map/all_gather | solution.py:329
  15.4 57.4 %all-gather.11.cloned.1.call-start = ((), (), s32[]{:S(2)}) async-start(), calls=%async_computation.22 | async-start | bytes 1474560 | tf_op jit(solution)/shard_map/all_gather | solution.py:330
  22.1 30.9 %copy-start.64 = (f32[512]{0:T(512)}, f32[512]{0:T(512)S(1)}, u32[]{:S(2)}) copy-start(f32[512]{0:T(512)S(1)} %get-tuple-element.156) | copy-start | bytes 6148
  53.1 22.8 %copy-start.54 = (f32[768]{0:T(1024)}, f32[768]{0:T(1024)S(1)}, u32[]{:S(2)}) copy-start(f32[768]{0:T(1024)S(1)} %get-tuple-element.110) | copy-start | bytes 9220
  75.3 124.1 %copy-start.20 = (f32[512,768]{1,0:T(8,128)}, f32[512,768]{1,0:T(8,128)S(1)}, u32[]{:S(2)}) copy-start(f32[512,768]{1,0:T(8,128)S(1)} %get-tuple-element.168) | copy-start | bytes 4718596
  77.1 79.6 %copy-start.35 = (bf16[512,768]{1,0:T(8,128)(2,1)}, bf16[512,768]{1,0:T(8,128)(2,1)S(1)}, u32[]{:S(2)}) copy-start(bf16[512,768]{1,0:T(8,128)(2,1)S(1)} %multiply_convert_fusion.6) | copy-start | bytes 2359300
  79.4 47.4 %all-to-all-start = ((bf16[8,144,768]{2,1,0:T(8,128)(2,1)}), bf16[8,144,768]{2,1,0:T(8,128)(2,1)}, u32[]{:S(2)}, u32[]{:S(2)}) async-start(bf16[8,144,768]{2,1,0:T(8,128)(2,1)} %bitcast.225), calls=%async_computation | async-start | bytes 3538944 | tf_op jit(solution)/shard_map/all_to_all | solution.py:265
  85.1 70.1 %all-gather.9.cloned.1.call-start = ((), (), s32[]{:S(2)}) async-start(), calls=%async_computation.17 | async-start | bytes 4669440 | tf_op jit(solution)/shard_map/all_gather | solution.py:329
  150.2 45.1 %all-to-all-start.1 = ((bf16[8,144,768]{2,1,0:T(8,128)(2,1)}), bf16[8,144,768]{2,1,0:T(8,128)(2,1)}, u32[]{:S(2)}, u32[]{:S(2)}) async-start(bf16[8,144,768]{2,1,0:T(8,128)(2,1)} %bitcast.222), calls=%async_computation.1 | async-start | bytes 3538944 | tf_op jit(solution)/shard_map/all_to_all | solution.py:265
  154.5 63.9 %all-gather.13.cloned.1.call-start = ((), (), s32[]{:S(2)}) async-start(), calls=%async_computation.23 | async-start | bytes 1474560 | tf_op jit(solution)/shard_map/all_gather | solution.py:330
  158.0 41.3 %copy-start.52 = (f32[512,2]{0,1:T(2,128)}, f32[512,2]{0,1:T(2,128)S(1)}, u32[]{:S(2)}) copy-start(f32[512,2]{0,1:T(2,128)S(1)} %select_reduce_fusion.5) | copy-start | bytes 12292
  158.0 41.3 %copy-start.56 = (f32[512]{0:T(512)}, f32[512]{0:T(512)S(1)}, u32[]{:S(2)}) copy-start(f32[512]{0:T(512)S(1)} %reduce_max.18) | copy-start | bytes 6148
  158.0 41.3 %copy-start.60 = (f32[512]{0:T(512)}, f32[512]{0:T(512)S(1)}, u32[]{:S(2)}) copy-start(f32[512]{0:T(512)S(1)} %fusion.169) | copy-start | bytes 6148
  225.2 45.1 %all-to-all-start.2 = ((bf16[8,144,768]{2,1,0:T(8,128)(2,1)}), bf16[8,144,768]{2,1,0:T(8,128)(2,1)}, u32[]{:S(2)}, u32[]{:S(2)}) async-start(bf16[8,144,768]{2,1,0:T(8,128)(2,1)} %bitcast.228), calls=%async_computation.2 | async-start | bytes 3538944 | tf_op jit(solution)/shard_map/all_to_all | solution.py:265
  270.3 45.3 %all-to-all-start.5 = ((bf16[8,144,768]{2,1,0:T(8,128)(2,1)}), bf16[8,144,768]{2,1,0:T(8,128)(2,1)}, u32[]{:S(2)}, u32[]{:S(2)}) async-start(bf16[8,144,768]{2,1,0:T(8,128)(2,1)} %bitcast.227), calls=%async_computation.5 | async-start | bytes 3538944 | tf_op jit(solution)/shard_map/all_to_all | solution.py:265
  332.8 10.1 all-to-all-start.7
  353.3 43.8 %all-to-all-start.3 = ((bf16[8,144,768]{2,1,0:T(8,128)(2,1)}), bf16[8,144,768]{2,1,0:T(8,128)(2,1)}, u32[]{:S(2)}, u32[]{:S(2)}) async-start(bf16[8,144,768]{2,1,0:T(8,128)(2,1)} %bitcast.223), calls=%async_computation.3 | async-start | bytes 3538944 | tf_op jit(solution)/shard_map/all_to_all | solution.py:265
  397.0 45.2 %all-to-all-start.6 = ((bf16[8,144,768]{2,1,0:T(8,128)(2,1)}), bf16[8,144,768]{2,1,0:T(8,128)(2,1)}, u32[]{:S(2)}, u32[]{:S(2)}) async-start(bf16[8,144,768]{2,1,0:T(8,128)(2,1)} %bitcast.224), calls=%async_computation.6 | async-start | bytes 3538944 | tf_op jit(solution)/shard_map/all_to_all | solution.py:265
  449.0 23.3 %copy-start.26 = (f32[512,768]{1,0:T(8,128)}, f32[512,768]{1,0:T(8,128)S(1)}, u32[]{:S(2)}) copy-start(f32[512,768]{1,0:T(8,128)S(1)} %get-tuple-element.139) | copy-start | bytes 4718596
  451.0 17.7 %copy-start.43 = (bf16[768,2432]{1,0:T(8,128)(2,1)S(1)}, bf16[768,2432]{1,0:T(8,128)(2,1)}, u32[]{:S(2)}) copy-start(bf16[768,2432]{1,0:T(8,128)(2,1)} %all-gather.9.cloned.1.call-done) | copy-start | bytes 11206660
  477.1 45.3 %all-to-all-start.8 = ((bf16[8,144,768]{2,1,0:T(8,128)(2,1)}), bf16[8,144,768]{2,1,0:T(8,128)(2,1)}, u32[]{:S(2)}, u32[]{:S(2)}) async-start(bf16[8,144,768]{2,1,0:T(8,128)(2,1)} %bitcast.221), calls=%async_computation.8 | async-start | bytes 3538944 | tf_op jit(solution)/shard_map/all_to_all | solution.py:265
  481.6 205.3 %reduce-scatter.21.cloned.1.call-start = ((), (), s32[]{:S(2)}) async-start(), calls=%async_computation.25 | async-start | bytes 6144000
  490.6 47.8 %slice-start = ((s8[9437184]{0:T(1024)(128)(4,1)}), s8[1048576]{0:T(1024)(128)(4,1)S(1)}, s32[]{:S(2)}) async-start(s8[9437184]{0:T(1024)(128)(4,1)} %bitcast.254), calls=%async_computation.27 | async-start | bytes 2097152
  545.3 45.2 %copy-start.32 = (bf16[1152,512]{1,0:T(8,128)(2,1)S(1)}, bf16[1152,512]{1,0:T(8,128)(2,1)}, u32[]{:S(2)}) copy-start(bf16[1152,512]{1,0:T(8,128)(2,1)} %slice_add_fusion) | copy-start | bytes 3538948
  545.4 45.2 %all-to-all-start.9 = ((bf16[8,144,768]{2,1,0:T(8,128)(2,1)}), bf16[8,144,768]{2,1,0:T(8,128)(2,1)S(1)}, u32[]{:S(2)}, u32[]{:S(2)}) async-start(bf16[8,144,768]{2,1,0:T(8,128)(2,1)} %bitcast.226), calls=%async_computation.9 | async-start | bytes 3538944 | tf_op jit(solution)/shard_map/all_to_all | solution.py:265
  549.1 140.4 %reduce-scatter.19.cloned.1.call-start = ((), (), s32[]{:S(2)}) async-start(), calls=%async_computation.24 | async-start | bytes 6144000
  597.4 17.4 %copy-start.41 = (bf16[768,2432]{1,0:T(8,128)(2,1)S(1)}, bf16[768,2432]{1,0:T(8,128)(2,1)}, u32[]{:S(2)}) copy-start(bf16[768,2432]{1,0:T(8,128)(2,1)} %all-gather.7.cloned.1.call-done) | copy-start | bytes 11206660
  635.3 98.6 %reduce-scatter.17.cloned.1.call-start = ((), (), s32[]{:S(2)}) async-start(), calls=%async_computation.21 | async-start | bytes 5898240 | tf_op jit(solution)/shard_map/reduce_scatter | solution.py:451
  651.3 133.1 %reduce-scatter.15.cloned.1.call-start = ((), (), s32[]{:S(2)}) async-start(), calls=%async_computation.20 | async-start | bytes 5898240 | tf_op jit(solution)/shard_map/reduce_scatter | solution.py:451
  665.4 170.1 %reduce-scatter.13.cloned.1.call-start = ((), (), s32[]{:S(2)}) async-start(), calls=%async_computation.19 | async-start | bytes 5898240 | tf_op jit(solution)/shard_map/reduce_scatter | solution.py:451
  676.0 209.9 %reduce-scatter.11.cloned.1.call-start = ((), (), s32[]{:S(2)}) async-start(), calls=%async_computation.18 | async-start | bytes 5898240 | tf_op jit(solution)/shard_map/reduce_scatter | solution.py:451
  686.8 335.4 %all-reduce.11.cloned.1.call-start = ((), (), s32[]{:S(2)}) async-start(), calls=%async_computation.26 | async-start | bytes 6553600 | tf_op jit(solution)/shard_map/psum | solution.py:492
  (63 other events, 189.3 us)
Sparse Core Ops, SparseCore 0:
  15.5 34.5 all-gather.6
  52.3 17.4 all-gather.10
  88.0 32.3 all-gather.8
  157.1 17.8 all-gather.12
  498.4 49.5 reduce-scatter.20
  635.4 47.3 reduce-scatter.18
  685.9 47.9 reduce-scatter.16
  736.4 47.9 reduce-scatter.14
  787.5 47.9 reduce-scatter.12
  837.9 47.9 reduce-scatter.10
  889.6 132.5 all-reduce.10

commit v2 on v1

--- a/solution.py
+++ b/solution.py
@@ -246,6 +246,225 @@
     return back_query, back_key, back_value, sums.reshape(heads, 2 * length)
 
 
+def mesh_copy(source, target, sends, receives, where, device):
+    return pltpu.make_async_remote_copy(
+        src_ref=source,
+        dst_ref=target,
+        send_sem=sends.at[where],
+        recv_sem=receives.at[where],
+        device_id=device,
+        device_id_type=pl.DeviceIdType.MESH,
+    )
+
+
+def reduce_mixer(
+    owners,
+    chunks,
+    q_ref,
+    k_ref,
+    v_ref,
+    p_ref,
+    small_ref,
+    out_ref,
+    core_in,
+    side_out,
+    side_in,
+    keep,
+    owner_in,
+    small_in,
+    part,
+    whole_in,
+    core_send,
+    core_recv,
+    side_send,
+    side_recv,
+    owner_send,
+    owner_recv,
+    small_send,
+    small_recv,
+    whole_send,
+    whole_recv,
+):
+    me = lax.axis_index("dp")
+    place = lax.axis_index("fsdp")
+    core, side = lax.rem(place, 2), place // 2
+    partner = 2 * side + (1 - core)
+    across = 2 * (1 - side) + core
+    refs = (q_ref, k_ref, v_ref, p_ref, small_ref)
+    rows = q_ref.shape[1]
+    spare = small_ref.shape[1]
+    main = 4 * rows
+    block = main // owners
+    columns = q_ref.shape[2] // chunks
+    spans = [(index * rows, ref.shape[1]) for index, ref in enumerate(refs)]
+
+    barrier = pltpu.get_barrier_semaphore()
+    for other in (partner, across):
+        pl.semaphore_signal(
+            barrier, inc=1, device_id={"fsdp": other}, device_id_type=pl.DeviceIdType.MESH
+        )
+    for step in range(1, owners):
+        pl.semaphore_signal(
+            barrier,
+            inc=1,
+            device_id={"dp": lax.rem(me + step, owners)},
+            device_id_type=pl.DeviceIdType.MESH,
+        )
+    pl.semaphore_wait(barrier, owners + 1)
+
+    waits = []
+    core_copies = [[] for _ in range(chunks)]
+    for chunk in range(chunks):
+        lanes = pl.ds(chunk * columns, columns)
+        for turn in range(2):
+            there = 1 - side if turn == 0 else side
+            for index, (start, count) in enumerate(spans):
+                copy = mesh_copy(
+                    refs[index].at[2 * there + 1 - core, :, lanes],
+                    core_in.at[turn, pl.ds(start, count), lanes],
+                    core_send,
+                    core_recv,
+                    (chunk * 2 + turn) * 5 + index,
+                    {"fsdp": partner},
+                )
+                copy.start()
+                core_copies[chunk].append(copy)
+
+    side_copies = []
+    for chunk in range(chunks):
+        lanes = pl.ds(chunk * columns, columns)
+        for copy in core_copies[chunk]:
+            copy.wait()
+        for turn in range(2):
+            there = 1 - side if turn == 0 else side
+            target = side_out if turn == 0 else keep
+            for index, (start, count) in enumerate(spans):
+                at = pl.ds(start, count)
+                total = refs[index][2 * there + core, :, lanes].astype(jnp.float32)
+                total = total + core_in[turn, at, lanes].astype(jnp.float32)
+                target[at, lanes] = low(total)
+            if turn == 0:
+                copy = mesh_copy(
+                    side_out.at[:, lanes],
+                    side_in.at[:, lanes],
+                    side_send,
+                    side_recv,
+                    chunk,
+                    {"fsdp": across},
+                )
+                copy.start()
+                side_copies.append(copy)
+
+    owner_copies = []
+    for chunk in range(chunks):
+        lanes = pl.ds(chunk * columns, columns)
+        side_copies[chunk].wait()
+        keep[:, lanes] = low(
+            keep[:, lanes].astype(jnp.float32) + side_in[:, lanes].astype(jnp.float32)
+        )
+        copies = []
+        for step in range(1, owners):
+            other = lax.rem(me + step, owners)
+            where = chunk * owners + step
+            at = pl.ds(pl.multiple_of(other * block, block), block)
+            copies.append(
+                mesh_copy(
+                    keep.at[at, lanes],
+                    owner_in.at[step, :, lanes],
+                    owner_send,
+                    owner_recv,
+                    where,
+                    {"dp": other},
+                )
+            )
+            copies.append(
+                mesh_copy(
+                    keep.at[pl.ds(main, spare), lanes],
+                    small_in.at[me, :, lanes],
+                    small_send,
+                    small_recv,
+                    where,
+                    {"dp": other},
+                )
+            )
+            copies[-2].start()
+            copies[-1].start()
+        owner_copies.append(copies)
+
+    mine = pl.ds(pl.multiple_of(me * block, block), block)
+    whole_copies = []
+    for chunk in range(chunks):
+        lanes = pl.ds(chunk * columns, columns)
+        for copy in owner_copies[chunk]:
+            copy.wait()
+        total = keep[mine, lanes].astype(jnp.float32)
+        for step in range(1, owners):
+            total = total + owner_in[step, :, lanes].astype(jnp.float32)
+        part[:, lanes] = low(total)
+        out_ref[mine, lanes] = low(total).astype(jnp.float32)
+        copies = []
+        for step in range(1, owners):
+            copy = mesh_copy(
+                part.at[:, lanes],
+                whole_in.at[me, :, lanes],
+                whole_send,
+                whole_recv,
+                chunk * owners + step,
+                {"dp": lax.rem(me + step, owners)},
+            )
+            copy.start()
+            copies.append(copy)
+        whole_copies.append(copies)
+        small_in[me, :, lanes] = keep[pl.ds(main, spare), lanes]
+        narrow = small_in[0, :, lanes].astype(jnp.float32)
+        for other in range(1, owners):
+            narrow = narrow + small_in[other, :, lanes].astype(jnp.float32)
+        out_ref[pl.ds(main, spare), lanes] = narrow
+
+    for chunk in range(chunks):
+        lanes = pl.ds(chunk * columns, columns)
+        for copy in whole_copies[chunk]:
+            copy.wait()
+        for step in range(1, owners):
+            other = lax.rem(me + step, owners)
+            at = pl.ds(pl.multiple_of(other * block, block), block)
+            out_ref[at, lanes] = whole_in[other, :, lanes].astype(jnp.float32)
+
+
+def reduce_in_kernel(changes, small, owners):
+    shards, rows, width = changes[0].shape
+    spare = small.shape[1]
+    main = 4 * rows
+    total = main + spare
+    block = main // owners
+    chunks = 3
+    low_type = jnp.bfloat16
+    space = pl.BlockSpec(memory_space=pltpu.VMEM)
+    return pl.pallas_call(
+        functools.partial(reduce_mixer, owners, chunks),
+        out_shape=jax.ShapeDtypeStruct((total, width), jnp.float32),
+        in_specs=[space] * 5,
+        out_specs=space,
+        scratch_shapes=[
+            pltpu.VMEM((2, total, width), low_type),
+            pltpu.VMEM((total, width), low_type),
+            pltpu.VMEM((total, width), low_type),
+            pltpu.VMEM((total, width), low_type),
+            pltpu.VMEM((owners, block, width), low_type),
+            pltpu.VMEM((owners, spare, width), low_type),
+            pltpu.VMEM((block, width), low_type),
+            pltpu.VMEM((owners, block, width), low_type),
+        ]
+        + [pltpu.SemaphoreType.DMA((10 * chunks,))] * 2
+        + [pltpu.SemaphoreType.DMA((chunks,))] * 2
+        + [pltpu.SemaphoreType.DMA((chunks * owners,))] * 6,
+        compiler_params=pltpu.CompilerParams(
+            collective_id=1, has_side_effects=True, vmem_limit_bytes=40 << 20
+        ),
+        name="reduce_mixer",
+    )(*changes, small)
+
+
 def plan_routes(routes, experts, capacity):
     length = routes.shape[0]
     flat = routes.reshape(-1)
@@ -356,6 +575,8 @@
         normed = low(hidden * scale * gain_attention)
         joined = low(dot(normed, joined_weight))
         mixed, log_total = attention_forward(joined, table, heads)
+        if layer == 0:
+            mixed, early = lax.optimization_barrier((mixed, early))
         middle = hidden + dot(mixed, projection_full)
         scale_expert = row_scale(middle)
         normed_expert = low(middle * scale_expert * gain_expert)
@@ -364,14 +585,16 @@
         gates = jax.nn.softmax(picked, axis=-1)
         gate_line = gates.T.reshape(-1)
         received = exchange_rows(low(dot(both, normed_expert)), experts)
+        if layer == layers - 1:
+            gate_places = exchange_numbers(
+                jnp.sum(jnp.where(taken, gate_line[None, :], 0.0), axis=1), experts
+            )
+            received, gate_places = lax.optimization_barrier((received, gate_places))
         inner = dot(received, up_matrix)
         activity, slope = smooth_pair(inner)
         activity = low(activity)
         result = low(dot(activity, down_matrix))
         if layer == layers - 1:
-            gate_places = exchange_numbers(
-                jnp.sum(jnp.where(taken, gate_line[None, :], 0.0), axis=1), experts
-            )
             back_places = jnp.sum(early.astype(jnp.float32) * result.astype(jnp.float32), axis=1)
             back_places = exchange_numbers(back_places, experts)
             back_sent = low(gate_places[:, None] * early.astype(jnp.float32))
@@ -445,12 +668,13 @@
             back_sent = exchange_rows(low(dot(pick, gated)), experts)
             back_inner = low(dot_last(back_sent, down_matrix) * slope)
             back_rows = exchange_rows(low(dot_last(back_inner, up_matrix)), experts)
-        down_change = dot_first(activity, back_sent)
-        up_change = dot_first(received, back_inner)
+        down_change = low(dot_first(activity, back_sent))
+        up_change = low(dot_first(received, back_inner))
+        back_rows, down_change, up_change = lax.optimization_barrier(
+            (back_rows, down_change, up_change)
+        )
         expert_results[layer] = tuple(
-            lax.psum_scatter(low(change), "fsdp", scatter_dimension=0, tiled=True).astype(
-                jnp.float32
-            )
+            lax.psum_scatter(change, "fsdp", scatter_dimension=0, tiled=True).astype(jnp.float32)
             for change in (up_change, down_change)
         )
         back_picked = gates * (back_gates - jnp.sum(gates * back_gates, axis=-1, keepdims=True))
@@ -474,41 +698,54 @@
         )
         rows, attention_gain_change = norm_back(hidden, scale, gain_attention, back_normed)
         back_out = back_middle + rows
-        column = jnp.pad(
-            bias_change.reshape(shards, -1), ((0, 0), (0, (width - heads * NB) // shards))
-        ).reshape(-1)
+        changes = [
+            change.reshape(shards, width // shards, width)
+            for change in changes + [low(projection_change)]
+        ]
         small = jnp.concatenate(
             [
-                router_change,
-                attention_gain_change[:, None],
-                expert_gain_change[:, None],
-                column[:, None],
+                change.reshape(shards, -1)
+                for change in (
+                    router_change,
+                    attention_gain_change,
+                    expert_gain_change,
+                    bias_change,
+                )
             ],
             axis=1,
         )
-        small = jnp.pad(small, ((0, 0), (0, -small.shape[1] % LANES)))
-        packed = jnp.concatenate(changes + [low(projection_change), low(small)], axis=1)
-        shard = lax.psum_scatter(packed, "fsdp", scatter_dimension=0, tiled=True)
-        mixer_results[layer] = lax.psum(shard, "dp").astype(jnp.float32)
-
-    stacked = jnp.stack(mixer_results)
-    router_gradient = stacked[:, :, 4 * width : 4 * width + experts]
-    tail = 4 * width + experts
-    bias_gradient = stacked[:, : position_bias.shape[1] * NB, tail + 2].reshape(
-        position_bias.shape
-    )
+        small = low(jnp.pad(small, ((0, 0), (0, -small.shape[1] % (16 * width)))))
+        small = small.reshape(shards, -1, width)
+        if layer == 0 and shards == 4 and owners == 8:
+            mixer_results[layer] = reduce_in_kernel(changes, small, owners)
+        else:
+            packed = jnp.concatenate(changes + [small], axis=1)
+            shard = lax.psum_scatter(packed, "fsdp", scatter_dimension=0)
+            mixer_results[layer] = lax.psum(shard, "dp").astype(jnp.float32)
+
+    rows = width // shards
+    counts = (rows * experts, rows, rows, heads // shards * NB)
+    smalls = []
+    for result in mixer_results:
+        flat = result[4 * rows :].reshape(-1)
+        ends = [sum(counts[: index + 1]) for index in range(4)]
+        smalls.append([flat[end - count : end] for end, count in zip(ends, counts)])
+    small_gradients = [jnp.stack([small[index] for small in smalls]) for index in range(4)]
+    router_gradient = small_gradients[0].reshape(layers, rows, experts)
+    bias_gradient = small_gradients[3].reshape(position_bias.shape)
+    mixer_gradients = [
+        jnp.stack([result[index * rows : (index + 1) * rows] for result in mixer_results])
+        for index in range(4)
+    ]
     up_stack = jnp.stack([expert_results[layer][0] for layer in range(layers)])[:, None]
     down_stack = jnp.stack([expert_results[layer][1] for layer in range(layers)])[:, None]
     return (
         output,
         back_out,
-        stacked[:, :, :width],
-        stacked[:, :, width : 2 * width],
-        stacked[:, :, 2 * width : 3 * width],
-        stacked[:, :, 3 * width : 4 * width],
+        *mixer_gradients,
         router_gradient,
-        stacked[:, :, tail],
-        stacked[:, :, tail + 1],
+        small_gradients[1],
+        small_gradients[2],
         bias_gradient,
         up_stack,
         down_stack,

time: 1060 us -> 847 us (0.80)
  waiting for transfers between devices: 602 us -> 313 us
  Pallas kernels: 60 us -> 148 us
  local copies, waits for them, and re-layouts: 68.9 us -> 54 us
    psum x1, waiting for transfers between devices: 132 us -> 0.01 us  [per_device(): mixer_results[layer] = lax.psum(shard, 'dp').astype(jnp.float32)]
    pallas_call x0 -> x1, Pallas kernels: none -> 88.6 us  [reduce_in_kernel(): pl.pallas_call(functools.partial(reduce_mixer, owners, chunks), out_shape...]
    all_to_all x9 -> x10, waiting for transfers between devices: 257 us -> 175 us  [exchange(): return lax.all_to_all(values, 'dp', split_axis=0, concat_axis=0, tiled=True)]
    reduce_scatter x4 -> x5, waiting for transfers between devices: 186 us -> 118 us  [the longest x4 83 us: per_device(): lax.psum_scatter(change, 'fsdp', scatter_dimension=0, tiled=True)]
    unnamed x167 -> x179, local copies, waits for them, and re-layouts: 50.6 us -> 31.2 us
    all_to_all x9 -> x10, starting transfers between devices: 39.7 us -> 45.5 us  [exchange(): return lax.all_to_all(values, 'dp', split_axis=0, concat_axis=0, tiled=True)]
  transfers between devices with their start and end apart: 20 -> 20, of which waited for: 15 -> 13; matrix products, arithmetic and copies ran while one was open for 22% -> 25% of each run, Pallas kernels for 4% -> 16%
where the time goes in v2:
time: 847 us; the launch traced here: 838 us
  waiting for transfers between devices  313 us (37%)
  matrix products  219 us (26%)
  Pallas kernels  148 us (17%)
  local copies, waits for them, and re-layouts  54 us (6%)
  starting transfers between devices  46.5 us (5%)
  other arithmetic  41.8 us (5%)
  between operations  15.7 us (2%)
    all_to_all x10, waiting for transfers between devices, exchange(): return lax.all_to_all(values, 'dp', split_axis=0, concat_axis=0, tiled=True)  175 us
    pallas_call x1, Pallas kernels, reduce_in_kernel(): pl.pallas_call(functools.partial(reduce_mixer, owners, chunks), out_shape...  88.6 us
    reduce_scatter x4, waiting for transfers between devices, per_device(): lax.psum_scatter(change, 'fsdp', scatter_dimension=0, tiled=True)  83 us
    dot_general x18, matrix products, dot_first(): lax.dot_general(left, right, contract_first, preferred_element_type=jnp.f...  77 us
    dot_general x14, matrix products, dot(): return jnp.dot(left, right, preferred_element_type=jnp.float32)  74.1 us
    dot_general x14, matrix products, dot_last(): lax.dot_general(left, right, contract_last, preferred_element_type=jnp.fl...  67.8 us
    all_to_all x10, starting transfers between devices, exchange(): return lax.all_to_all(values, 'dp', split_axis=0, concat_axis=0, tiled=True)  45.5 us
    reduce_scatter x1, waiting for transfers between devices, per_device(): shard = lax.psum_scatter(packed, 'fsdp', scatter_dimension=0)  34.8 us
  transfers between devices with their start and end apart: 20, of which 13 were waited for; matrix products, arithmetic and copies ran while one was open for 25% of the time, Pallas kernels for 16%

profile of v2, /device:TPU:0, one launch (start us, length us, event | category | flops | bytes accessed | tf_op | source)
XLA Modules:
  0.0 838.1 jit_solution(5473946270380040414)
XLA Ops:
  23.6 7.4 all-to-all-start
  32.8 17.4 %all-gather.7.cloned.1.call-done = bf16[768,2432]{1,0:T(8,128)(2,1)} async-done(((bf16[192,2432]{1,0:T(8,128)(2,1)}), bf16[768,2432]{1,0:T(8,128)(2,1)}) %all-gather.7.cloned.1.call-update) | async-done | bytes 3735568 | tf_op jit(solution)/shard_map/all_gather | solution.py:548
  57.3 12.5 %attend.2 = (bf16[512,768]{1,0:T(8,128)(2,1)S(1)}, f32[512,768]{1,0:T(8,128)S(1)}) custom-call(bf16[512,2304]{1,0:T(8,128)(2,1)S(1)} %convolution_convert_fusion.5.q_ref.k_ref.v_ref, bf16[512,2304]{1,0:T(8,128)(2,1)S(1)} %convolution_convert_fusion.5.q_ref.k_ref.v_ref, bf16[512,2304]{1,0:T(8,128)(2,1)S(1)} %convolution_convert_fusion.5.q_ref.k_ref.v_ref, ...), custom_call_target="tpu_custom_call" | custom-call | flops 805306368 | bytes 4718592 | tf_op jit(solution)/shard_map/attend/pallas_call | solution.py:195
  78.9 5.6 all-to-all-start.1
  85.9 40.3 %all-to-all-done.1 = bf16[8,144,768]{2,1,0:T(8,128)(2,1)} async-done(((bf16[8,144,768]{2,1,0:T(8,128)(2,1)}), bf16[8,144,768]{2,1,0:T(8,128)(2,1)}, u32[]{:S(2)}, u32[]{:S(2)}) %all-to-all-start.1) | async-done | bytes 1769504 | tf_op jit(solution)/shard_map/all_to_all | solution.py:484
  126.2 8.1 fusion.24
  134.3 15.3 %fusion.45 = bf16[1152,768]{1,0:T(8,128)(2,1)} fusion(bf16[2,1,3072,768]{3,2,1,0:T(8,128)(2,1)} %param.23, f32[1152,3072]{1,0:T(8,128)S(1)} %fusion.24), kind=kOutput, calls=%fused_computation.70 | convolution fusion | flops 5468553216 | bytes 20643840 | tf_op jit(solution)/shard_map/dot_general | solution.py:27
  158.9 35.9 %all-to-all-done.2 = bf16[8,144,768]{2,1,0:T(8,128)(2,1)} async-done(((bf16[8,144,768]{2,1,0:T(8,128)(2,1)}), bf16[8,144,768]{2,1,0:T(8,128)(2,1)}, u32[]{:S(2)}, u32[]{:S(2)}) %all-to-all-start.2) | async-done | bytes 1769504 | tf_op jit(solution)/shard_map/all_to_all | solution.py:484
  204.2 12.5 %attend.3 = (bf16[512,768]{1,0:T(8,128)(2,1)S(1)}, f32[512,768]{1,0:T(8,128)S(1)}) custom-call(bf16[512,2304]{1,0:T(8,128)(2,1)S(1)} %convolution_convert_fusion.4.q_ref.k_ref.v_ref, bf16[512,2304]{1,0:T(8,128)(2,1)S(1)} %convolution_convert_fusion.4.q_ref.k_ref.v_ref, bf16[512,2304]{1,0:T(8,128)(2,1)S(1)} %convolution_convert_fusion.4.q_ref.k_ref.v_ref, ...), custom_call_target="tpu_custom_call" | custom-call | flops 805306368 | bytes 4718592 | tf_op jit(solution)/shard_map/attend/pallas_call | solution.py:195
  240.3 40.1 %all-to-all-done.3 = bf16[8,144,768]{2,1,0:T(8,128)(2,1)} async-done(((bf16[8,144,768]{2,1,0:T(8,128)(2,1)}), bf16[8,144,768]{2,1,0:T(8,128)(2,1)}, u32[]{:S(2)}, u32[]{:S(2)}) %all-to-all-start.3) | async-done | bytes 1769504 | tf_op jit(solution)/shard_map/all_to_all | solution.py:484
  280.4 8.1 fusion.17
  288.5 17.3 %fusion.39 = (f32[1152]{0:T(1024)S(1)}, bf16[1152,768]{1,0:T(8,128)(2,1)}) fusion(bf16[1152,768]{1,0:T(8,128)(2,1)} %bitcast.10, bf16[2,1,3072,768]{3,2,1,0:T(8,128)(2,1)} %param.23, f32[1152,3072]{1,0:T(8,128)S(1)} %fusion.17), kind=kOutput, calls=%fused_computation.60 | convolution fusion | flops 5472091136 | bytes 22417920 | tf_op jit(solution)/shard_map/dot_general | solution.py:27
  310.1 6.5 all-to-all-done.7
  321.4 16.0 %fusion.10 = bf16[1152,3072]{1,0:T(8,128)(2,1)S(1)} fusion(f32[1152,3072]{1,0:T(8,128)} %copy-done.80, bf16[2,1,3072,768]{3,2,1,0:T(8,128)(2,1)} %param.23, bf16[1152,768]{1,0:T(8,128)(2,1)} %bitcast.10, f32[1152]{0:T(1024)S(1)} %reshape.457), kind=kOutput, calls=%fused_computation.20 | convolution fusion | flops 5505712128 | bytes 27726336 | tf_op jit(solution)/shard_map/dot_general | solution.py:31
  340.3 9.1 %fusion.48 = bf16[1152,768]{1,0:T(8,128)(2,1)} fusion(bf16[1152,3072]{1,0:T(8,128)(2,1)S(1)} %fusion.10, bf16[2,1,768,3072]{3,2,1,0:T(8,128)(2,1)} %param.22), kind=kOutput, calls=%fused_computation.71 | convolution fusion | flops 5436702720 | bytes 13565952 | tf_op jit(solution)/shard_map/dot_general | solution.py:31
  349.4 12.2 %all-to-all-done.5 = bf16[8,144,768]{2,1,0:T(8,128)(2,1)} async-done(((bf16[8,144,768]{2,1,0:T(8,128)(2,1)}), bf16[8,144,768]{2,1,0:T(8,128)(2,1)}, u32[]{:S(2)}, u32[]{:S(2)}) %all-to-all-start.5) | async-done | bytes 1769504 | tf_op jit(solution)/shard_map/all_to_all | solution.py:484
  366.2 13.9 %convolution_convert_fusion.3 = bf16[3072,768]{1,0:T(8,128)(2,1)} fusion(bf16[1152,768]{1,0:T(8,128)(2,1)} %bitcast.10, f32[1152]{0:T(1024)S(1)} %reshape.457, f32[1152,3072]{1,0:T(8,128)} %copy-done.80), kind=kOutput, calls=%fused_computation.25 | convolution fusion | flops 5472681984 | bytes 20648448 | tf_op jit(solution)/shard_map/dot_general | solution.py:35
  380.1 10.7 %convolution_convert_fusion.2 = bf16[768,3072]{1,0:T(8,128)(2,1)} fusion(bf16[1152,768]{1,0:T(8,128)(2,1)} %bitcast.29, bf16[1152,3072]{1,0:T(8,128)(2,1)} %copy-done.77), kind=kOutput, calls=%fused_computation.24 | convolution fusion | flops 5438177280 | bytes 13565952 | tf_op jit(solution)/shard_map/dot_general | solution.py:35
  393.3 5.1 fusion.63
  398.4 8.4 %all-to-all-done.6 = bf16[8,144,768]{2,1,0:T(8,128)(2,1)} async-done(((bf16[8,144,768]{2,1,0:T(8,128)(2,1)}), bf16[8,144,768]{2,1,0:T(8,128)(2,1)}, u32[]{:S(2)}, u32[]{:S(2)}) %all-to-all-start.6) | async-done | bytes 1769504 | tf_op jit(solution)/shard_map/all_to_all | solution.py:484
  420.0 17.4 %attend_back.2 = (bf16[512,768]{1,0:T(8,128)(2,1)S(1)}, bf16[512,768]{1,0:T(8,128)(2,1)S(1)}, bf16[512,768]{1,0:T(8,128)(2,1)S(1)}, f32[6,2,1024]{2,1,0:T(2,128)S(1)}) custom-call(bf16[512,2304]{1,0:T(8,128)(2,1)S(1)} %convolution_convert_fusion.4.q_ref.k_ref.v_ref, bf16[512,2304]{1,0:T(8,128)(2,1)S(1)} %convolution_convert_fusion.4.q_ref.k_ref.v_ref, ...), custom_call_target="tpu_custom_call" | custom-call | flops 2013265920 | bytes 7864320 | tf_op jit(solution)/shard_map/attend_back/pallas_call | solution.py:219
  470.3 34.8 %reduce-scatter.6.cloned.1.call-done = bf16[1,784,768]{2,1,0:T(8,128)(2,1)} async-done(((bf16[4,784,768]{2,1,0:T(8,128)(2,1)}), bf16[1,784,768]{2,1,0:T(8,128)(2,1)}) %reduce-scatter.6.cloned.1.call-update) | async-done | bytes 1204240 | tf_op jit(solution)/shard_map/reduce_scatter | solution.py:723
  505.9 5.8 all-to-all-done.8
  511.7 16.2 %fusion.11 = bf16[1152,3072]{1,0:T(8,128)(2,1)S(1)} fusion(f32[1152,3072]{1,0:T(8,128)} %copy-done.79, bf16[1152,768]{1,0:T(8,128)(2,1)S(1)} %bitcast.240, bf16[2,1,3072,768]{3,2,1,0:T(8,128)(2,1)} %param.23), kind=kOutput, calls=%fused_computation.21 | convolution fusion | flops 5503057920 | bytes 27721728 | tf_op jit(solution)/shard_map/dot_general | solution.py:31
  528.0 6.9 fusion.42
  538.6 10.7 %convolution_convert_fusion = bf16[768,3072]{1,0:T(8,128)(2,1)} fusion(bf16[1152,768]{1,0:T(8,128)(2,1)} %bitcast.14, bf16[1152,3072]{1,0:T(8,128)(2,1)} %copy-done.78), kind=kOutput, calls=%fused_computation.22 | convolution fusion | flops 5438177280 | bytes 13565952 | tf_op jit(solution)/shard_map/dot_general | solution.py:35
  549.3 12.8 %convolution_convert_fusion.1 = bf16[3072,768]{1,0:T(8,128)(2,1)} fusion(bf16[1152,768]{1,0:T(8,128)(2,1)S(1)} %bitcast.241, f32[1152,3072]{1,0:T(8,128)} %copy-done.79), kind=kOutput, calls=%fused_computation.23 | convolution fusion | flops 5470027776 | bytes 20643840 | tf_op jit(solution)/shard_map/dot_general | solution.py:35
  562.1 23.4 %all-to-all-done.9 = bf16[8,144,768]{2,1,0:T(8,128)(2,1)S(1)} async-done(((bf16[8,144,768]{2,1,0:T(8,128)(2,1)}), bf16[8,144,768]{2,1,0:T(8,128)(2,1)S(1)}, u32[]{:S(2)}, u32[]{:S(2)}) %all-to-all-start.9) | async-done | bytes 1769504 | tf_op jit(solution)/shard_map/all_to_all | solution.py:484
  599.9 17.4 %attend_back.3 = (bf16[512,768]{1,0:T(8,128)(2,1)S(1)}, bf16[512,768]{1,0:T(8,128)(2,1)S(1)}, bf16[512,768]{1,0:T(8,128)(2,1)S(1)}, f32[6,2,1024]{2,1,0:T(2,128)S(1)}) custom-call(bf16[512,2304]{1,0:T(8,128)(2,1)S(1)} %copy-done.1, bf16[512,2304]{1,0:T(8,128)(2,1)S(1)} %copy-done.1, bf16[512,2304]{1,0:T(8,128)(2,1)S(1)} %copy-done.1, ...), custom_call_target="tpu_custom_call" | custom-call | flops 2013265920 | bytes 7864320 | tf_op jit(solution)/shard_map/attend_back/pallas_call | solution.py:219
  630.6 88.6 %reduce_mixer.1 = f32[784,768]{1,0:T(8,128)S(1)} custom-call(bf16[4,192,768]{2,1,0:T(8,128)(2,1)S(1)} %bitcast.233, bf16[4,192,768]{2,1,0:T(8,128)(2,1)S(1)} %bitcast.234, bf16[4,192,768]{2,1,0:T(8,128)(2,1)S(1)} %bitcast.235, bf16[4,192,768]{2,1,0:T(8,128)(2,1)S(1)} %bitcast.232, bf16[4,16,768]{2,1,0:T(8,128)(2,1)S(1)} %bitcast.236), custom_call_target="tpu_custom_call" | custom-call | tf_op jit(solution)/shard_map/reduce_mixer/pallas_call | solution.py:443
  743.9 32.6 %reduce-scatter.10.cloned.1.call-done = bf16[192,3072]{1,0:T(8,128)(2,1)} async-done(((bf16[768,3072]{1,0:T(8,128)(2,1)}), bf16[192,3072]{1,0:T(8,128)(2,1)}) %reduce-scatter.10.cloned.1.call-update) | async-done | bytes 1179664 | tf_op jit(solution)/shard_map/reduce_scatter | solution.py:677
  776.6 50.4 %reduce-scatter.8.cloned.1.call-done = bf16[192,3072]{1,0:T(8,128)(2,1)} async-done(((bf16[768,3072]{1,0:T(8,128)(2,1)}), bf16[192,3072]{1,0:T(8,128)(2,1)}) %reduce-scatter.8.cloned.1.call-update) | async-done | bytes 1179664 | tf_op jit(solution)/shard_map/reduce_scatter | solution.py:677
  (387 shorter events, 203.1 us)
Async XLA Ops:
  7.2 43.0 %all-gather.7.cloned.1.call-start = ((), (), s32[]{:S(2)}) async-start(), calls=%async_computation.15 | async-start | bytes 4669440 | tf_op jit(solution)/shard_map/all_gather | solution.py:548
  23.6 48.7 %all-to-all-start = ((bf16[8,144,768]{2,1,0:T(8,128)(2,1)}), bf16[8,144,768]{2,1,0:T(8,128)(2,1)}, u32[]{:S(2)}, u32[]{:S(2)}) async-start(bf16[8,144,768]{2,1,0:T(8,128)(2,1)} %bitcast.9), calls=%async_computation | async-start | bytes 3538944 | tf_op jit(solution)/shard_map/all_to_all | solution.py:484
  31.0 41.3 %all-gather.11.cloned.1.call-start = ((), (), s32[]{:S(2)}) async-start(), calls=%async_computation.23 | async-start | bytes 1474560 | tf_op jit(solution)/shard_map/all_gather | solution.py:549
  32.8 24.4 %copy-start.71 = (f32[512]{0:T(512)}, f32[512]{0:T(512)S(1)}, u32[]{:S(2)}) copy-start(f32[512]{0:T(512)S(1)} %get-tuple-element.178) | copy-start | bytes 6148
  53.1 22.2 %copy-start.60 = (f32[768]{0:T(1024)}, f32[768]{0:T(1024)S(1)}, u32[]{:S(2)}) copy-start(f32[768]{0:T(1024)S(1)} %get-tuple-element.130) | copy-start | bytes 9220
  74.7 124.1 %copy-start.16 = (f32[512,768]{1,0:T(8,128)}, f32[512,768]{1,0:T(8,128)S(1)}, u32[]{:S(2)}) copy-start(f32[512,768]{1,0:T(8,128)S(1)} %get-tuple-element.190) | copy-start | bytes 4718596
  76.6 79.6 %copy-start.33 = (bf16[512,768]{1,0:T(8,128)(2,1)}, bf16[512,768]{1,0:T(8,128)(2,1)S(1)}, u32[]{:S(2)}) copy-start(bf16[512,768]{1,0:T(8,128)(2,1)S(1)} %multiply_convert_fusion.6) | copy-start | bytes 2359300
  78.9 47.4 %all-to-all-start.1 = ((bf16[8,144,768]{2,1,0:T(8,128)(2,1)}), bf16[8,144,768]{2,1,0:T(8,128)(2,1)}, u32[]{:S(2)}, u32[]{:S(2)}) async-start(bf16[8,144,768]{2,1,0:T(8,128)(2,1)} %bitcast.243), calls=%async_computation.1 | async-start | bytes 3538944 | tf_op jit(solution)/shard_map/all_to_all | solution.py:484
  84.5 70.1 %all-gather.9.cloned.1.call-start = ((), (), s32[]{:S(2)}) async-start(), calls=%async_computation.16 | async-start | bytes 4669440 | tf_op jit(solution)/shard_map/all_gather | solution.py:548
  134.3 15.4 %copy-start.79 = (f32[1152,3072]{1,0:T(8,128)}, f32[1152,3072]{1,0:T(8,128)S(1)}, u32[]{:S(2)}) copy-start(f32[1152,3072]{1,0:T(8,128)S(1)} %fusion.24) | copy-start | bytes 42467332
  149.7 45.1 %all-to-all-start.2 = ((bf16[8,144,768]{2,1,0:T(8,128)(2,1)}), bf16[8,144,768]{2,1,0:T(8,128)(2,1)}, u32[]{:S(2)}, u32[]{:S(2)}) async-start(bf16[8,144,768]{2,1,0:T(8,128)(2,1)} %bitcast.242), calls=%async_computation.2 | async-start | bytes 3538944 | tf_op jit(solution)/shard_map/all_to_all | solution.py:484
  154.0 63.9 %all-gather.13.cloned.1.call-start = ((), (), s32[]{:S(2)}) async-start(), calls=%async_computation.24 | async-start | bytes 1474560 | tf_op jit(solution)/shard_map/all_gather | solution.py:549
  157.4 41.3 %copy-start.56 = (f32[512,2]{0,1:T(2,128)}, f32[512,2]{0,1:T(2,128)S(1)}, u32[]{:S(2)}) copy-start(f32[512,2]{0,1:T(2,128)S(1)} %select_reduce_fusion.5) | copy-start | bytes 12292
  157.5 41.3 %copy-start.62 = (f32[512]{0:T(512)}, f32[512]{0:T(512)S(1)}, u32[]{:S(2)}) copy-start(f32[512]{0:T(512)S(1)} %reduce_max.18) | copy-start | bytes 6148
  157.5 41.3 %copy-start.67 = (f32[512]{0:T(512)}, f32[512]{0:T(512)S(1)}, u32[]{:S(2)}) copy-start(f32[512]{0:T(512)S(1)} %fusion.146) | copy-start | bytes 6148
  225.4 10.2 %all-to-all-start.4 = ((f32[8,1,144]{2,1,0:T(1,128)}), f32[8,1,144]{2,1,0:T(1,128)S(1)}, u32[]{:S(2)}, u32[]{:S(2)}) async-start(f32[8,1,144]{2,1,0:T(1,128)} %reshape.456), calls=%async_computation.4 | async-start | bytes 16384 | tf_op jit(solution)/shard_map/all_to_all | solution.py:484
  235.5 44.8 %all-to-all-start.3 = ((bf16[8,144,768]{2,1,0:T(8,128)(2,1)}), bf16[8,144,768]{2,1,0:T(8,128)(2,1)}, u32[]{:S(2)}, u32[]{:S(2)}) async-start(bf16[8,144,768]{2,1,0:T(8,128)(2,1)} %bitcast.246), calls=%async_computation.3 | async-start | bytes 3538944 | tf_op jit(solution)/shard_map/all_to_all | solution.py:484
  288.5 17.3 %copy-start.80 = (f32[1152,3072]{1,0:T(8,128)}, f32[1152,3072]{1,0:T(8,128)S(1)}, u32[]{:S(2)}) copy-start(f32[1152,3072]{1,0:T(8,128)S(1)} %fusion.17) | copy-start | bytes 42467332
  306.5 10.2 %all-to-all-start.7 = ((f32[8,1,144]{2,1,0:T(1,128)}), f32[8,1,144]{2,1,0:T(1,128)S(1)}, u32[]{:S(2)}, u32[]{:S(2)}) async-start(f32[8,1,144]{2,1,0:T(1,128)} %reshape.462), calls=%async_computation.7 | async-start | bytes 16384 | tf_op jit(solution)/shard_map/all_to_all | solution.py:484
  316.6 45.0 %all-to-all-start.5 = ((bf16[8,144,768]{2,1,0:T(8,128)(2,1)}), bf16[8,144,768]{2,1,0:T(8,128)(2,1)}, u32[]{:S(2)}, u32[]{:S(2)}) async-start(bf16[8,144,768]{2,1,0:T(8,128)(2,1)} %bitcast.244), calls=%async_computation.5 | async-start | bytes 3538944 | tf_op jit(solution)/shard_map/all_to_all | solution.py:484
  361.6 45.1 %all-to-all-start.6 = ((bf16[8,144,768]{2,1,0:T(8,128)(2,1)}), bf16[8,144,768]{2,1,0:T(8,128)(2,1)}, u32[]{:S(2)}, u32[]{:S(2)}) async-start(bf16[8,144,768]{2,1,0:T(8,128)(2,1)} %bitcast.239), calls=%async_computation.6 | async-start | bytes 3538944 | tf_op jit(solution)/shard_map/all_to_all | solution.py:484
  366.0 139.2 %reduce-scatter.6.cloned.1.call-start = ((), (), s32[]{:S(2)}) async-start(), calls=%async_computation.17 | async-start | bytes 6021120 | tf_op jit(solution)/shard_map/reduce_scatter | solution.py:723
  466.7 45.0 %all-to-all-start.8 = ((bf16[8,144,768]{2,1,0:T(8,128)(2,1)}), bf16[8,144,768]{2,1,0:T(8,128)(2,1)S(1)}, u32[]{:S(2)}, u32[]{:S(2)}) async-start(bf16[8,144,768]{2,1,0:T(8,128)(2,1)} %bitcast.39), calls=%async_computation.8 | async-start | bytes 3538944 | tf_op jit(solution)/shard_map/all_to_all | solution.py:484
  470.3 257.7 %all-reduce.8.cloned.1.call-start = ((), (), s32[]{:S(2)}) async-start(), calls=%async_computation.18 | async-start | bytes 2408448 | tf_op jit(solution)/shard_map/psum | solution.py:724
  505.1 22.8 %slice-start.1 = ((s8[9437184]{0:T(1024)(128)(4,1)}), s8[1048576]{0:T(1024)(128)(4,1)S(1)}, s32[]{:S(2)}) async-start(s8[9437184]{0:T(1024)(128)(4,1)} %bitcast.279), calls=%async_computation.26 | async-start | bytes 2097152
  505.1 234.6 %reduce-scatter.14.cloned.1.call-start = ((), (), s32[]{:S(2)}) async-start(), calls=%async_computation.22 | async-start | bytes 5898240 | tf_op jit(solution)/shard_map/reduce_scatter | solution.py:677
  511.7 16.3 %slice-start.2 = ((s8[9437184]{0:T(1024)(128)(4,1)}), s8[4194304]{0:T(1024)(128)(4,1)S(1)}, s32[]{:S(2)}) async-start(s8[9437184]{0:T(1024)(128)(4,1)} %bitcast.279), calls=%async_computation.27 | async-start | bytes 8388608
  511.7 16.3 %slice-start.3 = ((s8[9437184]{0:T(1024)(128)(4,1)}), s8[4194304]{0:T(1024)(128)(4,1)S(1)}, s32[]{:S(2)}) async-start(s8[9437184]{0:T(1024)(128)(4,1)} %bitcast.279), calls=%async_computation.28 | async-start | bytes 8388608
  534.9 50.5 %all-to-all-start.9 = ((bf16[8,144,768]{2,1,0:T(8,128)(2,1)}), bf16[8,144,768]{2,1,0:T(8,128)(2,1)S(1)}, u32[]{:S(2)}, u32[]{:S(2)}) async-start(bf16[8,144,768]{2,1,0:T(8,128)(2,1)} %bitcast.245), calls=%async_computation.9 | async-start | bytes 3538944 | tf_op jit(solution)/shard_map/all_to_all | solution.py:484
  538.5 201.2 %reduce-scatter.12.cloned.1.call-start = ((), (), s32[]{:S(2)}) async-start(), calls=%async_computation.21 | async-start | bytes 5898240 | tf_op jit(solution)/shard_map/reduce_scatter | solution.py:677
  585.5 191.1 %reduce-scatter.10.cloned.1.call-start = ((), (), s32[]{:S(2)}) async-start(), calls=%async_computation.20 | async-start | bytes 5898240 | tf_op jit(solution)/shard_map/reduce_scatter | solution.py:677
  586.2 240.7 %reduce-scatter.8.cloned.1.call-start = ((), (), s32[]{:S(2)}) async-start(), calls=%async_computation.19 | async-start | bytes 5898240 | tf_op jit(solution)/shard_map/reduce_scatter | solution.py:677
  (73 other events, 184.6 us)
Sparse Core Ops, SparseCore 0:
  15.5 34.6 all-gather.6
  52.3 17.4 all-gather.10
  87.5 32.3 all-gather.8
  156.6 17.8 all-gather.12
  458.4 46.6 reduce-scatter.5
  508.5 97.1 all-reduce.7
  608.9 64.6 reduce-scatter.13
  676.1 49.3 reduce-scatter.11
  728.6 47.9 reduce-scatter.9
  778.9 47.9 reduce-scatter.7

commit v3 on v2

--- a/solution.py
+++ b/solution.py
@@ -493,6 +493,15 @@
     return exchange(values.reshape(experts, 1, -1)).reshape(-1)
 
 
+def gather_rows(pick, returned, gates):
+    length = gates.shape[0]
+    routed = low(dot_first(pick, returned)).reshape(TOP, length, -1)
+    update = sum(
+        gates[:, choice : choice + 1] * routed[choice].astype(jnp.float32) for choice in range(TOP)
+    )
+    return routed, update
+
+
 def pack_small(router, attention_gain, expert_gain, bias):
     rows = router.shape[0]
     flat = bias.reshape(-1)
@@ -599,14 +608,15 @@
             back_places = exchange_numbers(back_places, experts)
             back_sent = low(gate_places[:, None] * early.astype(jnp.float32))
             back_inner = low(dot_last(back_sent, down_matrix) * slope)
-            back_rows = exchange_rows(low(dot_last(back_inner, up_matrix)), experts)
+            back_rows, back_sent = lax.optimization_barrier(
+                (low(dot_last(back_inner, up_matrix)), back_sent)
+            )
+            back_rows = exchange_rows(back_rows, experts)
             last = (back_places, back_sent, back_inner, back_rows)
         returned = exchange_rows(result, experts)
-        routed = low(dot_first(pick, returned)).reshape(TOP, length, width)
-        update = sum(
-            gates[:, choice : choice + 1] * routed[choice].astype(jnp.float32)
-            for choice in range(TOP)
-        )
+        routed = None
+        if layer < layers - 1:
+            routed, update = gather_rows(pick, returned, gates)
         saved.append(
             (
                 hidden,
@@ -625,12 +635,13 @@
                 routed,
             )
         )
-        hidden = middle + update
-    output = low(hidden)
+        if layer < layers - 1:
+            hidden = middle + update
 
     back_out = cotangent.astype(jnp.float32)
     mixer_results = [None] * layers
     expert_results = [None] * layers
+    above = None
     for layer in range(layers - 1, -1, -1):
         joined_weight, projection_full, router, gain_attention, gain_expert, table = mixers[layer]
         up_matrix, down_matrix = expert_up[layer, 0], expert_down[layer, 0]
@@ -666,16 +677,24 @@
                 [low(gates[:, choice : choice + 1] * back_out) for choice in range(TOP)], axis=0
             )
             back_sent = exchange_rows(low(dot(pick, gated)), experts)
+            up_above, down_above = expert_results[layer + 1]
+            back_sent, up_above = lax.optimization_barrier((back_sent, up_above))
+            expert_results[layer + 1] = (up_above, down_above)
             back_inner = low(dot_last(back_sent, down_matrix) * slope)
-            back_rows = exchange_rows(low(dot_last(back_inner, up_matrix)), experts)
+            back_inner, above = lax.optimization_barrier((back_inner, above))
+            mixer_results[layer + 1] = lax.psum(above, "dp")
+            back_rows, back_sent = lax.optimization_barrier(
+                (low(dot_last(back_inner, up_matrix)), back_sent)
+            )
+            back_rows = exchange_rows(back_rows, experts)
         down_change = low(dot_first(activity, back_sent))
         up_change = low(dot_first(received, back_inner))
+        expert_results[layer] = tuple(
+            lax.psum_scatter(change, "fsdp", scatter_dimension=0, tiled=True)
+            for change in (up_change, down_change)
+        )
         back_rows, down_change, up_change = lax.optimization_barrier(
             (back_rows, down_change, up_change)
-        )
-        expert_results[layer] = tuple(
-            lax.psum_scatter(change, "fsdp", scatter_dimension=0, tiled=True).astype(jnp.float32)
-            for change in (up_change, down_change)
         )
         back_picked = gates * (back_gates - jnp.sum(gates * back_gates, axis=-1, keepdims=True))
         back_logits = low(jnp.sum(jnp.where(chosen, back_picked[:, :, None], 0.0), axis=1))
@@ -688,6 +707,15 @@
         back_query, back_key, back_value, sums = attention_backward(
             joined, table, log_total, back_mixed, heads
         )
+        if layer == layers - 1:
+            back_query, returned = lax.optimization_barrier((back_query, returned))
+            output = low(middle + gather_rows(pick, returned, gates)[1])
+        if layer > 0:
+            up_shard, down_shard = expert_results[layer]
+            back_query, back_key, back_value, down_shard = lax.optimization_barrier(
+                (back_query, back_key, back_value, down_shard)
+            )
+            expert_results[layer] = (up_shard, down_shard)
         bias_change = jnp.dot(sums, offsets, precision=highest)
         projection_change = dot_first(mixed, back_attended)
         parts = (back_query, back_key, back_value)
@@ -720,9 +748,12 @@
             mixer_results[layer] = reduce_in_kernel(changes, small, owners)
         else:
             packed = jnp.concatenate(changes + [small], axis=1)
-            shard = lax.psum_scatter(packed, "fsdp", scatter_dimension=0)
-            mixer_results[layer] = lax.psum(shard, "dp").astype(jnp.float32)
-
+            above = lax.psum_scatter(packed, "fsdp", scatter_dimension=0)
+            if layer == 0:
+                mixer_results[layer] = lax.psum(above, "dp")
+
+    mixer_results = lax.optimization_barrier(mixer_results)
+    mixer_results = [result.astype(jnp.float32) for result in mixer_results]
     rows = width // shards
     counts = (rows * experts, rows, rows, heads // shards * NB)
     smalls = []
@@ -737,8 +768,10 @@
         jnp.stack([result[index * rows : (index + 1) * rows] for result in mixer_results])
         for index in range(4)
     ]
-    up_stack = jnp.stack([expert_results[layer][0] for layer in range(layers)])[:, None]
-    down_stack = jnp.stack([expert_results[layer][1] for layer in range(layers)])[:, None]
+    up_stack, down_stack = (
+        jnp.stack([results[index].astype(jnp.float32) for results in expert_results])[:, None]
+        for index in range(2)
+    )
     return (
         output,
         back_out,

time: 847 us -> 768 us (0.907)
  waiting for transfers between devices: 313 us -> 257 us
  Pallas kernels: 148 us -> 132 us
  blocking collectives: 0 us -> 9.94 us
    reduce_scatter x4, waiting for transfers between devices: 83 us -> 11.6 us  [per_device(): lax.psum_scatter(change, 'fsdp', scatter_dimension=0, tiled=True)]
    all_to_all x10 -> x9, waiting for transfers between devices: 175 us -> 228 us  [exchange(): return lax.all_to_all(values, 'dp', split_axis=0, concat_axis=0, tiled=True)]
    reduce_scatter x1, waiting for transfers between devices: 34.8 us -> 0.01 us  [per_device(): above = lax.psum_scatter(packed, 'fsdp', scatter_dimension=0)]
    pallas_call x1, Pallas kernels: 88.6 us -> 72.4 us  [reduce_in_kernel(): pl.pallas_call(functools.partial(reduce_mixer, owners, chunks), out_shape...]
    all_to_all x0 -> x1, blocking collectives: none -> 9.94 us  [exchange(): return lax.all_to_all(values, 'dp', split_axis=0, concat_axis=0, tiled=True)]
    all_to_all x10 -> x9, starting transfers between devices: 45.5 us -> 41.3 us  [exchange(): return lax.all_to_all(values, 'dp', split_axis=0, concat_axis=0, tiled=True)]
    unnamed x179 -> x177, local copies, waits for them, and re-layouts: 31.2 us -> 29.6 us
  transfers between devices with their start and end apart: 20 -> 19, of which waited for: 13 -> 10; matrix products, arithmetic and copies ran while one was open for 25% -> 24% of each run, Pallas kernels for 16% -> 17%
where the time goes in v3:
time: 768 us; the launch traced here: 759 us
  waiting for transfers between devices  257 us (33%)
  matrix products  213 us (28%)
  Pallas kernels  132 us (17%)
  local copies, waits for them, and re-layouts  51.9 us (7%)
  starting transfers between devices  42.5 us (6%)
  other arithmetic  36.3 us (5%)
  between operations  15.9 us (2%)
  blocking collectives  9.94 us (1%)
    all_to_all x9, waiting for transfers between devices, exchange(): return lax.all_to_all(values, 'dp', split_axis=0, concat_axis=0, tiled=True)  228 us
    dot_general x14, matrix products, dot(): return jnp.dot(left, right, preferred_element_type=jnp.float32)  73.8 us
    pallas_call x1, Pallas kernels, reduce_in_kernel(): pl.pallas_call(functools.partial(reduce_mixer, owners, chunks), out_shape...  72.4 us
    dot_general x18, matrix products, dot_first(): lax.dot_general(left, right, contract_first, preferred_element_type=jnp.f...  70.1 us
    dot_general x14, matrix products, dot_last(): lax.dot_general(left, right, contract_last, preferred_element_type=jnp.fl...  68.9 us
    all_to_all x9, starting transfers between devices, exchange(): return lax.all_to_all(values, 'dp', split_axis=0, concat_axis=0, tiled=True)  41.3 us
    pallas_call x2, Pallas kernels, attention_backward(): pl.pallas_call(functools.partial(attend_back, pair, size ** (-0.5)), grid...  35 us
    unnamed x177, local copies, waits for them, and re-layouts  29.6 us
  transfers between devices with their start and end apart: 19, of which 10 were waited for; matrix products, arithmetic and copies ran while one was open for 24% of the time, Pallas kernels for 17%

profile of v3, /device:TPU:0, one launch (start us, length us, event | category | flops | bytes accessed | tf_op | source)
XLA Modules:
  0.0 759.2 jit_solution(10909356446167070774)
XLA Ops:
  23.6 7.4 all-to-all-start
  32.8 17.4 %all-gather.7.cloned.1.call-done = bf16[768,2432]{1,0:T(8,128)(2,1)} async-done(((bf16[192,2432]{1,0:T(8,128)(2,1)}), bf16[768,2432]{1,0:T(8,128)(2,1)}) %all-gather.7.cloned.1.call-update) | async-done | bytes 3735568 | tf_op jit(solution)/shard_map/all_gather | solution.py:557
  57.8 12.5 %attend.2 = (bf16[512,768]{1,0:T(8,128)(2,1)S(1)}, f32[512,768]{1,0:T(8,128)S(1)}) custom-call(bf16[512,2304]{1,0:T(8,128)(2,1)S(1)} %convolution_convert_fusion.5.q_ref.k_ref.v_ref, bf16[512,2304]{1,0:T(8,128)(2,1)S(1)} %convolution_convert_fusion.5.q_ref.k_ref.v_ref, bf16[512,2304]{1,0:T(8,128)(2,1)S(1)} %convolution_convert_fusion.5.q_ref.k_ref.v_ref, ...), custom_call_target="tpu_custom_call" | custom-call | flops 805306368 | bytes 4718592 | tf_op jit(solution)/shard_map/attend/pallas_call | solution.py:195
  79.4 5.6 all-to-all-start.1
  86.5 40.3 %all-to-all-done.1 = bf16[8,144,768]{2,1,0:T(8,128)(2,1)} async-done(((bf16[8,144,768]{2,1,0:T(8,128)(2,1)}), bf16[8,144,768]{2,1,0:T(8,128)(2,1)}, u32[]{:S(2)}, u32[]{:S(2)}) %all-to-all-start.1) | async-done | bytes 1769504 | tf_op jit(solution)/shard_map/all_to_all | solution.py:484
  126.8 8.1 %fusion.24 = f32[1152,3072]{1,0:T(8,128)S(1)} fusion(bf16[1152,768]{1,0:T(8,128)(2,1)} %bitcast.14, bf16[2,1,768,3072]{3,2,1,0:T(8,128)(2,1)} %param.22), kind=kOutput, calls=%fused_computation.38 | convolution fusion | flops 5435817984 | bytes 20643840 | tf_op jit(solution)/shard_map/dot_general | solution.py:27
  134.8 15.3 %fusion.45 = bf16[1152,768]{1,0:T(8,128)(2,1)} fusion(bf16[2,1,3072,768]{3,2,1,0:T(8,128)(2,1)} %param.23, f32[1152,3072]{1,0:T(8,128)S(1)} %fusion.24), kind=kOutput, calls=%fused_computation.70 | convolution fusion | flops 5468553216 | bytes 20643840 | tf_op jit(solution)/shard_map/dot_general | solution.py:27
  150.2 4.3 all-to-all-start.2
  159.4 35.9 %all-to-all-done.2 = bf16[8,144,768]{2,1,0:T(8,128)(2,1)} async-done(((bf16[8,144,768]{2,1,0:T(8,128)(2,1)}), bf16[8,144,768]{2,1,0:T(8,128)(2,1)}, u32[]{:S(2)}, u32[]{:S(2)}) %all-to-all-start.2) | async-done | bytes 1769504 | tf_op jit(solution)/shard_map/all_to_all | solution.py:484
  204.8 12.5 %attend.3 = (bf16[512,768]{1,0:T(8,128)(2,1)S(1)}, f32[512,768]{1,0:T(8,128)S(1)}) custom-call(bf16[512,2304]{1,0:T(8,128)(2,1)S(1)} %convolution_convert_fusion.4.q_ref.k_ref.v_ref, bf16[512,2304]{1,0:T(8,128)(2,1)S(1)} %convolution_convert_fusion.4.q_ref.k_ref.v_ref, bf16[512,2304]{1,0:T(8,128)(2,1)S(1)} %convolution_convert_fusion.4.q_ref.k_ref.v_ref, ...), custom_call_target="tpu_custom_call" | custom-call | flops 805306368 | bytes 4718592 | tf_op jit(solution)/shard_map/attend/pallas_call | solution.py:195
  236.1 4.3 all-to-all-start.3
  240.8 39.9 %all-to-all-done.3 = bf16[8,144,768]{2,1,0:T(8,128)(2,1)} async-done(((bf16[8,144,768]{2,1,0:T(8,128)(2,1)}), bf16[8,144,768]{2,1,0:T(8,128)(2,1)}, u32[]{:S(2)}, u32[]{:S(2)}) %all-to-all-start.3) | async-done | bytes 1769504 | tf_op jit(solution)/shard_map/all_to_all | solution.py:484
  280.7 11.3 %fusion.14 = f32[1152,3072]{1,0:T(8,128)} fusion(bf16[1152,768]{1,0:T(8,128)(2,1)} %bitcast.29, bf16[2,1,768,3072]{3,2,1,0:T(8,128)(2,1)} %param.22), kind=kOutput, calls=%fused_computation.28 | convolution fusion | flops 5435817984 | bytes 20643840 | tf_op jit(solution)/shard_map/dot_general | solution.py:27
  291.9 13.8 %fusion.39 = (f32[1152]{0:T(1024)S(1)}, bf16[1152,768]{1,0:T(8,128)(2,1)S(1)}, bf16[1152,768]{1,0:T(8,128)(2,1)}) fusion(bf16[1152,768]{1,0:T(8,128)(2,1)} %bitcast.10, f32[1152]{0:T(1024)S(1)} %reshape.457, bf16[2,1,3072,768]{3,2,1,0:T(8,128)(2,1)} %param.23, f32[1152,3072]{1,0:T(8,128)} %fusion.14), kind=kOutput, calls=%fused_computation.60 | convolution fusion | flops 5473860608 | bytes 24192000 | tf_op jit(solution)/shard_map/dot_general | solution.py:27
  305.7 15.4 %fusion.11 = bf16[1152,3072]{1,0:T(8,128)(2,1)} fusion(f32[1152,3072]{1,0:T(8,128)} %fusion.14, bf16[1152,768]{1,0:T(8,128)(2,1)S(1)} %get-tuple-element.54, bf16[2,1,3072,768]{3,2,1,0:T(8,128)(2,1)S(1)} %bitcast.282), kind=kOutput, calls=%fused_computation.21 | convolution fusion | flops 5503057920 | bytes 27721728 | tf_op jit(solution)/shard_map/dot_general | solution.py:31
  321.1 9.0 %fusion.51 = bf16[1152,768]{1,0:T(8,128)(2,1)} fusion(bf16[1152,3072]{1,0:T(8,128)(2,1)} %fusion.11, bf16[2,1,768,3072]{3,2,1,0:T(8,128)(2,1)S(1)} %bitcast.284), kind=kOutput, calls=%fused_computation.72 | convolution fusion | flops 5436702720 | bytes 13565952 | tf_op jit(solution)/shard_map/dot_general | solution.py:31
  330.1 13.0 %convolution_convert_fusion.3 = bf16[3072,768]{1,0:T(8,128)(2,1)} fusion(bf16[1152,768]{1,0:T(8,128)(2,1)S(1)} %get-tuple-element.54, f32[1152,3072]{1,0:T(8,128)} %fusion.14), kind=kOutput, calls=%fused_computation.25 | convolution fusion | flops 5470027776 | bytes 20643840 | tf_op jit(solution)/shard_map/dot_general | solution.py:35
  343.2 9.9 %all_to_all.50 = f32[8,1,144]{2,1,0:T(1,128)S(1)} all-to-all(f32[8,1,144]{2,1,0:T(1,128)S(1)} %reshape.460), channel_id=1, replica_groups=mesh['dp'=8,'fsdp'=4] {'dp'}, dimensions={0} | all-to-all | bytes 9216 | tf_op jit(solution)/shard_map/all_to_all | solution.py:484
  357.5 10.5 %convolution_convert_fusion.2 = bf16[768,3072]{1,0:T(8,128)(2,1)} fusion(bf16[1152,768]{1,0:T(8,128)(2,1)} %bitcast.29, bf16[1152,3072]{1,0:T(8,128)(2,1)} %fusion.11), kind=kOutput, calls=%fused_computation.24 | convolution fusion | flops 5438177280 | bytes 13565952 | tf_op jit(solution)/shard_map/dot_general | solution.py:35
  368.1 29.7 %all-to-all-done.5 = bf16[8,144,768]{2,1,0:T(8,128)(2,1)} async-done(((bf16[8,144,768]{2,1,0:T(8,128)(2,1)}), bf16[8,144,768]{2,1,0:T(8,128)(2,1)}, u32[]{:S(2)}, u32[]{:S(2)}) %all-to-all-start.5) | async-done | bytes 1769504 | tf_op jit(solution)/shard_map/all_to_all | solution.py:484
  397.7 4.5 all-to-all-start.7
  413.2 17.6 %attend_back.2 = (bf16[512,768]{1,0:T(8,128)(2,1)S(1)}, bf16[512,768]{1,0:T(8,128)(2,1)S(1)}, bf16[512,768]{1,0:T(8,128)(2,1)S(1)}, f32[6,2,1024]{2,1,0:T(2,128)S(1)}) custom-call(bf16[512,2304]{1,0:T(8,128)(2,1)S(1)} %convolution_convert_fusion.4.q_ref.k_ref.v_ref, bf16[512,2304]{1,0:T(8,128)(2,1)S(1)} %convolution_convert_fusion.4.q_ref.k_ref.v_ref, ...), custom_call_target="tpu_custom_call" | custom-call | flops 2013265920 | bytes 7864320 | tf_op jit(solution)/shard_map/attend_back/pallas_call | solution.py:219
  433.4 9.4 %all-to-all-done.7 = bf16[8,144,768]{2,1,0:T(8,128)(2,1)} async-done(((bf16[8,144,768]{2,1,0:T(8,128)(2,1)}), bf16[8,144,768]{2,1,0:T(8,128)(2,1)}, u32[]{:S(2)}, u32[]{:S(2)}) %all-to-all-start.7) | async-done | bytes 1769504 | tf_op jit(solution)/shard_map/all_to_all | solution.py:484
  475.1 41.2 %all-to-all-done.8 = bf16[8,144,768]{2,1,0:T(8,128)(2,1)S(1)} async-done(((bf16[8,144,768]{2,1,0:T(8,128)(2,1)}), bf16[8,144,768]{2,1,0:T(8,128)(2,1)S(1)}, u32[]{:S(2)}, u32[]{:S(2)}) %all-to-all-start.8) | async-done | bytes 1769504 | tf_op jit(solution)/shard_map/all_to_all | solution.py:484
  516.3 16.7 %fusion.10 = bf16[1152,3072]{1,0:T(8,128)(2,1)} fusion(f32[1152,3072]{1,0:T(8,128)} %copy-done.76, bf16[1152,768]{1,0:T(8,128)(2,1)S(1)} %bitcast.245, bf16[2,1,3072,768]{3,2,1,0:T(8,128)(2,1)} %param.23), kind=kOutput, calls=%fused_computation.20 | convolution fusion | flops 5503057920 | bytes 27721728 | tf_op jit(solution)/shard_map/dot_general | solution.py:31
  533.0 10.2 %fusion.42 = bf16[1152,768]{1,0:T(8,128)(2,1)} fusion(bf16[1152,3072]{1,0:T(8,128)(2,1)} %fusion.10, bf16[2,1,768,3072]{3,2,1,0:T(8,128)(2,1)} %param.22), kind=kOutput, calls=%fused_computation.69 | convolution fusion | flops 5436702720 | bytes 13565952 | tf_op jit(solution)/shard_map/dot_general | solution.py:31
  543.3 12.7 %convolution_convert_fusion.1 = bf16[3072,768]{1,0:T(8,128)(2,1)} fusion(bf16[1152,768]{1,0:T(8,128)(2,1)S(1)} %bitcast.246, f32[1152,3072]{1,0:T(8,128)} %copy-done.76), kind=kOutput, calls=%fused_computation.23 | convolution fusion | flops 5470027776 | bytes 20643840 | tf_op jit(solution)/shard_map/dot_general | solution.py:35
  559.7 10.7 %convolution_convert_fusion = bf16[768,3072]{1,0:T(8,128)(2,1)} fusion(bf16[1152,768]{1,0:T(8,128)(2,1)} %bitcast.14, bf16[1152,3072]{1,0:T(8,128)(2,1)} %fusion.10), kind=kOutput, calls=%fused_computation.22 | convolution fusion | flops 5438177280 | bytes 13565952 | tf_op jit(solution)/shard_map/dot_general | solution.py:35
  576.7 28.4 %all-to-all-done.9 = bf16[8,144,768]{2,1,0:T(8,128)(2,1)S(1)} async-done(((bf16[8,144,768]{2,1,0:T(8,128)(2,1)}), bf16[8,144,768]{2,1,0:T(8,128)(2,1)S(1)}, u32[]{:S(2)}, u32[]{:S(2)}) %all-to-all-start.9) | async-done | bytes 1769504 | tf_op jit(solution)/shard_map/all_to_all | solution.py:484
  612.0 17.4 %attend_back.3 = (bf16[512,768]{1,0:T(8,128)(2,1)S(1)}, bf16[512,768]{1,0:T(8,128)(2,1)S(1)}, bf16[512,768]{1,0:T(8,128)(2,1)S(1)}, f32[6,2,1024]{2,1,0:T(2,128)S(1)}) custom-call(bf16[512,2304]{1,0:T(8,128)(2,1)S(1)} %copy-done.1, bf16[512,2304]{1,0:T(8,128)(2,1)S(1)} %copy-done.1, bf16[512,2304]{1,0:T(8,128)(2,1)S(1)} %copy-done.1, ...), custom_call_target="tpu_custom_call" | custom-call | flops 2013265920 | bytes 7864320 | tf_op jit(solution)/shard_map/attend_back/pallas_call | solution.py:219
  639.2 72.4 %reduce_mixer.1 = f32[784,768]{1,0:T(8,128)S(1)} custom-call(bf16[4,192,768]{2,1,0:T(8,128)(2,1)S(1)} %bitcast.235, bf16[4,192,768]{2,1,0:T(8,128)(2,1)S(1)} %bitcast.236, bf16[4,192,768]{2,1,0:T(8,128)(2,1)S(1)} %bitcast.237, bf16[4,192,768]{2,1,0:T(8,128)(2,1)S(1)} %bitcast.234, bf16[4,16,768]{2,1,0:T(8,128)(2,1)S(1)} %bitcast.238), custom_call_target="tpu_custom_call" | custom-call | tf_op jit(solution)/shard_map/reduce_mixer/pallas_call | solution.py:443
  736.6 11.6 %reduce-scatter.12.cloned.1.call-done = bf16[192,3072]{1,0:T(8,128)(2,1)} async-done(((bf16[768,3072]{1,0:T(8,128)(2,1)}), bf16[192,3072]{1,0:T(8,128)(2,1)}) %reduce-scatter.12.cloned.1.call-update) | async-done | bytes 1179664 | tf_op jit(solution)/shard_map/reduce_scatter | solution.py:693
  (386 shorter events, 174.4 us)
Async XLA Ops:
  7.2 43.0 %all-gather.7.cloned.1.call-start = ((), (), s32[]{:S(2)}) async-start(), calls=%async_computation.15 | async-start | bytes 4669440 | tf_op jit(solution)/shard_map/all_gather | solution.py:557
  23.6 49.2 %all-to-all-start = ((bf16[8,144,768]{2,1,0:T(8,128)(2,1)}), bf16[8,144,768]{2,1,0:T(8,128)(2,1)}, u32[]{:S(2)}, u32[]{:S(2)}) async-start(bf16[8,144,768]{2,1,0:T(8,128)(2,1)} %bitcast.242), calls=%async_computation | async-start | bytes 3538944 | tf_op jit(solution)/shard_map/all_to_all | solution.py:484
  31.0 41.8 %all-gather.11.cloned.1.call-start = ((), (), s32[]{:S(2)}) async-start(), calls=%async_computation.23 | async-start | bytes 1474560 | tf_op jit(solution)/shard_map/all_gather | solution.py:558
  32.8 20.3 %copy-start.69 = (f32[512]{0:T(512)}, f32[512]{0:T(512)S(1)}, u32[]{:S(2)}) copy-start(f32[512]{0:T(512)S(1)} %get-tuple-element.202) | copy-start | bytes 6148
  53.1 22.8 %copy-start.58 = (f32[768]{0:T(1024)}, f32[768]{0:T(1024)S(1)}, u32[]{:S(2)}) copy-start(f32[768]{0:T(1024)S(1)} %get-tuple-element.154) | copy-start | bytes 9220
  75.3 124.1 %copy-start.22 = (f32[512,768]{1,0:T(8,128)}, f32[512,768]{1,0:T(8,128)S(1)}, u32[]{:S(2)}) copy-start(f32[512,768]{1,0:T(8,128)S(1)} %get-tuple-element.214) | copy-start | bytes 4718596
  77.1 79.6 %copy-start.37 = (bf16[512,768]{1,0:T(8,128)(2,1)}, bf16[512,768]{1,0:T(8,128)(2,1)S(1)}, u32[]{:S(2)}) copy-start(bf16[512,768]{1,0:T(8,128)(2,1)S(1)} %multiply_convert_fusion.6) | copy-start | bytes 2359300
  79.4 47.4 %all-to-all-start.1 = ((bf16[8,144,768]{2,1,0:T(8,128)(2,1)}), bf16[8,144,768]{2,1,0:T(8,128)(2,1)}, u32[]{:S(2)}, u32[]{:S(2)}) async-start(bf16[8,144,768]{2,1,0:T(8,128)(2,1)} %bitcast.247), calls=%async_computation.1 | async-start | bytes 3538944 | tf_op jit(solution)/shard_map/all_to_all | solution.py:484
  85.1 70.1 %all-gather.9.cloned.1.call-start = ((), (), s32[]{:S(2)}) async-start(), calls=%async_computation.16 | async-start | bytes 4669440 | tf_op jit(solution)/shard_map/all_gather | solution.py:557
  150.2 45.1 %all-to-all-start.2 = ((bf16[8,144,768]{2,1,0:T(8,128)(2,1)}), bf16[8,144,768]{2,1,0:T(8,128)(2,1)}, u32[]{:S(2)}, u32[]{:S(2)}) async-start(bf16[8,144,768]{2,1,0:T(8,128)(2,1)} %bitcast.243), calls=%async_computation.2 | async-start | bytes 3538944 | tf_op jit(solution)/shard_map/all_to_all | solution.py:484
  154.5 63.9 %all-gather.13.cloned.1.call-start = ((), (), s32[]{:S(2)}) async-start(), calls=%async_computation.24 | async-start | bytes 1474560 | tf_op jit(solution)/shard_map/all_gather | solution.py:558
  157.9 41.3 %copy-start.56 = (f32[512,2]{0,1:T(2,128)}, f32[512,2]{0,1:T(2,128)S(1)}, u32[]{:S(2)}) copy-start(f32[512,2]{0,1:T(2,128)S(1)} %select_reduce_fusion.5) | copy-start | bytes 12292
  158.0 41.3 %copy-start.60 = (f32[512]{0:T(512)}, f32[512]{0:T(512)S(1)}, u32[]{:S(2)}) copy-start(f32[512]{0:T(512)S(1)} %reduce_max.18) | copy-start | bytes 6148
  158.0 41.3 %copy-start.65 = (f32[512]{0:T(512)}, f32[512]{0:T(512)S(1)}, u32[]{:S(2)}) copy-start(f32[512]{0:T(512)S(1)} %fusion.144) | copy-start | bytes 6148
  225.9 10.2 %all-to-all-start.4 = ((f32[8,1,144]{2,1,0:T(1,128)}), f32[8,1,144]{2,1,0:T(1,128)S(1)}, u32[]{:S(2)}, u32[]{:S(2)}) async-start(f32[8,1,144]{2,1,0:T(1,128)} %reshape.456), calls=%async_computation.4 | async-start | bytes 16384 | tf_op jit(solution)/shard_map/all_to_all | solution.py:484
  236.1 44.6 %all-to-all-start.3 = ((bf16[8,144,768]{2,1,0:T(8,128)(2,1)}), bf16[8,144,768]{2,1,0:T(8,128)(2,1)}, u32[]{:S(2)}, u32[]{:S(2)}) async-start(bf16[8,144,768]{2,1,0:T(8,128)(2,1)} %bitcast.248), calls=%async_computation.3 | async-start | bytes 3538944 | tf_op jit(solution)/shard_map/all_to_all | solution.py:484
  240.4 206.1 %reduce-scatter.6.cloned.1.call-start = ((), (), s32[]{:S(2)}) async-start(), calls=%async_computation.17 | async-start | bytes 5898240 | tf_op jit(solution)/shard_map/reduce_scatter | solution.py:693
  280.7 25.0 %slice-start.1 = ((s8[9437184]{0:T(1024)(128)(4,1)}), s8[4194304]{0:T(1024)(128)(4,1)S(1)}, s32[]{:S(2)}) async-start(s8[9437184]{0:T(1024)(128)(4,1)} %bitcast.281), calls=%async_computation.26 | async-start | bytes 8388608
  280.7 25.0 %slice-start.2 = ((s8[9437184]{0:T(1024)(128)(4,1)}), s8[4194304]{0:T(1024)(128)(4,1)S(1)}, s32[]{:S(2)}) async-start(s8[9437184]{0:T(1024)(128)(4,1)} %bitcast.281), calls=%async_computation.27 | async-start | bytes 8388608
  291.9 29.2 %slice-start.4 = ((s8[9437184]{0:T(1024)(128)(4,1)}), s8[4194304]{0:T(1024)(128)(4,1)S(1)}, s32[]{:S(2)}) async-start(s8[9437184]{0:T(1024)(128)(4,1)} %bitcast.283), calls=%async_computation.29 | async-start | bytes 8388608
  291.9 29.2 %slice-start.5 = ((s8[9437184]{0:T(1024)(128)(4,1)}), s8[4194304]{0:T(1024)(128)(4,1)S(1)}, s32[]{:S(2)}) async-start(s8[9437184]{0:T(1024)(128)(4,1)} %bitcast.283), calls=%async_computation.30 | async-start | bytes 8388608
  353.2 44.6 %all-to-all-start.5 = ((bf16[8,144,768]{2,1,0:T(8,128)(2,1)}), bf16[8,144,768]{2,1,0:T(8,128)(2,1)}, u32[]{:S(2)}, u32[]{:S(2)}) async-start(bf16[8,144,768]{2,1,0:T(8,128)(2,1)} %bitcast.244), calls=%async_computation.5 | async-start | bytes 3538944 | tf_op jit(solution)/shard_map/all_to_all | solution.py:484
  357.5 117.7 %reduce-scatter.8.cloned.1.call-start = ((), (), s32[]{:S(2)}) async-start(), calls=%async_computation.18 | async-start | bytes 5898240 | tf_op jit(solution)/shard_map/reduce_scatter | solution.py:693
  397.7 45.1 %all-to-all-start.7 = ((bf16[8,144,768]{2,1,0:T(8,128)(2,1)}), bf16[8,144,768]{2,1,0:T(8,128)(2,1)}, u32[]{:S(2)}, u32[]{:S(2)}) async-start(bf16[8,144,768]{2,1,0:T(8,128)(2,1)} %bitcast.241), calls=%async_computation.7 | async-start | bytes 3538944 | tf_op jit(solution)/shard_map/all_to_all | solution.py:484
  402.2 130.8 %reduce-scatter.10.cloned.1.call-start = ((), (), s32[]{:S(2)}) async-start(), calls=%async_computation.19 | async-start | bytes 6021120 | tf_op jit(solution)/shard_map/reduce_scatter | solution.py:751
  471.5 44.9 %all-to-all-start.8 = ((bf16[8,144,768]{2,1,0:T(8,128)(2,1)}), bf16[8,144,768]{2,1,0:T(8,128)(2,1)S(1)}, u32[]{:S(2)}, u32[]{:S(2)}) async-start(bf16[8,144,768]{2,1,0:T(8,128)(2,1)} %bitcast.39), calls=%async_computation.9 | async-start | bytes 3538944 | tf_op jit(solution)/shard_map/all_to_all | solution.py:484
  475.1 236.6 %all-reduce.8.cloned.1.call-start = ((), (), s32[]{:S(2)}) async-start(), calls=%async_computation.20 | async-start | bytes 2408448 | tf_op jit(solution)/shard_map/psum | solution.py:685
  543.3 189.5 %reduce-scatter.14.cloned.1.call-start = ((), (), s32[]{:S(2)}) async-start(), calls=%async_computation.22 | async-start | bytes 5898240 | tf_op jit(solution)/shard_map/reduce_scatter | solution.py:693
  556.1 49.0 %all-to-all-start.9 = ((bf16[8,144,768]{2,1,0:T(8,128)(2,1)}), bf16[8,144,768]{2,1,0:T(8,128)(2,1)S(1)}, u32[]{:S(2)}, u32[]{:S(2)}) async-start(bf16[8,144,768]{2,1,0:T(8,128)(2,1)} %bitcast.46), calls=%async_computation.12 | async-start | bytes 3538944 | tf_op jit(solution)/shard_map/all_to_all | solution.py:484
  559.7 188.5 %reduce-scatter.12.cloned.1.call-start = ((), (), s32[]{:S(2)}) async-start(), calls=%async_computation.21 | async-start | bytes 5898240 | tf_op jit(solution)/shard_map/reduce_scatter | solution.py:693
  574.6 30.4 %copy-start.33 = (bf16[1152,512]{1,0:T(8,128)(2,1)S(1)}, bf16[1152,512]{1,0:T(8,128)(2,1)}, u32[]{:S(2)}) copy-start(bf16[1152,512]{1,0:T(8,128)(2,1)} %copy-done.31) | copy-start | bytes 3538948
  612.0 17.4 %copy-start.43 = (bf16[768,2432]{1,0:T(8,128)(2,1)S(1)}, bf16[768,2432]{1,0:T(8,128)(2,1)}, u32[]{:S(2)}) copy-start(bf16[768,2432]{1,0:T(8,128)(2,1)} %all-gather.7.cloned.1.call-done) | copy-start | bytes 11206660
  (71 other events, 204.5 us)
Sparse Core Ops, SparseCore 0:
  15.5 34.6 all-gather.6
  52.3 17.4 all-gather.10
  88.0 32.3 all-gather.8
  157.2 17.8 all-gather.12
  343.3 46.0 reduce-scatter.5
  392.3 47.9 reduce-scatter.7
  463.1 46.6 reduce-scatter.9
  543.4 102.9 all-reduce.7
  649.5 48.8 reduce-scatter.13
  701.3 46.8 reduce-scatter.11

commit v4 on v3

--- a/solution.py
+++ b/solution.py
@@ -465,6 +465,258 @@
     )(*changes, small)
 
 
+def partner_of(me, index):
+    other = me
+    for bit, weight in ((1, 1), (2, 4), (4, 2)):
+        if index & bit:
+            other = other + weight * (1 - 2 * (lax.rem(me // weight, 2)))
+    return other
+
+
+def flip_row(row):
+    count = row.shape[1]
+    down = lax.broadcasted_iota(jnp.int32, (count, count), 0)
+    along = lax.broadcasted_iota(jnp.int32, (count, count), 1)
+    return jnp.sum(jnp.where(down == along, row, 0.0), axis=1, keepdims=True)
+
+
+def flip_column(column):
+    count = column.shape[0]
+    down = lax.broadcasted_iota(jnp.int32, (count, count), 0)
+    along = lax.broadcasted_iota(jnp.int32, (count, count), 1)
+    return jnp.sum(jnp.where(down == along, column, 0.0), axis=0, keepdims=True)
+
+
+def run_experts(mode, tile, *refs):
+    refs = list(refs)
+
+    def take(count):
+        taken = refs[:count]
+        del refs[:count]
+        return taken
+
+    sent, up_any, down_any = take(3)
+    if mode == "forward":
+        home, rows_in, activity_any, slope_any = take(4)
+    elif mode == "backward":
+        (slope_any,) = take(1)
+        home, rows_in, inner_any = take(3)
+    else:
+        gates, early = take(2)
+        home, rows_in, activity_any, inner_any, scaled, result, places = take(7)
+    up, down, ready = take(3)
+    if mode == "forward":
+        activity, slope = take(2)
+        outs = [(activity, activity_any), (slope, slope_any)]
+    elif mode == "backward":
+        slope, inner = take(2)
+        outs = [(inner, inner_any)]
+    else:
+        activity, inner, gates_in, place_out = take(4)
+        outs = [(activity, activity_any), (inner, inner_any)]
+    load, own, stores, go_send, go_recv, back_send, back_recv = take(7)
+    if mode == "both":
+        gate_send, gate_recv, place_send, place_recv = take(4)
+
+    owners, capacity, width = sent.shape
+    hidden = up.shape[1]
+    me = lax.axis_index("dp")
+    barrier = pltpu.get_barrier_semaphore()
+    for index in range(1, owners):
+        pl.semaphore_signal(
+            barrier,
+            inc=1,
+            device_id={"dp": partner_of(me, index)},
+            device_id_type=pl.DeviceIdType.MESH,
+        )
+    pl.semaphore_wait(barrier, owners - 1)
+
+    going = {}
+    gate_going = {}
+    for index in range(1, owners):
+        other = partner_of(me, index)
+        copy = mesh_copy(
+            sent.at[other], rows_in.at[index], go_send, go_recv, index, {"dp": other}
+        )
+        copy.start()
+        going[index] = copy
+        if mode == "both":
+            copy = mesh_copy(
+                gates.at[other], gates_in.at[index], gate_send, gate_recv, index, {"dp": other}
+            )
+            copy.start()
+            gate_going[index] = copy
+    first = [pltpu.make_async_copy(sent.at[me], rows_in.at[0], own.at[0])]
+    if mode == "both":
+        first.append(pltpu.make_async_copy(gates.at[me], gates_in.at[0], own.at[1]))
+    first.append(pltpu.make_async_copy(up_any, up, load.at[0]))
+    first.append(pltpu.make_async_copy(down_any, down, load.at[1]))
+    if mode == "backward":
+        first.append(pltpu.make_async_copy(slope_any, slope, load.at[2]))
+    for copy in first:
+        copy.start()
+
+    coming = []
+    for pair in range(owners // 2):
+        blocks = (2 * pair, 2 * pair + 1)
+        both = pl.ds(2 * pair, 2)
+        count = 2 * capacity
+        if pair == 0:
+            for copy in first:
+                copy.wait()
+        for index in blocks:
+            if index:
+                going[index].wait_recv()
+                if mode == "both":
+                    gate_going[index].wait_recv()
+        if mode == "both":
+            for index in blocks:
+                gate = flip_row(gates_in[index][:, :capacity])
+                rows = early[partner_of(me, index)].astype(jnp.float32)
+                scaled[index] = low(gate * rows)
+
+        def widen(step, carry):
+            columns = pl.ds(pl.multiple_of(step * tile, tile), tile)
+            rows = rows_in[both].reshape(count, width)
+            if mode == "backward":
+                back = dot_last(rows, down[columns, :])
+                inner[pair, :, columns] = low(back * slope[pair, :, columns].astype(jnp.float32))
+                return carry
+            value, steep = smooth_pair(dot(rows, up[:, columns]))
+            activity[pair, :, columns] = low(value)
+            if mode == "forward":
+                slope[pair, :, columns] = low(steep)
+            else:
+                back = dot_last(scaled[both].reshape(count, width), down[columns, :])
+                inner[pair, :, columns] = low(back * steep)
+            return carry
+
+        lax.fori_loop(0, hidden // tile, widen, 0)
+        for at, (source, target) in enumerate(outs):
+            copy = pltpu.make_async_copy(
+                source.at[pair], target.at[pair], stores.at[at * (owners // 2) + pair]
+            )
+            copy.start()
+            coming.append(copy)
+
+        def narrow(step, carry):
+            columns = pl.ds(pl.multiple_of(step * 256, 256), 256)
+            if mode == "forward":
+                rows = dot(activity[pair], down[:, columns])
+            else:
+                rows = dot_last(inner[pair], up[columns, :])
+            ready[both, :, columns] = low(rows).reshape(2, capacity, 256)
+            return carry
+
+        lax.fori_loop(0, width // 256, narrow, 0)
+        for index in blocks:
+            other = partner_of(me, index)
+            if index:
+                copy = mesh_copy(
+                    ready.at[index], home.at[me], back_send, back_recv, index, {"dp": other}
+                )
+            else:
+                copy = pltpu.make_async_copy(ready.at[index], home.at[me], own.at[2])
+            copy.start()
+            coming.append(copy)
+
+        if mode == "both":
+
+            def finish(step, carry):
+                columns = pl.ds(pl.multiple_of(step * 256, 256), 256)
+                rows = low(dot(activity[pair], down[:, columns])).reshape(2, capacity, 256)
+                sums = []
+                for at, index in enumerate(blocks):
+                    other = partner_of(me, index)
+                    result[other, :, columns] = rows[at]
+                    sums.append(
+                        jnp.sum(
+                            early[other, :, columns].astype(jnp.float32)
+                            * rows[at].astype(jnp.float32),
+                            axis=1,
+                            keepdims=True,
+                        )
+                    )
+                return tuple(old + new for old, new in zip(carry, sums))
+
+            zero = jnp.zeros((capacity, 1), jnp.float32)
+            totals = lax.fori_loop(0, width // 256, finish, (zero, zero))
+            for at, index in enumerate(blocks):
+                other = partner_of(me, index)
+                place_out[index, :, :capacity] = flip_column(totals[at])
+                if index:
+                    copy = mesh_copy(
+                        place_out.at[index],
+                        places.at[me],
+                        place_send,
+                        place_recv,
+                        index,
+                        {"dp": other},
+                    )
+                else:
+                    copy = pltpu.make_async_copy(place_out.at[index], places.at[me], own.at[3])
+                copy.start()
+                coming.append(copy)
+
+    for index in range(1, owners):
+        going[index].wait_send()
+        if mode == "both":
+            gate_going[index].wait_send()
+    for copy in coming:
+        copy.wait()
+
+
+def experts_in_kernel(mode, sent, up_matrix, down_matrix, extra=()):
+    owners, capacity, width = sent.shape
+    hidden = up_matrix.shape[1]
+    pairs = owners // 2
+    low_type = jnp.bfloat16
+    near = pl.BlockSpec(memory_space=pltpu.VMEM)
+    far = pl.BlockSpec(memory_space=pl.ANY)
+    rows = jax.ShapeDtypeStruct((owners, capacity, width), low_type)
+    wide = jax.ShapeDtypeStruct((pairs, 2 * capacity, hidden), low_type)
+    wide_scratch = pltpu.VMEM((pairs, 2 * capacity, hidden), low_type)
+    lines = -(-capacity // LANES) * LANES
+    line = jax.ShapeDtypeStruct((owners, 1, lines), jnp.float32)
+    line_scratch = pltpu.VMEM((owners, 1, lines), jnp.float32)
+    many = pltpu.SemaphoreType.DMA((owners,))
+    if mode == "forward":
+        ins, outs = [near, far, far], [(rows, near), (rows, near), (wide, far), (wide, far)]
+        scratch = [wide_scratch] * 2
+    elif mode == "backward":
+        ins, outs = [near, far, far, far], [(rows, near), (rows, near), (wide, far)]
+        scratch = [wide_scratch] * 2
+    else:
+        ins = [near, far, far, near, near]
+        outs = [(rows, near), (rows, near), (wide, far), (wide, far)]
+        outs += [(rows, near), (rows, near), (line, near)]
+        scratch = [wide_scratch] * 2 + [line_scratch] * 2
+    return pl.pallas_call(
+        functools.partial(run_experts, mode, 512),
+        out_shape=tuple(shape for shape, _ in outs),
+        in_specs=ins,
+        out_specs=tuple(spec for _, spec in outs),
+        scratch_shapes=[
+            pltpu.VMEM(up_matrix.shape, low_type),
+            pltpu.VMEM(down_matrix.shape, low_type),
+            pltpu.VMEM((owners, capacity, width), low_type),
+        ]
+        + scratch
+        + [
+            pltpu.SemaphoreType.DMA((3,)),
+            pltpu.SemaphoreType.DMA((4,)),
+            pltpu.SemaphoreType.DMA((2 * pairs,)),
+        ]
+        + [many] * (8 if mode == "both" else 4),
+        compiler_params=pltpu.CompilerParams(
+            collective_id={"forward": 2, "backward": 3, "both": 4}[mode],
+            has_side_effects=True,
+            vmem_limit_bytes=56 << 20,
+        ),
+        name="experts_" + mode,
+    )(sent, up_matrix, down_matrix, *extra)
+
+
 def plan_routes(routes, experts, capacity):
     length = routes.shape[0]
     flat = routes.reshape(-1)
@@ -543,6 +795,7 @@
     experts = owners * EXP_DEV
     heads = position_bias.shape[1] * shards
     capacity = max(2, 9 * length * TOP // (8 * experts))
+    fused = shards == 4 and owners == 8 and capacity % 16 == 0
     taken, pick, both, chosen = plan_routes(routes, experts, capacity)
     offsets = offset_selector(length)
 
@@ -593,27 +846,60 @@
         picked = jnp.sum(jnp.where(chosen, logits[:, None, :], 0.0), axis=-1)
         gates = jax.nn.softmax(picked, axis=-1)
         gate_line = gates.T.reshape(-1)
-        received = exchange_rows(low(dot(both, normed_expert)), experts)
-        if layer == layers - 1:
-            gate_places = exchange_numbers(
-                jnp.sum(jnp.where(taken, gate_line[None, :], 0.0), axis=1), experts
-            )
-            received, gate_places = lax.optimization_barrier((received, gate_places))
-        inner = dot(received, up_matrix)
-        activity, slope = smooth_pair(inner)
-        activity = low(activity)
-        result = low(dot(activity, down_matrix))
-        if layer == layers - 1:
-            back_places = jnp.sum(early.astype(jnp.float32) * result.astype(jnp.float32), axis=1)
-            back_places = exchange_numbers(back_places, experts)
-            back_sent = low(gate_places[:, None] * early.astype(jnp.float32))
-            back_inner = low(dot_last(back_sent, down_matrix) * slope)
-            back_rows, back_sent = lax.optimization_barrier(
-                (low(dot_last(back_inner, up_matrix)), back_sent)
-            )
-            back_rows = exchange_rows(back_rows, experts)
-            last = (back_places, back_sent, back_inner, back_rows)
-        returned = exchange_rows(result, experts)
+        sent = low(dot(both, normed_expert))
+        slope = None
+        if fused and layer < layers - 1:
+            returned, received, activity, slope = experts_in_kernel(
+                "forward", sent.reshape(experts, capacity, width), up_matrix, down_matrix
+            )
+            returned = returned.reshape(-1, width)
+            received = received.reshape(-1, width)
+            activity = activity.reshape(received.shape[0], -1)
+        elif fused:
+            gate_places = jnp.sum(jnp.where(taken, gate_line[None, :], 0.0), axis=1)
+            gate_places = gate_places.reshape(experts, 1, capacity)
+            gate_places = jnp.pad(gate_places, ((0, 0), (0, 0), (0, -capacity % LANES)))
+            back_rows, received, activity, back_inner, back_sent, result, back_places = (
+                experts_in_kernel(
+                    "both",
+                    sent.reshape(experts, capacity, width),
+                    up_matrix,
+                    down_matrix,
+                    (gate_places, early.reshape(experts, capacity, width)),
+                )
+            )
+            count = experts * capacity
+            last = (
+                back_places[:, 0, :capacity].reshape(-1),
+                back_sent.reshape(count, width),
+                back_inner.reshape(count, -1),
+                back_rows.reshape(count, width),
+            )
+            received = received.reshape(count, width)
+            activity = activity.reshape(count, -1)
+            returned = exchange_rows(result.reshape(count, width), experts)
+        else:
+            received = exchange_rows(sent, experts)
+            if layer == layers - 1:
+                gate_places = exchange_numbers(
+                    jnp.sum(jnp.where(taken, gate_line[None, :], 0.0), axis=1), experts
+                )
+                received, gate_places = lax.optimization_barrier((received, gate_places))
+            inner = dot(received, up_matrix)
+            activity, slope = smooth_pair(inner)
+            activity = low(activity)
+            result = low(dot(activity, down_matrix))
+            if layer == layers - 1:
+                back_places = jnp.sum(early.astype(jnp.float32) * result.astype(jnp.float32), axis=1)
+                back_places = exchange_numbers(back_places, experts)
+                back_sent = low(gate_places[:, None] * early.astype(jnp.float32))
+                back_inner = low(dot_last(back_sent, down_matrix) * slope)
+                back_rows, back_sent = lax.optimization_barrier(
+                    (low(dot_last(back_inner, up_matrix)), back_sent)
+                )
+                back_rows = exchange_rows(back_rows, experts)
+                last = (back_places, back_sent, back_inner, back_rows)
+            returned = exchange_rows(result, experts)
         routed = None
         if layer < layers - 1:
             routed, update = gather_rows(pick, returned, gates)
@@ -676,17 +962,33 @@
             gated = jnp.concatenate(
                 [low(gates[:, choice : choice + 1] * back_out) for choice in range(TOP)], axis=0
             )
-            back_sent = exchange_rows(low(dot(pick, gated)), experts)
+            back_sent = low(dot(pick, gated))
             up_above, down_above = expert_results[layer + 1]
-            back_sent, up_above = lax.optimization_barrier((back_sent, up_above))
+            if fused:
+                back_rows, back_sent, back_inner = experts_in_kernel(
+                    "backward",
+                    back_sent.reshape(experts, capacity, width),
+                    up_matrix,
+                    down_matrix,
+                    (slope,),
+                )
+                back_rows, back_sent, up_above, above = lax.optimization_barrier(
+                    (back_rows, back_sent, up_above, above)
+                )
+                back_rows = back_rows.reshape(-1, width)
+                back_sent = back_sent.reshape(-1, width)
+                back_inner = back_inner.reshape(back_sent.shape[0], -1)
+            else:
+                back_sent = exchange_rows(back_sent, experts)
+                back_sent, up_above = lax.optimization_barrier((back_sent, up_above))
+                back_inner = low(dot_last(back_sent, down_matrix) * slope)
+                back_inner, above = lax.optimization_barrier((back_inner, above))
+                back_rows, back_sent = lax.optimization_barrier(
+                    (low(dot_last(back_inner, up_matrix)), back_sent)
+                )
+                back_rows = exchange_rows(back_rows, experts)
             expert_results[layer + 1] = (up_above, down_above)
-            back_inner = low(dot_last(back_sent, down_matrix) * slope)
-            back_inner, above = lax.optimization_barrier((back_inner, above))
             mixer_results[layer + 1] = lax.psum(above, "dp")
-            back_rows, back_sent = lax.optimization_barrier(
-                (low(dot_last(back_inner, up_matrix)), back_sent)
-            )
-            back_rows = exchange_rows(back_rows, experts)
         down_change = low(dot_first(activity, back_sent))
         up_change = low(dot_first(received, back_inner))
         expert_results[layer] = tuple(

time: 768 us -> 712 us (0.927)
  Pallas kernels: 132 us -> 388 us
  waiting for transfers between devices: 257 us -> 72.1 us
  matrix products: 213 us -> 112 us
  starting transfers between devices: 42.5 us -> 21.8 us
  blocking collectives: 9.94 us -> 0 us
    pallas_call x0 -> x3, Pallas kernels: none -> 241 us  [experts_in_kernel(): pl.pallas_call(functools.partial(run_experts, mode, 512), out_shape=tuple...]
    all_to_all x9 -> x2, waiting for transfers between devices: 228 us -> 6.06 us  [exchange(): return lax.all_to_all(values, 'dp', split_axis=0, concat_axis=0, tiled=True)]
    dot_general x14 -> x10, matrix products: 68.9 us -> 18.6 us  [dot_last(): lax.dot_general(left, right, contract_last, preferred_element_type=jnp.fl...]
    dot_general x14 -> x10, matrix products: 73.8 us -> 23.9 us  [dot(): return jnp.dot(left, right, preferred_element_type=jnp.float32)]
    reduce_scatter x4, waiting for transfers between devices: 11.6 us -> 36 us  [per_device(): lax.psum_scatter(change, 'fsdp', scatter_dimension=0, tiled=True)]
    all_to_all x9 -> x2, starting transfers between devices: 41.3 us -> 20.1 us  [exchange(): return lax.all_to_all(values, 'dp', split_axis=0, concat_axis=0, tiled=True)]
    squeeze x0 -> x2, local copies, waits for them, and re-layouts: none -> 16.4 us  [per_device(): up_matrix, down_matrix = (expert_up[layer, 0], expert_down[layer, 0])]
    pallas_call x1, Pallas kernels: 72.4 us -> 88 us  [reduce_in_kernel(): pl.pallas_call(functools.partial(reduce_mixer, owners, chunks), out_shape...]
  transfers between devices with their start and end apart: 19 -> 12, of which waited for: 10 -> 5; matrix products, arithmetic and copies ran while one was open for 24% -> 22% of each run, Pallas kernels for 17% -> 43%
where the time goes in v4:
time: 712 us; the launch traced here: 707 us
  Pallas kernels  388 us (54%)
  matrix products  112 us (16%)
  waiting for transfers between devices  72.1 us (10%)
  local copies, waits for them, and re-layouts  59.1 us (8%)
  other arithmetic  37.3 us (5%)
  starting transfers between devices  21.8 us (3%)
  between operations  15.6 us (2%)
    pallas_call x3, Pallas kernels, experts_in_kernel(): pl.pallas_call(functools.partial(run_experts, mode, 512), out_shape=tuple...  241 us
    pallas_call x1, Pallas kernels, reduce_in_kernel(): pl.pallas_call(functools.partial(reduce_mixer, owners, chunks), out_shape...  88 us
    dot_general x18, matrix products, dot_first(): lax.dot_general(left, right, contract_first, preferred_element_type=jnp.f...  69.3 us
    reduce_scatter x4, waiting for transfers between devices, per_device(): lax.psum_scatter(change, 'fsdp', scatter_dimension=0, tiled=True)  36 us
    pallas_call x2, Pallas kernels, attention_backward(): pl.pallas_call(functools.partial(attend_back, pair, size ** (-0.5)), grid...  34.6 us
    unnamed x127, local copies, waits for them, and re-layouts  27.9 us
    pallas_call x2, Pallas kernels, attention_forward(): pl.pallas_call(functools.partial(attend, pair, size ** (-0.5)), grid=(gro...  25 us
    dot_general x10, matrix products, dot(): return jnp.dot(left, right, preferred_element_type=jnp.float32)  23.9 us
  transfers between devices with their start and end apart: 12, of which 5 were waited for; matrix products, arithmetic and copies ran while one was open for 22% of the time, Pallas kernels for 43%

profile of v4, /device:TPU:0, one launch (start us, length us, event | category | flops | bytes accessed | tf_op | source)
XLA Modules:
  0.0 706.5 jit_solution(12615670182234600155)
XLA Ops:
  23.4 7.5 %all-to-all-start = ((bf16[8,144,768]{2,1,0:T(8,128)(2,1)}), bf16[8,144,768]{2,1,0:T(8,128)(2,1)}, u32[]{:S(2)}, u32[]{:S(2)}) async-start(bf16[8,144,768]{2,1,0:T(8,128)(2,1)} %bitcast.219), calls=%async_computation | async-start | bytes 3538944 | tf_op jit(solution)/shard_map/all_to_all | solution.py:736
  32.2 8.4 %slice_bitcast_fusion.1 = (bf16[768,3072]{1,0:T(8,128)(2,1)}, bf16[768,3072]{1,0:T(8,128)(2,1)}) fusion(bf16[2,1,768,3072]{3,2,1,0:T(8,128)(2,1)} %param.22), kind=kLoop, calls=%fused_computation.7 | loop fusion | bytes 18874368 | tf_op jit(solution)/shard_map/squeeze | solution.py:835
  40.6 8.0 %slice_bitcast_fusion = (bf16[3072,768]{1,0:T(8,128)(2,1)}, bf16[3072,768]{1,0:T(8,128)(2,1)}) fusion(bf16[2,1,3072,768]{3,2,1,0:T(8,128)(2,1)} %param.23), kind=kLoop, calls=%fused_computation.6 | loop fusion | bytes 18874368 | tf_op jit(solution)/shard_map/squeeze | solution.py:835
  51.5 4.1 convolution_convert_fusion.5.q_ref.k_ref.v_ref
  55.6 12.5 %attend.2 = (bf16[512,768]{1,0:T(8,128)(2,1)S(1)}, f32[512,768]{1,0:T(8,128)S(1)}) custom-call(bf16[512,2304]{1,0:T(8,128)(2,1)S(1)} %convolution_convert_fusion.5.q_ref.k_ref.v_ref, bf16[512,2304]{1,0:T(8,128)(2,1)S(1)} %convolution_convert_fusion.5.q_ref.k_ref.v_ref, bf16[512,2304]{1,0:T(8,128)(2,1)S(1)} %convolution_convert_fusion.5.q_ref.k_ref.v_ref, ...), custom_call_target="tpu_custom_call" | custom-call | flops 805306368 | bytes 4718592 | tf_op jit(solution)/shard_map/attend/pallas_call | solution.py:195
  80.1 21.1 %all-gather.9.cloned.1.call-done = bf16[768,2432]{1,0:T(8,128)(2,1)} async-done(((bf16[192,2432]{1,0:T(8,128)(2,1)}), bf16[768,2432]{1,0:T(8,128)(2,1)}) %all-gather.9.cloned.1.call-update) | async-done | bytes 3735568 | tf_op jit(solution)/shard_map/all_gather | solution.py:810
  102.8 76.2 %experts_forward.1 = (bf16[8,144,768]{2,1,0:T(8,128)(2,1)}, bf16[8,144,768]{2,1,0:T(8,128)(2,1)}, bf16[4,288,3072]{2,1,0:T(8,128)(2,1)}, bf16[4,288,3072]{2,1,0:T(8,128)(2,1)}) custom-call(bf16[8,144,768]{2,1,0:T(8,128)(2,1)} %bitcast.220, bf16[768,3072]{1,0:T(8,128)(2,1)} %get-tuple-element.190.refs_1_, bf16[3072,768]{1,0:T(8,128)(2,1)} %get-tuple-element.188.refs_2_), custom_call_target="tpu_custom_call" | custom-call | tf_op jit(solution)/shard_map/experts_forward/pallas_call | solution.py:694
  179.3 4.0 fusion.14
  187.9 12.5 %attend.3 = (bf16[512,768]{1,0:T(8,128)(2,1)S(1)}, f32[512,768]{1,0:T(8,128)S(1)}) custom-call(bf16[512,2304]{1,0:T(8,128)(2,1)S(1)} %convolution_convert_fusion.4.q_ref.k_ref.v_ref, bf16[512,2304]{1,0:T(8,128)(2,1)S(1)} %convolution_convert_fusion.4.q_ref.k_ref.v_ref, bf16[512,2304]{1,0:T(8,128)(2,1)S(1)} %convolution_convert_fusion.4.q_ref.k_ref.v_ref, ...), custom_call_target="tpu_custom_call" | custom-call | flops 805306368 | bytes 4718592 | tf_op jit(solution)/shard_map/attend/pallas_call | solution.py:195
  212.5 88.0 %experts_both.1 = (bf16[8,144,768]{2,1,0:T(8,128)(2,1)}, bf16[8,144,768]{2,1,0:T(8,128)(2,1)}, bf16[4,288,3072]{2,1,0:T(8,128)(2,1)}, bf16[4,288,3072]{2,1,0:T(8...) custom-call(bf16[8,144,768]{2,1,0:T(8,128)(2,1)} %bitcast.221, ...), custom_call_target="tpu_custom_call" | custom-call | tf_op jit(solution)/shard_map/experts_both/pallas_call | solution.py:694
  300.5 10.6 %convolution_convert_fusion.3 = bf16[3072,768]{1,0:T(8,128)(2,1)} fusion(bf16[1152,3072]{1,0:T(8,128)(2,1)} %bitcast.256, bf16[1152,768]{1,0:T(8,128)(2,1)} %bitcast.261), kind=kOutput, calls=%fused_computation.3 | convolution fusion | flops 5438177280 | bytes 13565952 | tf_op jit(solution)/shard_map/dot_general | solution.py:35
  311.1 10.5 %convolution_convert_fusion.2 = bf16[768,3072]{1,0:T(8,128)(2,1)} fusion(bf16[1152,768]{1,0:T(8,128)(2,1)} %bitcast.260, bf16[1152,3072]{1,0:T(8,128)(2,1)} %bitcast.255), kind=kOutput, calls=%fused_computation.2 | convolution fusion | flops 5438177280 | bytes 13565952 | tf_op jit(solution)/shard_map/dot_general | solution.py:35
  322.4 12.6 %all-to-all-start.1 = ((bf16[8,144,768]{2,1,0:T(8,128)(2,1)}), bf16[8,144,768]{2,1,0:T(8,128)(2,1)}, u32[]{:S(2)}, u32[]{:S(2)}) async-start(bf16[8,144,768]{2,1,0:T(8,128)(2,1)} %get-tuple-element.68), calls=%async_computation.1 | async-start | bytes 3538944 | tf_op jit(solution)/shard_map/all_to_all | solution.py:736
  338.0 3.2 fusion.110
  349.1 17.2 %attend_back.2 = (bf16[512,768]{1,0:T(8,128)(2,1)S(1)}, bf16[512,768]{1,0:T(8,128)(2,1)S(1)}, bf16[512,768]{1,0:T(8,128)(2,1)S(1)}, f32[6,2,1024]{2,1,0:T(2,128)S(1)}) custom-call(bf16[512,2304]{1,0:T(8,128)(2,1)S(1)} %copy-done.1, bf16[512,2304]{1,0:T(8,128)(2,1)S(1)} %copy-done.1, bf16[512,2304]{1,0:T(8,128)(2,1)S(1)} %copy-done.1, ...), custom_call_target="tpu_custom_call" | custom-call | flops 2013265920 | bytes 7864320 | tf_op jit(solution)/shard_map/attend_back/pallas_call | solution.py:219
  369.2 3.2 convolution_convert_fusion.13
  372.4 3.2 all-to-all-done.1
  380.7 3.5 multiply_reduce_fusion.3
  394.9 3.8 fusion.18
  399.8 3.4 fusion.6
  403.3 76.7 %experts_backward.1 = (bf16[8,144,768]{2,1,0:T(8,128)(2,1)}, bf16[8,144,768]{2,1,0:T(8,128)(2,1)}, bf16[4,288,3072]{2,1,0:T(8,128)(2,1)}) custom-call(bf16[8,144,768]{2,1,0:T(8,128)(2,1)} %bitcast.216, bf16[768,3072]{1,0:T(8,128)(2,1)} %get-tuple-element.190.refs_1_, bf16[3072,768]{1,0:T(8,128)(2,1)} %get-tuple-element.188.refs_2_, ...), custom_call_target="tpu_custom_call" | custom-call | tf_op jit(solution)/shard_map/experts_backward/pallas_call | solution.py:694
  479.9 10.9 %convolution_convert_fusion = bf16[768,3072]{1,0:T(8,128)(2,1)} fusion(bf16[1152,768]{1,0:T(8,128)(2,1)S(1)} %bitcast.258, bf16[1152,3072]{1,0:T(8,128)(2,1)} %bitcast.257), kind=kOutput, calls=%fused_computation | convolution fusion | flops 5438177280 | bytes 13565952 | tf_op jit(solution)/shard_map/dot_general | solution.py:35
  491.9 10.6 %convolution_convert_fusion.1 = bf16[3072,768]{1,0:T(8,128)(2,1)} fusion(bf16[1152,3072]{1,0:T(8,128)(2,1)} %bitcast.254, bf16[1152,768]{1,0:T(8,128)(2,1)} %bitcast.259), kind=kOutput, calls=%fused_computation.1 | convolution fusion | flops 5438177280 | bytes 13565952 | tf_op jit(solution)/shard_map/dot_general | solution.py:35
  502.5 4.2 fusion.15
  508.7 3.2 fusion.111
  517.3 17.4 %attend_back.3 = (bf16[512,768]{1,0:T(8,128)(2,1)S(1)}, bf16[512,768]{1,0:T(8,128)(2,1)S(1)}, bf16[512,768]{1,0:T(8,128)(2,1)S(1)}, f32[6,2,1024]{2,1,0:T(2,128)S(1)}) custom-call(bf16[512,2304]{1,0:T(8,128)(2,1)S(1)} %convolution_convert_fusion.5.q_ref.k_ref.v_ref, bf16[512,2304]{1,0:T(8,128)(2,1)S(1)} %convolution_convert_fusion.5.q_ref.k_ref.v_ref, ...), custom_call_target="tpu_custom_call" | custom-call | flops 2013265920 | bytes 7864320 | tf_op jit(solution)/shard_map/attend_back/pallas_call | solution.py:219
  544.5 88.0 %reduce_mixer.1 = f32[784,768]{1,0:T(8,128)S(1)} custom-call(bf16[4,192,768]{2,1,0:T(8,128)(2,1)S(1)} %bitcast.211, bf16[4,192,768]{2,1,0:T(8,128)(2,1)S(1)} %bitcast.212, bf16[4,192,768]{2,1,0:T(8,128)(2,1)S(1)} %bitcast.213, bf16[4,192,768]{2,1,0:T(8,128)(2,1)S(1)} %bitcast.210, bf16[4,16,768]{2,1,0:T(8,128)(2,1)S(1)} %bitcast.214), custom_call_target="tpu_custom_call" | custom-call | tf_op jit(solution)/shard_map/reduce_mixer/pallas_call | solution.py:443
  634.1 4.1 fusion.7
  638.2 7.6 %all-reduce.9.cloned.1.call-done = bf16[784,768]{1,0:T(8,128)(2,1)} async-done(((bf16[784,768]{1,0:T(8,128)(2,1)}), bf16[784,768]{1,0:T(8,128)(2,1)}) %all-reduce.9.cloned.1.call-update) | async-done | bytes 1204240 | tf_op jit(solution)/shard_map/psum | solution.py:991
  645.8 2.9 convert_element_type.447
  659.6 36.0 %reduce-scatter.14.cloned.1.call-done = bf16[768,768]{1,0:T(8,128)(2,1)} async-done(((bf16[3072,768]{1,0:T(8,128)(2,1)}), bf16[768,768]{1,0:T(8,128)(2,1)}) %reduce-scatter.14.cloned.1.call-update) | async-done | bytes 1179664 | tf_op jit(solution)/shard_map/reduce_scatter | solution.py:995
  695.7 3.8 fusion.8
  (313 shorter events, 112.1 us)
Async XLA Ops:
  7.2 4.5 copy-start.52
  7.2 4.5 copy-start.53
  7.2 41.4 %all-gather.7.cloned.1.call-start = ((), (), s32[]{:S(2)}) async-start(), calls=%async_computation.7 | async-start | bytes 4669440 | tf_op jit(solution)/shard_map/all_gather | solution.py:810
  12.9 59.3 %all-gather.11.cloned.1.call-start = ((), (), s32[]{:S(2)}) async-start(), calls=%async_computation.15 | async-start | bytes 1474560 | tf_op jit(solution)/shard_map/all_gather | solution.py:811
  14.0 87.2 %all-gather.9.cloned.1.call-start = ((), (), s32[]{:S(2)}) async-start(), calls=%async_computation.8 | async-start | bytes 4669440 | tf_op jit(solution)/shard_map/all_gather | solution.py:810
  23.4 8.6 %copy-start.35 = (bf16[512,768]{1,0:T(8,128)(2,1)S(1)}, bf16[512,768]{1,0:T(8,128)(2,1)}, u32[]{:S(2)}) copy-start(bf16[512,768]{1,0:T(8,128)(2,1)} %param.13) | copy-start | bytes 2359300
  23.4 48.8 %all-to-all-start = ((bf16[8,144,768]{2,1,0:T(8,128)(2,1)}), bf16[8,144,768]{2,1,0:T(8,128)(2,1)}, u32[]{:S(2)}, u32[]{:S(2)}) async-start(bf16[8,144,768]{2,1,0:T(8,128)(2,1)} %bitcast.219), calls=%async_computation | async-start | bytes 3538944 | tf_op jit(solution)/shard_map/all_to_all | solution.py:736
  30.8 172.2 %all-gather.13.cloned.1.call-start = ((), (), s32[]{:S(2)}) async-start(), calls=%async_computation.16 | async-start | bytes 1474560 | tf_op jit(solution)/shard_map/all_gather | solution.py:811
  31.4 344.2 %reduce-scatter.6.cloned.1.call-start = ((), (), s32[]{:S(2)}) async-start(), calls=%async_computation.9 | async-start | bytes 5898240 | tf_op jit(solution)/shard_map/reduce_scatter | solution.py:995
  69.3 5.2 copy-start.6
  74.5 4.2 copy-start.23
  102.8 76.2 %copy-start.45 = (bf16[768,2432]{1,0:T(8,128)(2,1)S(1)}, bf16[768,2432]{1,0:T(8,128)(2,1)}, u32[]{:S(2)}) copy-start(bf16[768,2432]{1,0:T(8,128)(2,1)} %all-gather.9.cloned.1.call-done) | copy-start | bytes 11206660
  179.3 4.1 copy-start.24
  205.7 4.2 copy-start.18
  311.1 179.9 %reduce-scatter.8.cloned.1.call-start = ((), (), s32[]{:S(2)}) async-start(), calls=%async_computation.10 | async-start | bytes 5898240 | tf_op jit(solution)/shard_map/reduce_scatter | solution.py:995
  322.4 53.2 %all-to-all-start.1 = ((bf16[8,144,768]{2,1,0:T(8,128)(2,1)}), bf16[8,144,768]{2,1,0:T(8,128)(2,1)}, u32[]{:S(2)}, u32[]{:S(2)}) async-start(bf16[8,144,768]{2,1,0:T(8,128)(2,1)} %get-tuple-element.68), calls=%async_computation.1 | async-start | bytes 3538944 | tf_op jit(solution)/shard_map/all_to_all | solution.py:736
  335.1 155.9 %reduce-scatter.10.cloned.1.call-start = ((), (), s32[]{:S(2)}) async-start(), calls=%async_computation.11 | async-start | bytes 6021120 | tf_op jit(solution)/shard_map/reduce_scatter | solution.py:1053
  338.0 3.2 copy-start.19
  344.1 2.7 copy-start.47
  344.1 3.9 copy-start.5
  378.1 2.6 copy-start.9
  394.7 239.4 %reduce-scatter.12.cloned.1.call-start = ((), (), s32[]{:S(2)}) async-start(), calls=%async_computation.13 | async-start | bytes 5898240 | tf_op jit(solution)/shard_map/reduce_scatter | solution.py:995
  403.3 76.7 %copy-start.56 = (bf16[8,144,768]{2,1,0:T(8,128)(2,1)S(1)}, bf16[8,144,768]{2,1,0:T(8,128)(2,1)}, u32[]{:S(2)}) copy-start(bf16[8,144,768]{2,1,0:T(8,128)(2,1)} %get-tuple-element.83) | copy-start | bytes 5308420
  490.9 154.9 %all-reduce.9.cloned.1.call-start = ((), (), s32[]{:S(2)}) async-start(), calls=%async_computation.12 | async-start | bytes 2408448 | tf_op jit(solution)/shard_map/psum | solution.py:991
  491.6 204.0 %reduce-scatter.14.cloned.1.call-start = ((), (), s32[]{:S(2)}) async-start(), calls=%async_computation.14 | async-start | bytes 5898240 | tf_op jit(solution)/shard_map/reduce_scatter | solution.py:995
  502.5 4.2 copy-start.20
  508.7 3.2 copy-start.25
  517.3 17.4 %copy-start.44 = (bf16[768,2432]{1,0:T(8,128)(2,1)S(1)}, bf16[768,2432]{1,0:T(8,128)(2,1)}, u32[]{:S(2)}) copy-start(bf16[768,2432]{1,0:T(8,128)(2,1)} %all-gather.7.cloned.1.call-done) | copy-start | bytes 11206660
  537.0 2.9 copy-start.17
  544.4 88.1 %copy-start.37 = (bf16[512,768]{1,0:T(8,128)(2,1)S(1)}, bf16[512,768]{1,0:T(8,128)(2,1)}, u32[]{:S(2)}) copy-start(bf16[512,768]{1,0:T(8,128)(2,1)} %param.13) | copy-start | bytes 2359300
  544.4 88.1 %copy-start.42 = (f32[512,768]{1,0:T(8,128)S(1)}, f32[512,768]{1,0:T(8,128)}, u32[]{:S(2)}) copy-start(f32[512,768]{1,0:T(8,128)} %get-tuple-element.238) | copy-start | bytes 4718596
  658.6 37.1 %copy-start.46 = (bf16[768,768]{1,0:T(8,128)(2,1)S(1)}, bf16[768,768]{1,0:T(8,128)(2,1)}, u32[]{:S(2)}) copy-start(bf16[768,768]{1,0:T(8,128)(2,1)} %reduce-scatter.6.cloned.1.call-done) | copy-start | bytes 3538948
  (38 other events, 57.2 us)
Sparse Core Ops, SparseCore 0:
  13.0 34.5 all-gather.6
  49.7 17.4 all-gather.10
  69.3 31.8 all-gather.8
  103.2 17.4 all-gather.12
  311.2 55.0 reduce-scatter.5
  369.3 47.9 reduce-scatter.7
  419.8 48.5 reduce-scatter.9
  491.0 54.3 reduce-scatter.11
  549.0 96.7 all-reduce.8
  648.7 46.8 reduce-scatter.13

commit v5 on v4

--- a/solution.py
+++ b/solution.py
@@ -257,46 +257,32 @@
     )
 
 
-def reduce_mixer(
-    owners,
-    chunks,
-    q_ref,
-    k_ref,
-    v_ref,
-    p_ref,
-    small_ref,
-    out_ref,
-    core_in,
-    side_out,
-    side_in,
-    keep,
-    owner_in,
-    small_in,
-    part,
-    whole_in,
-    core_send,
-    core_recv,
-    side_send,
-    side_recv,
-    owner_send,
-    owner_recv,
-    small_send,
-    small_recv,
-    whole_send,
-    whole_recv,
-):
+def reduce_mixer(chunks, *refs):
+    q_ref, k_ref, v_ref, p_ref, small_ref, above, out_ref, narrow_ref = refs[:8]
+    core_in, side_out, side_in, keep, cross_in, half, line_in, whole, other_half, small_in = refs[
+        8:18
+    ]
+    core_send, core_recv, side_send, side_recv = refs[18:22]
+    x1_send, x1_recv, z1_send, z1_recv, z2_send, z2_recv, x2_send, x2_recv = refs[22:30]
+    small_send, small_recv = refs[30:32]
+    owners = small_in.shape[1]
     me = lax.axis_index("dp")
     place = lax.axis_index("fsdp")
     core, side = lax.rem(place, 2), place // 2
     partner = 2 * side + (1 - core)
     across = 2 * (1 - side) + core
-    refs = (q_ref, k_ref, v_ref, p_ref, small_ref)
+    x, z = lax.rem(me, 2), me // 2
+    x_peer = me + 1 - 2 * x
+    depth = owners // 2
+    inputs = (q_ref, k_ref, v_ref, p_ref, small_ref)
     rows = q_ref.shape[1]
     spare = small_ref.shape[1]
     main = 4 * rows
-    block = main // owners
+    quarter = main // 2
+    block = quarter // depth
     columns = q_ref.shape[2] // chunks
-    spans = [(index * rows, ref.shape[1]) for index, ref in enumerate(refs)]
+    spans = [(index * rows, ref.shape[1]) for index, ref in enumerate(inputs)]
+    sources = (keep, above)
 
     barrier = pltpu.get_barrier_semaphore()
     for other in (partner, across):
@@ -312,35 +298,53 @@
         )
     pl.semaphore_wait(barrier, owners + 1)
 
-    waits = []
-    core_copies = [[] for _ in range(chunks)]
-    for chunk in range(chunks):
-        lanes = pl.ds(chunk * columns, columns)
+    def lanes_of(chunk):
+        return pl.ds(chunk * columns, columns)
+
+    def half_at(index):
+        return pl.ds(pl.multiple_of(index * quarter, quarter), quarter)
+
+    def block_at(index):
+        return pl.ds(pl.multiple_of(index * block, block), block)
+
+    live = {}
+
+    def start(key, copies):
+        for copy in copies:
+            copy.start()
+        live[key] = copies
+
+    def finish(key):
+        for copy in live.pop(key):
+            copy.wait()
+
+    def start_core(chunk):
+        lanes = lanes_of(chunk)
+        copies = []
         for turn in range(2):
             there = 1 - side if turn == 0 else side
-            for index, (start, count) in enumerate(spans):
-                copy = mesh_copy(
-                    refs[index].at[2 * there + 1 - core, :, lanes],
-                    core_in.at[turn, pl.ds(start, count), lanes],
-                    core_send,
-                    core_recv,
-                    (chunk * 2 + turn) * 5 + index,
-                    {"fsdp": partner},
+            for index, (first, count) in enumerate(spans):
+                copies.append(
+                    mesh_copy(
+                        inputs[index].at[2 * there + 1 - core, :, lanes],
+                        core_in.at[turn, pl.ds(first, count), lanes],
+                        core_send,
+                        core_recv,
+                        (chunk * 2 + turn) * 5 + index,
+                        {"fsdp": partner},
+                    )
                 )
-                copy.start()
-                core_copies[chunk].append(copy)
-
-    side_copies = []
-    for chunk in range(chunks):
-        lanes = pl.ds(chunk * columns, columns)
-        for copy in core_copies[chunk]:
-            copy.wait()
+        start(("core", chunk), copies)
+
+    def add_core(chunk):
+        lanes = lanes_of(chunk)
+        finish(("core", chunk))
         for turn in range(2):
             there = 1 - side if turn == 0 else side
             target = side_out if turn == 0 else keep
-            for index, (start, count) in enumerate(spans):
-                at = pl.ds(start, count)
-                total = refs[index][2 * there + core, :, lanes].astype(jnp.float32)
+            for index, (first, count) in enumerate(spans):
+                at = pl.ds(first, count)
+                total = inputs[index][2 * there + core, :, lanes].astype(jnp.float32)
                 total = total + core_in[turn, at, lanes].astype(jnp.float32)
                 target[at, lanes] = low(total)
             if turn == 0:
@@ -352,117 +356,190 @@
                     chunk,
                     {"fsdp": across},
                 )
-                copy.start()
-                side_copies.append(copy)
-
-    owner_copies = []
-    for chunk in range(chunks):
-        lanes = pl.ds(chunk * columns, columns)
-        side_copies[chunk].wait()
-        keep[:, lanes] = low(
-            keep[:, lanes].astype(jnp.float32) + side_in[:, lanes].astype(jnp.float32)
+                start(("side", chunk), [copy])
+
+    def start_cross(layer, chunk):
+        lanes = lanes_of(chunk)
+        unit = layer * chunks + chunk
+        if layer == 0:
+            finish(("side", chunk))
+            keep[:, lanes] = low(
+                keep[:, lanes].astype(jnp.float32) + side_in[:, lanes].astype(jnp.float32)
+            )
+        source = sources[layer]
+        copies = [
+            mesh_copy(
+                source.at[half_at(1 - x), lanes],
+                cross_in.at[layer, :, lanes],
+                x1_send,
+                x1_recv,
+                unit,
+                {"dp": x_peer},
+            )
+        ]
+        start(("x1", unit), copies)
+        copies = [
+            mesh_copy(
+                source.at[pl.ds(main, spare), lanes],
+                small_in.at[layer, me, :, lanes],
+                small_send,
+                small_recv,
+                unit * owners + step,
+                {"dp": lax.rem(me + step, owners)},
+            )
+            for step in range(1, owners)
+        ]
+        start(("small", unit), copies)
+
+    def add_cross(layer, chunk):
+        lanes = lanes_of(chunk)
+        unit = layer * chunks + chunk
+        finish(("x1", unit))
+        half[layer, :, lanes] = low(
+            sources[layer][half_at(x), lanes].astype(jnp.float32)
+            + cross_in[layer, :, lanes].astype(jnp.float32)
         )
         copies = []
-        for step in range(1, owners):
-            other = lax.rem(me + step, owners)
-            where = chunk * owners + step
-            at = pl.ds(pl.multiple_of(other * block, block), block)
+        for step in range(1, depth):
+            there = lax.rem(z + step, depth)
             copies.append(
                 mesh_copy(
-                    keep.at[at, lanes],
-                    owner_in.at[step, :, lanes],
-                    owner_send,
-                    owner_recv,
-                    where,
-                    {"dp": other},
+                    half.at[layer, block_at(there), lanes],
+                    line_in.at[layer, step, :, lanes],
+                    z1_send,
+                    z1_recv,
+                    unit * depth + step,
+                    {"dp": 2 * there + x},
                 )
             )
+        start(("z1", unit), copies)
+
+    def add_line(layer, chunk):
+        lanes = lanes_of(chunk)
+        unit = layer * chunks + chunk
+        finish(("z1", unit))
+        total = half[layer, block_at(z), lanes].astype(jnp.float32)
+        for step in range(1, depth):
+            total = total + line_in[layer, step, :, lanes].astype(jnp.float32)
+        whole[layer, block_at(z), lanes] = low(total)
+        copies = []
+        for step in range(1, depth):
+            there = lax.rem(z + step, depth)
             copies.append(
                 mesh_copy(
-                    keep.at[pl.ds(main, spare), lanes],
-                    small_in.at[me, :, lanes],
-                    small_send,
-                    small_recv,
-                    where,
-                    {"dp": other},
+                    whole.at[layer, block_at(z), lanes],
+                    whole.at[layer, block_at(z), lanes],
+                    z2_send,
+                    z2_recv,
+                    unit * depth + step,
+                    {"dp": 2 * there + x},
                 )
             )
-            copies[-2].start()
-            copies[-1].start()
-        owner_copies.append(copies)
-
-    mine = pl.ds(pl.multiple_of(me * block, block), block)
-    whole_copies = []
+        start(("z2", unit), copies)
+
+    def return_cross(layer, chunk):
+        lanes = lanes_of(chunk)
+        unit = layer * chunks + chunk
+        finish(("z2", unit))
+        copy = mesh_copy(
+            whole.at[layer, :, lanes],
+            other_half.at[layer, :, lanes],
+            x2_send,
+            x2_recv,
+            unit,
+            {"dp": x_peer},
+        )
+        start(("x2", unit), [copy])
+
+    def write(layer, chunk):
+        lanes = lanes_of(chunk)
+        unit = layer * chunks + chunk
+        finish(("x2", unit))
+        for index in range(2):
+            at = pl.ds(index * rows, rows)
+            out_ref[2 * x + index, layer, :, lanes] = whole[layer, at, lanes].astype(jnp.float32)
+            out_ref[2 * (1 - x) + index, layer, :, lanes] = other_half[layer, at, lanes].astype(
+                jnp.float32
+            )
+        finish(("small", unit))
+        small_in[layer, me, :, lanes] = sources[layer][pl.ds(main, spare), lanes]
+        narrow = small_in[layer, 0, :, lanes].astype(jnp.float32)
+        for other in range(1, owners):
+            narrow = narrow + small_in[layer, other, :, lanes].astype(jnp.float32)
+        narrow_ref[layer, :, lanes] = narrow
+
     for chunk in range(chunks):
-        lanes = pl.ds(chunk * columns, columns)
-        for copy in owner_copies[chunk]:
-            copy.wait()
-        total = keep[mine, lanes].astype(jnp.float32)
-        for step in range(1, owners):
-            total = total + owner_in[step, :, lanes].astype(jnp.float32)
-        part[:, lanes] = low(total)
-        out_ref[mine, lanes] = low(total).astype(jnp.float32)
-        copies = []
-        for step in range(1, owners):
-            copy = mesh_copy(
-                part.at[:, lanes],
-                whole_in.at[me, :, lanes],
-                whole_send,
-                whole_recv,
-                chunk * owners + step,
-                {"dp": lax.rem(me + step, owners)},
-            )
-            copy.start()
-            copies.append(copy)
-        whole_copies.append(copies)
-        small_in[me, :, lanes] = keep[pl.ds(main, spare), lanes]
-        narrow = small_in[0, :, lanes].astype(jnp.float32)
-        for other in range(1, owners):
-            narrow = narrow + small_in[other, :, lanes].astype(jnp.float32)
-        out_ref[pl.ds(main, spare), lanes] = narrow
-
+        start_core(chunk)
     for chunk in range(chunks):
-        lanes = pl.ds(chunk * columns, columns)
-        for copy in whole_copies[chunk]:
-            copy.wait()
-        for step in range(1, owners):
-            other = lax.rem(me + step, owners)
-            at = pl.ds(pl.multiple_of(other * block, block), block)
-            out_ref[at, lanes] = whole_in[other, :, lanes].astype(jnp.float32)
-
-
-def reduce_in_kernel(changes, small, owners):
+        start_cross(1, chunk)
+    for chunk in range(chunks):
+        add_core(chunk)
+        add_cross(1, chunk)
+    for chunk in range(chunks):
+        add_line(1, chunk)
+    start_cross(0, 0)
+    return_cross(1, 0)
+    add_cross(0, 0)
+    return_cross(1, 1)
+    start_cross(0, 1)
+    return_cross(1, 2)
+    add_line(0, 0)
+    add_cross(0, 1)
+    for chunk in range(chunks):
+        write(1, chunk)
+    start_cross(0, 2)
+    add_line(0, 1)
+    add_cross(0, 2)
+    return_cross(0, 0)
+    return_cross(0, 1)
+    add_line(0, 2)
+    write(0, 0)
+    return_cross(0, 2)
+    write(0, 1)
+    write(0, 2)
+
+
+def reduce_in_kernel(changes, small, above, owners):
     shards, rows, width = changes[0].shape
     spare = small.shape[1]
     main = 4 * rows
     total = main + spare
     block = main // owners
     chunks = 3
+    units = 2 * chunks
     low_type = jnp.bfloat16
     space = pl.BlockSpec(memory_space=pltpu.VMEM)
     return pl.pallas_call(
-        functools.partial(reduce_mixer, owners, chunks),
-        out_shape=jax.ShapeDtypeStruct((total, width), jnp.float32),
-        in_specs=[space] * 5,
-        out_specs=space,
+        functools.partial(reduce_mixer, chunks),
+        out_shape=(
+            jax.ShapeDtypeStruct((4, 2, rows, width), jnp.float32),
+            jax.ShapeDtypeStruct((2, spare, width), jnp.float32),
+        ),
+        in_specs=[space] * 6,
+        out_specs=(space, space),
         scratch_shapes=[
             pltpu.VMEM((2, total, width), low_type),
             pltpu.VMEM((total, width), low_type),
             pltpu.VMEM((total, width), low_type),
             pltpu.VMEM((total, width), low_type),
-            pltpu.VMEM((owners, block, width), low_type),
-            pltpu.VMEM((owners, spare, width), low_type),
-            pltpu.VMEM((block, width), low_type),
-            pltpu.VMEM((owners, block, width), low_type),
+            pltpu.VMEM((2, main // 2, width), low_type),
+            pltpu.VMEM((2, main // 2, width), low_type),
+            pltpu.VMEM((2, owners // 2, block, width), low_type),
+            pltpu.VMEM((2, main // 2, width), low_type),
+            pltpu.VMEM((2, main // 2, width), low_type),
+            pltpu.VMEM((2, owners, spare, width), low_type),
         ]
         + [pltpu.SemaphoreType.DMA((10 * chunks,))] * 2
         + [pltpu.SemaphoreType.DMA((chunks,))] * 2
-        + [pltpu.SemaphoreType.DMA((chunks * owners,))] * 6,
+        + [pltpu.SemaphoreType.DMA((units,))] * 2
+        + [pltpu.SemaphoreType.DMA((units * owners // 2,))] * 4
+        + [pltpu.SemaphoreType.DMA((units,))] * 2
+        + [pltpu.SemaphoreType.DMA((units * owners,))] * 2,
         compiler_params=pltpu.CompilerParams(
-            collective_id=1, has_side_effects=True, vmem_limit_bytes=40 << 20
+            collective_id=1, has_side_effects=True, vmem_limit_bytes=48 << 20
         ),
         name="reduce_mixer",
-    )(*changes, small)
+    )(*changes, small, above)
 
 
 def partner_of(me, index):
@@ -795,11 +872,11 @@
     experts = owners * EXP_DEV
     heads = position_bias.shape[1] * shards
     capacity = max(2, 9 * length * TOP // (8 * experts))
-    fused = shards == 4 and owners == 8 and capacity % 16 == 0
+    fused = shards == 4 and owners == 8 and capacity % 16 == 0 and layers == 2
     taken, pick, both, chosen = plan_routes(routes, experts, capacity)
     offsets = offset_selector(length)
 
-    mixers = []
+    gathered = []
     for layer in range(layers):
         small = pack_small(
             router_weight[layer], attention_gain[layer], expert_gain[layer], position_bias[layer]
@@ -809,29 +886,29 @@
         )
         first = lax.all_gather(first, "fsdp", axis=0, tiled=True)
         second = lax.all_gather(projection[layer], "fsdp", axis=0, tiled=True)
+        gathered.append((first, second))
+
+    early = exchange_rows(low(dot(both, cotangent)), experts)
+
+    hidden = tokens.astype(jnp.float32)
+    mixers = []
+    saved = []
+    for layer in range(layers):
+        first, projection_full = gathered[layer]
+        if layer:
+            hidden, first, projection_full = lax.optimization_barrier(
+                (hidden, first, projection_full)
+            )
         router, gain_attention, gain_expert, bias = unpack_small(
             first[:, 3 * width :], experts, shards, heads
         )
+        gain_attention = gain_attention.astype(jnp.float32)
+        gain_expert = gain_expert.astype(jnp.float32)
         table = lax.dot_general(
             bias.astype(jnp.float32), offsets, contract_last, precision=highest
         )
-        mixers.append(
-            (
-                first[:, : 3 * width],
-                second,
-                router,
-                gain_attention.astype(jnp.float32),
-                gain_expert.astype(jnp.float32),
-                table,
-            )
-        )
-
-    early = exchange_rows(low(dot(both, cotangent)), experts)
-
-    hidden = tokens.astype(jnp.float32)
-    saved = []
-    for layer in range(layers):
-        joined_weight, projection_full, router, gain_attention, gain_expert, table = mixers[layer]
+        joined_weight = first[:, : 3 * width]
+        mixers.append((joined_weight, projection_full, router, gain_attention, gain_expert, table))
         up_matrix, down_matrix = expert_up[layer, 0], expert_down[layer, 0]
         scale = row_scale(hidden)
         normed = low(hidden * scale * gain_attention)
@@ -988,7 +1065,8 @@
                 )
                 back_rows = exchange_rows(back_rows, experts)
             expert_results[layer + 1] = (up_above, down_above)
-            mixer_results[layer + 1] = lax.psum(above, "dp")
+            if not fused:
+                mixer_results[layer + 1] = lax.psum(above, "dp")
         down_change = low(dot_first(activity, back_sent))
         up_change = low(dot_first(received, back_inner))
         expert_results[layer] = tuple(
@@ -1046,30 +1124,29 @@
         )
         small = low(jnp.pad(small, ((0, 0), (0, -small.shape[1] % (16 * width)))))
         small = small.reshape(shards, -1, width)
-        if layer == 0 and shards == 4 and owners == 8:
-            mixer_results[layer] = reduce_in_kernel(changes, small, owners)
+        if layer == 0 and fused:
+            summed, narrow = reduce_in_kernel(changes, small, above, owners)
         else:
             packed = jnp.concatenate(changes + [small], axis=1)
             above = lax.psum_scatter(packed, "fsdp", scatter_dimension=0)
             if layer == 0:
                 mixer_results[layer] = lax.psum(above, "dp")
 
-    mixer_results = lax.optimization_barrier(mixer_results)
-    mixer_results = [result.astype(jnp.float32) for result in mixer_results]
     rows = width // shards
     counts = (rows * experts, rows, rows, heads // shards * NB)
-    smalls = []
-    for result in mixer_results:
-        flat = result[4 * rows :].reshape(-1)
-        ends = [sum(counts[: index + 1]) for index in range(4)]
-        smalls.append([flat[end - count : end] for end, count in zip(ends, counts)])
-    small_gradients = [jnp.stack([small[index] for small in smalls]) for index in range(4)]
+    if fused:
+        mixer_gradients = [summed[index] for index in range(4)]
+        flat = narrow.reshape(layers, -1)
+    else:
+        mixer_results = jnp.stack(lax.optimization_barrier(mixer_results)).astype(jnp.float32)
+        mixer_gradients = [
+            mixer_results[:, index * rows : (index + 1) * rows] for index in range(4)
+        ]
+        flat = mixer_results[:, 4 * rows :].reshape(layers, -1)
+    ends = [sum(counts[: index + 1]) for index in range(4)]
+    small_gradients = [flat[:, end - count : end] for end, count in zip(ends, counts)]
     router_gradient = small_gradients[0].reshape(layers, rows, experts)
     bias_gradient = small_gradients[3].reshape(position_bias.shape)
-    mixer_gradients = [
-        jnp.stack([result[index * rows : (index + 1) * rows] for result in mixer_results])
-        for index in range(4)
-    ]
     up_stack, down_stack = (
         jnp.stack([results[index].astype(jnp.float32) for results in expert_results])[:, None]
         for index in range(2)

time: 712 us -> 638 us (0.90)
  waiting for transfers between devices: 72.1 us -> 10.1 us
    reduce_scatter x4, waiting for transfers between devices: 36 us -> 0.02 us  [per_device(): lax.psum_scatter(change, 'fsdp', scatter_dimension=0, tiled=True)]
    all_gather x2, waiting for transfers between devices: 21.1 us -> 2.47 us  [per_device(): first = lax.all_gather(first, 'fsdp', axis=0, tiled=True)]
    psum x1 -> x0, waiting for transfers between devices: 7.59 us -> none  [per_device(): mixer_results[layer + 1] = lax.psum(above, 'dp')]
    unnamed x127 -> x139, local copies, waits for them, and re-layouts: 27.9 us -> 25.5 us
  transfers between devices with their start and end apart: 12 -> 11, of which waited for: 5 -> 3; matrix products, arithmetic and copies ran while one was open for 22% -> 24% of each run, Pallas kernels for 43% -> 45%
where the time goes in v5:
time: 638 us; the launch traced here: 633 us
  Pallas kernels  382 us (60%)
  matrix products  118 us (18%)
  local copies, waits for them, and re-layouts  53.7 us (8%)
  other arithmetic  33.6 us (5%)
  starting transfers between devices  20.3 us (3%)
  between operations  15.2 us (2%)
  waiting for transfers between devices  10.1 us (2%)
    pallas_call x3, Pallas kernels, experts_in_kernel(): pl.pallas_call(functools.partial(run_experts, mode, 512), out_shape=tuple...  238 us
    pallas_call x1, Pallas kernels, reduce_in_kernel(): pl.pallas_call(functools.partial(reduce_mixer, chunks), out_shape=(jax.Sh...  84.4 us
    dot_general x18, matrix products, dot_first(): lax.dot_general(left, right, contract_first, preferred_element_type=jnp.f...  71.3 us
    pallas_call x2, Pallas kernels, attention_backward(): pl.pallas_call(functools.partial(attend_back, pair, size ** (-0.5)), grid...  34.5 us
    dot_general x10, matrix products, dot(): return jnp.dot(left, right, preferred_element_type=jnp.float32)  27.4 us
    unnamed x139, local copies, waits for them, and re-layouts  25.5 us
    pallas_call x2, Pallas kernels, attention_forward(): pl.pallas_call(functools.partial(attend, pair, size ** (-0.5)), grid=(gro...  25 us
    all_to_all x2, starting transfers between devices, exchange(): return lax.all_to_all(values, 'dp', split_axis=0, concat_axis=0, tiled=True)  18.7 us
  transfers between devices with their start and end apart: 11, of which 3 were waited for; matrix products, arithmetic and copies ran while one was open for 24% of the time, Pallas kernels for 45%

profile of v5, /device:TPU:0, one launch (start us, length us, event | category | flops | bytes accessed | tf_op | source)
XLA Modules:
  0.0 632.8 jit_solution(7127985178708394933)
XLA Ops:
  22.9 7.3 %all-to-all-start = ((bf16[8,144,768]{2,1,0:T(8,128)(2,1)}), bf16[8,144,768]{2,1,0:T(8,128)(2,1)}, u32[]{:S(2)}, u32[]{:S(2)}) async-start(bf16[8,144,768]{2,1,0:T(8,128)(2,1)} %bitcast.9), calls=%async_computation | async-start | bytes 3538944 | tf_op jit(solution)/shard_map/all_to_all | solution.py:813
  32.3 8.6 %slice_bitcast_fusion.1 = (bf16[768,3072]{1,0:T(8,128)(2,1)}, bf16[768,3072]{1,0:T(8,128)(2,1)}) fusion(bf16[2,1,768,3072]{3,2,1,0:T(8,128)(2,1)} %param.22), kind=kLoop, calls=%fused_computation.7 | loop fusion | bytes 18874368 | tf_op jit(solution)/shard_map/squeeze | solution.py:912
  40.9 4.2 slice_bitcast_fusion
  50.5 4.3 convolution_convert_fusion.5.q_ref.k_ref.v_ref
  54.8 12.5 %attend.2 = (bf16[512,768]{1,0:T(8,128)(2,1)S(1)}, f32[512,768]{1,0:T(8,128)S(1)}) custom-call(bf16[512,2304]{1,0:T(8,128)(2,1)S(1)} %convolution_convert_fusion.5.q_ref.k_ref.v_ref, bf16[512,2304]{1,0:T(8,128)(2,1)S(1)} %convolution_convert_fusion.5.q_ref.k_ref.v_ref, bf16[512,2304]{1,0:T(8,128)(2,1)S(1)} %convolution_convert_fusion.5.q_ref.k_ref.v_ref, ...), custom_call_target="tpu_custom_call" | custom-call | flops 805306368 | bytes 4718592 | tf_op jit(solution)/shard_map/attend/pallas_call | solution.py:195
  68.5 3.1 all-to-all-done
  75.7 3.6 convolution_convert_fusion.7
  79.4 75.0 %experts_forward.1 = (bf16[8,144,768]{2,1,0:T(8,128)(2,1)}, bf16[8,144,768]{2,1,0:T(8,128)(2,1)}, bf16[4,288,3072]{2,1,0:T(8,128)(2,1)}, bf16[4,288,3072]{2,1,0:T(8,128)(2,1)}) custom-call(bf16[8,144,768]{2,1,0:T(8,128)(2,1)} %bitcast.210, bf16[768,3072]{1,0:T(8,128)(2,1)} %get-tuple-element.182.refs_1_, bf16[3072,768]{1,0:T(8,128)(2,1)} %get-tuple-element.180.refs_2_), custom_call_target="tpu_custom_call" | custom-call | tf_op jit(solution)/shard_map/experts_forward/pallas_call | solution.py:771
  154.4 4.0 fusion.14
  166.5 5.5 convolution_convert_fusion.4.q_ref.k_ref.v_ref
  174.0 12.5 %attend.3 = (bf16[512,768]{1,0:T(8,128)(2,1)S(1)}, f32[512,768]{1,0:T(8,128)S(1)}) custom-call(bf16[512,2304]{1,0:T(8,128)(2,1)S(1)} %copy-done, bf16[512,2304]{1,0:T(8,128)(2,1)S(1)} %copy-done, bf16[512,2304]{1,0:T(8,128)(2,1)S(1)} %copy-done, f32[6,2,1024]{2,1,0:T(2,128)S(1)} %copy.115.table_ref), custom_call_target="tpu_custom_call" | custom-call | flops 805306368 | bytes 4718592 | tf_op jit(solution)/shard_map/attend/pallas_call | solution.py:195
  194.4 86.4 %experts_both.1 = (bf16[8,144,768]{2,1,0:T(8,128)(2,1)}, bf16[8,144,768]{2,1,0:T(8,128)(2,1)}, bf16[4,288,3072]{2,1,0:T(8,128)(2,1)}, bf16[4,288,3072]{2,1,0:T(8...) custom-call(bf16[8,144,768]{2,1,0:T(8,128)(2,1)} %bitcast.209, ...), custom_call_target="tpu_custom_call" | custom-call | tf_op jit(solution)/shard_map/experts_both/pallas_call | solution.py:771
  280.9 10.6 %convolution_convert_fusion.3 = bf16[3072,768]{1,0:T(8,128)(2,1)} fusion(bf16[1152,3072]{1,0:T(8,128)(2,1)} %bitcast.245, bf16[1152,768]{1,0:T(8,128)(2,1)} %bitcast.250), kind=kOutput, calls=%fused_computation.3 | convolution fusion | flops 5438177280 | bytes 13565952 | tf_op jit(solution)/shard_map/dot_general | solution.py:35
  291.5 10.5 %convolution_convert_fusion.2 = bf16[768,3072]{1,0:T(8,128)(2,1)} fusion(bf16[1152,768]{1,0:T(8,128)(2,1)} %bitcast.249, bf16[1152,3072]{1,0:T(8,128)(2,1)} %bitcast.244), kind=kOutput, calls=%fused_computation.2 | convolution fusion | flops 5438177280 | bytes 13565952 | tf_op jit(solution)/shard_map/dot_general | solution.py:35
  302.8 11.4 %all-to-all-start.1 = ((bf16[8,144,768]{2,1,0:T(8,128)(2,1)}), bf16[8,144,768]{2,1,0:T(8,128)(2,1)}, u32[]{:S(2)}, u32[]{:S(2)}) async-start(bf16[8,144,768]{2,1,0:T(8,128)(2,1)} %get-tuple-element.74), calls=%async_computation.1 | async-start | bytes 3538944 | tf_op jit(solution)/shard_map/all_to_all | solution.py:813
  317.1 3.6 fusion.106
  328.6 17.1 %attend_back.2 = (bf16[512,768]{1,0:T(8,128)(2,1)S(1)}, bf16[512,768]{1,0:T(8,128)(2,1)S(1)}, bf16[512,768]{1,0:T(8,128)(2,1)S(1)}, f32[6,2,1024]{2,1,0:T(2,128)S(1)}) custom-call(bf16[512,2304]{1,0:T(8,128)(2,1)S(1)} %copy-done.1, bf16[512,2304]{1,0:T(8,128)(2,1)S(1)} %copy-done.1, bf16[512,2304]{1,0:T(8,128)(2,1)S(1)} %copy-done.1, ...), custom_call_target="tpu_custom_call" | custom-call | flops 2013265920 | bytes 7864320 | tf_op jit(solution)/shard_map/attend_back/pallas_call | solution.py:219
  348.7 3.2 convolution_convert_fusion.13
  352.0 3.7 all-to-all-done.1
  360.6 3.6 multiply_reduce_fusion.3
  374.9 3.8 fusion.18
  379.8 3.4 fusion.6
  383.3 76.7 %experts_backward.1 = (bf16[8,144,768]{2,1,0:T(8,128)(2,1)}, bf16[8,144,768]{2,1,0:T(8,128)(2,1)}, bf16[4,288,3072]{2,1,0:T(8,128)(2,1)}) custom-call(bf16[8,144,768]{2,1,0:T(8,128)(2,1)} %bitcast.206, bf16[768,3072]{1,0:T(8,128)(2,1)} %get-tuple-element.182.refs_1_, bf16[3072,768]{1,0:T(8,128)(2,1)} %get-tuple-element.180.refs_2_, ...), custom_call_target="tpu_custom_call" | custom-call | tf_op jit(solution)/shard_map/experts_backward/pallas_call | solution.py:771
  460.0 10.9 %convolution_convert_fusion = bf16[768,3072]{1,0:T(8,128)(2,1)} fusion(bf16[1152,768]{1,0:T(8,128)(2,1)S(1)} %bitcast.247, bf16[1152,3072]{1,0:T(8,128)(2,1)} %bitcast.246), kind=kOutput, calls=%fused_computation | convolution fusion | flops 5438177280 | bytes 13565952 | tf_op jit(solution)/shard_map/dot_general | solution.py:35
  471.3 10.6 %convolution_convert_fusion.1 = bf16[3072,768]{1,0:T(8,128)(2,1)} fusion(bf16[1152,3072]{1,0:T(8,128)(2,1)} %bitcast.243, bf16[1152,768]{1,0:T(8,128)(2,1)} %bitcast.248), kind=kOutput, calls=%fused_computation.1 | convolution fusion | flops 5438177280 | bytes 13565952 | tf_op jit(solution)/shard_map/dot_general | solution.py:35
  481.9 4.6 fusion.15
  488.5 3.2 fusion.107
  497.1 17.4 %attend_back.3 = (bf16[512,768]{1,0:T(8,128)(2,1)S(1)}, bf16[512,768]{1,0:T(8,128)(2,1)S(1)}, bf16[512,768]{1,0:T(8,128)(2,1)S(1)}, f32[6,2,1024]{2,1,0:T(2,128)S(1)}) custom-call(bf16[512,2304]{1,0:T(8,128)(2,1)S(1)} %convolution_convert_fusion.5.q_ref.k_ref.v_ref, bf16[512,2304]{1,0:T(8,128)(2,1)S(1)} %convolution_convert_fusion.5.q_ref.k_ref.v_ref, ...), custom_call_target="tpu_custom_call" | custom-call | flops 2013265920 | bytes 7864320 | tf_op jit(solution)/shard_map/attend_back/pallas_call | solution.py:219
  525.8 84.4 %reduce_mixer.1 = (f32[4,2,192,768]{3,2,1,0:T(8,128)}, f32[2,16,768]{2,1,0:T(8,128)S(1)}) custom-call(bf16[4,192,768]{2,1,0:T(8,128)(2,1)S(1)} %bitcast.198, bf16[4,192,768]{2,1,0:T(8,128)(2,1)S(1)} %bitcast.199, bf16[4,192,768]{2,1,0:T(8,128)(2,1)S(1)} %bitcast.200, bf16[4,192,768]{2,1,0:T(8,128)(2,1)S(1)} %bitcast.196, bf16[4,16,768]{2,1,0:T(8,128)(2,1)S(1)} %bitcast.201, ...), custom_call_target="tpu_custom_call" | custom-call | tf_op jit(solution)/shard_map/reduce_mixer/pallas_call | solution.py:512
  612.5 3.6 fusion.25
  618.4 3.9 fusion.7
  622.3 3.8 fusion.8
  (303 shorter events, 100.7 us)
Async XLA Ops:
  7.2 4.5 copy-start.54
  7.2 4.5 copy-start.55
  7.2 40.4 %all-gather.7.cloned.1.call-start = ((), (), s32[]{:S(2)}) async-start(), calls=%async_computation.7 | async-start | bytes 4669440 | tf_op jit(solution)/shard_map/all_gather | solution.py:887
  12.9 58.7 %all-gather.11.cloned.1.call-start = ((), (), s32[]{:S(2)}) async-start(), calls=%async_computation.14 | async-start | bytes 1474560 | tf_op jit(solution)/shard_map/all_gather | solution.py:888
  14.0 147.2 %all-gather.13.cloned.1.call-start = ((), (), s32[]{:S(2)}) async-start(), calls=%async_computation.15 | async-start | bytes 1474560 | tf_op jit(solution)/shard_map/all_gather | solution.py:888
  22.9 48.7 %all-to-all-start = ((bf16[8,144,768]{2,1,0:T(8,128)(2,1)}), bf16[8,144,768]{2,1,0:T(8,128)(2,1)}, u32[]{:S(2)}, u32[]{:S(2)}) async-start(bf16[8,144,768]{2,1,0:T(8,128)(2,1)} %bitcast.9), calls=%async_computation | async-start | bytes 3538944 | tf_op jit(solution)/shard_map/all_to_all | solution.py:813
  30.3 130.9 %all-gather.9.cloned.1.call-start = ((), (), s32[]{:S(2)}) async-start(), calls=%async_computation.8 | async-start | bytes 4669440 | tf_op jit(solution)/shard_map/all_gather | solution.py:887
  31.5 324.2 %reduce-scatter.6.cloned.1.call-start = ((), (), s32[]{:S(2)}) async-start(), calls=%async_computation.9 | async-start | bytes 5898240 | tf_op jit(solution)/shard_map/reduce_scatter | solution.py:1073
  32.0 8.9 %slice-start = ((s8[9437184]{0:T(1024)(128)(4,1)}), s8[4194304]{0:T(1024)(128)(4,1)S(1)}, s32[]{:S(2)}) async-start(s8[9437184]{0:T(1024)(128)(4,1)} %bitcast.203), calls=%async_computation.16 | async-start | bytes 8388608
  32.3 8.6 %slice-start.1 = ((s8[9437184]{0:T(1024)(128)(4,1)}), s8[4194304]{0:T(1024)(128)(4,1)S(1)}, s32[]{:S(2)}) async-start(s8[9437184]{0:T(1024)(128)(4,1)} %bitcast.203), calls=%async_computation.17 | async-start | bytes 8388608
  32.3 8.6 %slice-start.2 = ((s8[9437184]{0:T(1024)(128)(4,1)}), s8[1048576]{0:T(1024)(128)(4,1)S(1)}, s32[]{:S(2)}) async-start(s8[9437184]{0:T(1024)(128)(4,1)} %bitcast.203), calls=%async_computation.18 | async-start | bytes 2097152
  68.5 5.4 copy-start.7
  74.2 5.2 copy-start.39
  154.4 5.2 copy-start.26
  161.2 4.2 copy-start.19
  174.0 12.5 %copy-start.20 = (f32[512,768]{1,0:T(8,128)S(1)}, f32[512,768]{1,0:T(8,128)}, u32[]{:S(2)}) copy-start(f32[512,768]{1,0:T(8,128)} %fusion.17) | copy-start | bytes 4718596
  174.0 12.5 %copy-start.48 = (bf16[1,768,768]{2,1,0:T(8,128)(2,1)S(1)}, bf16[1,768,768]{2,1,0:T(8,128)(2,1)}, u32[]{:S(2)}) copy-start(bf16[1,768,768]{2,1,0:T(8,128)(2,1)} %all-gather.13.cloned.1.call-done) | copy-start | bytes 3538948
  187.7 4.2 copy-start.22
  291.5 179.8 %reduce-scatter.8.cloned.1.call-start = ((), (), s32[]{:S(2)}) async-start(), calls=%async_computation.10 | async-start | bytes 5898240 | tf_op jit(solution)/shard_map/reduce_scatter | solution.py:1073
  302.8 52.8 %all-to-all-start.1 = ((bf16[8,144,768]{2,1,0:T(8,128)(2,1)}), bf16[8,144,768]{2,1,0:T(8,128)(2,1)}, u32[]{:S(2)}, u32[]{:S(2)}) async-start(bf16[8,144,768]{2,1,0:T(8,128)(2,1)} %get-tuple-element.74), calls=%async_computation.1 | async-start | bytes 3538944 | tf_op jit(solution)/shard_map/all_to_all | solution.py:813
  314.2 157.1 %reduce-scatter.10.cloned.1.call-start = ((), (), s32[]{:S(2)}) async-start(), calls=%async_computation.11 | async-start | bytes 6021120 | tf_op jit(solution)/shard_map/reduce_scatter | solution.py:1131
  317.1 3.6 copy-start.23
  323.5 3.9 copy-start.5
  374.7 243.7 %reduce-scatter.12.cloned.1.call-start = ((), (), s32[]{:S(2)}) async-start(), calls=%async_computation.12 | async-start | bytes 5898240 | tf_op jit(solution)/shard_map/reduce_scatter | solution.py:1073
  383.3 76.7 %copy-start.58 = (bf16[8,144,768]{2,1,0:T(8,128)(2,1)S(1)}, bf16[8,144,768]{2,1,0:T(8,128)(2,1)}, u32[]{:S(2)}) copy-start(bf16[8,144,768]{2,1,0:T(8,128)(2,1)} %get-tuple-element.89) | copy-start | bytes 5308420
  471.0 151.3 %reduce-scatter.14.cloned.1.call-start = ((), (), s32[]{:S(2)}) async-start(), calls=%async_computation.13 | async-start | bytes 5898240 | tf_op jit(solution)/shard_map/reduce_scatter | solution.py:1073
  481.9 4.6 copy-start.24
  488.5 3.3 copy-start.27
  497.1 17.4 %copy-start.45 = (bf16[768,2432]{1,0:T(8,128)(2,1)S(1)}, bf16[768,2432]{1,0:T(8,128)(2,1)}, u32[]{:S(2)}) copy-start(bf16[768,2432]{1,0:T(8,128)(2,1)} %all-gather.7.cloned.1.call-done) | copy-start | bytes 11206660
  525.8 86.7 %copy-start.38 = (bf16[512,768]{1,0:T(8,128)(2,1)S(1)}, bf16[512,768]{1,0:T(8,128)(2,1)}, u32[]{:S(2)}) copy-start(bf16[512,768]{1,0:T(8,128)(2,1)} %param.13) | copy-start | bytes 2359300
  612.5 3.6 copy-start.44
  618.4 3.9 copy-start.46
  (42 other events, 68.3 us)
Sparse Core Ops, SparseCore 0:
  13.0 34.5 all-gather.6
  49.7 17.4 all-gather.10
  69.3 17.4 all-gather.12
  88.8 31.8 all-gather.8
  291.6 54.7 reduce-scatter.5
  349.3 47.9 reduce-scatter.7
  399.9 48.6 reduce-scatter.9
  471.1 54.1 reduce-scatter.11
  528.4 64.0 reduce-scatter.13

commit v6 on v5

--- a/solution.py
+++ b/solution.py
@@ -6,6 +6,7 @@
 from jax.experimental import pallas as pl
 from jax.experimental.pallas import tpu as pltpu
 from jax.sharding import PartitionSpec as P
+
 
 EXP_DEV = 1
 TOP = 2
@@ -500,7 +501,7 @@
 
 
 def reduce_in_kernel(changes, small, above, owners):
-    shards, rows, width = changes[0].shape
+    _, rows, width = changes[0].shape
     spare = small.shape[1]
     main = 4 * rows
     total = main + spare
@@ -576,21 +577,21 @@
     if mode == "forward":
         home, rows_in, activity_any, slope_any = take(4)
     elif mode == "backward":
-        (slope_any,) = take(1)
-        home, rows_in, inner_any = take(3)
+        slope_any, activity_any, rows_before = take(3)
+        home, rows_in, up_any_out, down_any_out = take(4)
     else:
         gates, early = take(2)
-        home, rows_in, activity_any, inner_any, scaled, result, places = take(7)
+        home, rows_in, result, places, up_any_out, down_any_out = take(6)
     up, down, ready = take(3)
     if mode == "forward":
         activity, slope = take(2)
         outs = [(activity, activity_any), (slope, slope_any)]
     elif mode == "backward":
-        slope, inner = take(2)
-        outs = [(inner, inner_any)]
+        slope, inner, activity, up_out, down_out = take(5)
+        outs = []
     else:
-        activity, inner, gates_in, place_out = take(4)
-        outs = [(activity, activity_any), (inner, inner_any)]
+        activity, inner, gates_in, place_out, scaled, up_out, down_out = take(7)
+        outs = []
     load, own, stores, go_send, go_recv, back_send, back_recv = take(7)
     if mode == "both":
         gate_send, gate_recv, place_send, place_recv = take(4)
@@ -630,6 +631,7 @@
     first.append(pltpu.make_async_copy(down_any, down, load.at[1]))
     if mode == "backward":
         first.append(pltpu.make_async_copy(slope_any, slope, load.at[2]))
+        first.append(pltpu.make_async_copy(activity_any, activity, load.at[3]))
     for copy in first:
         copy.start()
 
@@ -735,6 +737,43 @@
                 copy.start()
                 coming.append(copy)
 
+    if mode != "forward":
+        before = rows_before if mode == "backward" else rows_in
+        back = rows_in if mode == "backward" else scaled
+        part = hidden // 3
+
+        for third in range(3):
+
+            def change(step, carry):
+                start = pl.multiple_of(third * part + step * 256, 256)
+                columns = pl.ds(start, 256)
+                count = owners * capacity
+                down_out[columns, :] = low(
+                    dot_first(
+                        activity[:, :, columns].reshape(count, 256),
+                        back[...].reshape(count, width),
+                    )
+                )
+                up_out[:, columns] = low(
+                    dot_first(
+                        before[...].reshape(count, width),
+                        inner[:, :, columns].reshape(count, 256),
+                    )
+                )
+                return carry
+
+            lax.fori_loop(0, part // 256, change, 0)
+            some = pl.ds(third * part, part)
+            for at, (source, target) in enumerate(
+                (
+                    (down_out.at[some, :], down_any_out.at[some, :]),
+                    (up_out.at[:, some], up_any_out.at[:, some]),
+                )
+            ):
+                copy = pltpu.make_async_copy(source, target, stores.at[2 * third + at])
+                copy.start()
+                coming.append(copy)
+
     for index in range(1, owners):
         going[index].wait_send()
         if mode == "both":
@@ -757,17 +796,21 @@
     line = jax.ShapeDtypeStruct((owners, 1, lines), jnp.float32)
     line_scratch = pltpu.VMEM((owners, 1, lines), jnp.float32)
     many = pltpu.SemaphoreType.DMA((owners,))
+    changes = [
+        (jax.ShapeDtypeStruct(matrix.shape, low_type), far) for matrix in (up_matrix, down_matrix)
+    ]
+    change_scratch = [pltpu.VMEM(matrix.shape, low_type) for matrix in (up_matrix, down_matrix)]
+    rows_scratch = pltpu.VMEM((owners, capacity, width), low_type)
     if mode == "forward":
         ins, outs = [near, far, far], [(rows, near), (rows, near), (wide, far), (wide, far)]
         scratch = [wide_scratch] * 2
     elif mode == "backward":
-        ins, outs = [near, far, far, far], [(rows, near), (rows, near), (wide, far)]
-        scratch = [wide_scratch] * 2
+        ins, outs = [near, far, far, far, far, near], [(rows, near), (rows, near)] + changes
+        scratch = [wide_scratch] * 3 + change_scratch
     else:
         ins = [near, far, far, near, near]
-        outs = [(rows, near), (rows, near), (wide, far), (wide, far)]
-        outs += [(rows, near), (rows, near), (line, near)]
-        scratch = [wide_scratch] * 2 + [line_scratch] * 2
+        outs = [(rows, near), (rows, near), (rows, near), (line, near)] + changes
+        scratch = [wide_scratch] * 2 + [line_scratch] * 2 + [rows_scratch] + change_scratch
     return pl.pallas_call(
         functools.partial(run_experts, mode, 512),
         out_shape=tuple(shape for shape, _ in outs),
@@ -776,11 +819,11 @@
         scratch_shapes=[
             pltpu.VMEM(up_matrix.shape, low_type),
             pltpu.VMEM(down_matrix.shape, low_type),
-            pltpu.VMEM((owners, capacity, width), low_type),
+            rows_scratch,
         ]
         + scratch
         + [
-            pltpu.SemaphoreType.DMA((3,)),
+            pltpu.SemaphoreType.DMA((4,)),
             pltpu.SemaphoreType.DMA((4,)),
             pltpu.SemaphoreType.DMA((2 * pairs,)),
         ]
@@ -788,9 +831,13 @@
         compiler_params=pltpu.CompilerParams(
             collective_id={"forward": 2, "backward": 3, "both": 4}[mode],
             has_side_effects=True,
-            vmem_limit_bytes=56 << 20,
+            vmem_limit_bytes=60 << 20,
         ),
-        name="experts_" + mode,
+        cost_estimate=pl.CostEstimate(
+            flops=80 * owners * capacity * width * hidden // 2,
+            bytes_accessed=12 * width * hidden,
+            transcendentals=0,
+        ),
     )(sent, up_matrix, down_matrix, *extra)
 
 
@@ -930,13 +977,11 @@
                 "forward", sent.reshape(experts, capacity, width), up_matrix, down_matrix
             )
             returned = returned.reshape(-1, width)
-            received = received.reshape(-1, width)
-            activity = activity.reshape(received.shape[0], -1)
         elif fused:
             gate_places = jnp.sum(jnp.where(taken, gate_line[None, :], 0.0), axis=1)
             gate_places = gate_places.reshape(experts, 1, capacity)
             gate_places = jnp.pad(gate_places, ((0, 0), (0, 0), (0, -capacity % LANES)))
-            back_rows, received, activity, back_inner, back_sent, result, back_places = (
+            back_rows, received, result, back_places, up_change, down_change = (
                 experts_in_kernel(
                     "both",
                     sent.reshape(experts, capacity, width),
@@ -948,12 +993,11 @@
             count = experts * capacity
             last = (
                 back_places[:, 0, :capacity].reshape(-1),
-                back_sent.reshape(count, width),
-                back_inner.reshape(count, -1),
+                up_change,
+                down_change,
                 back_rows.reshape(count, width),
             )
-            received = received.reshape(count, width)
-            activity = activity.reshape(count, -1)
+            activity = None
             returned = exchange_rows(result.reshape(count, width), experts)
         else:
             received = exchange_rows(sent, experts)
@@ -1025,7 +1069,10 @@
             routed,
         ) = saved[layer]
         if layer == layers - 1:
-            back_places, back_sent, back_inner, back_rows = last
+            if fused:
+                back_places, up_change, down_change, back_rows = last
+            else:
+                back_places, back_sent, back_inner, back_rows = last
             back_gates = jnp.sum(jnp.where(taken, back_places[:, None], 0.0), axis=0)
             back_gates = back_gates.reshape(TOP, length).T
         else:
@@ -1042,19 +1089,17 @@
             back_sent = low(dot(pick, gated))
             up_above, down_above = expert_results[layer + 1]
             if fused:
-                back_rows, back_sent, back_inner = experts_in_kernel(
+                back_rows, _, up_change, down_change = experts_in_kernel(
                     "backward",
                     back_sent.reshape(experts, capacity, width),
                     up_matrix,
                     down_matrix,
-                    (slope,),
-                )
-                back_rows, back_sent, up_above, above = lax.optimization_barrier(
-                    (back_rows, back_sent, up_above, above)
+                    (slope, activity, received),
+                )
+                back_rows, up_above, above = lax.optimization_barrier(
+                    (back_rows, up_above, above)
                 )
                 back_rows = back_rows.reshape(-1, width)
-                back_sent = back_sent.reshape(-1, width)
-                back_inner = back_inner.reshape(back_sent.shape[0], -1)
             else:
                 back_sent = exchange_rows(back_sent, experts)
                 back_sent, up_above = lax.optimization_barrier((back_sent, up_above))
@@ -1067,15 +1112,19 @@
             expert_results[layer + 1] = (up_above, down_above)
             if not fused:
                 mixer_results[layer + 1] = lax.psum(above, "dp")
-        down_change = low(dot_first(activity, back_sent))
-        up_change = low(dot_first(received, back_inner))
-        expert_results[layer] = tuple(
-            lax.psum_scatter(change, "fsdp", scatter_dimension=0, tiled=True)
-            for change in (up_change, down_change)
-        )
-        back_rows, down_change, up_change = lax.optimization_barrier(
-            (back_rows, down_change, up_change)
-        )
+        if not fused:
+            down_change = low(dot_first(activity, back_sent))
+            up_change = low(dot_first(received, back_inner))
+        shards_of = []
+        for change in (up_change, down_change):
+            shards_of.append(
+                lax.psum_scatter(change, "fsdp", scatter_dimension=0, tiled=True)
+            )
+        expert_results[layer] = tuple(shards_of)
+        if not fused:
+            back_rows, down_change, up_change = lax.optimization_barrier(
+                (back_rows, down_change, up_change)
+            )
         back_picked = gates * (back_gates - jnp.sum(gates * back_gates, axis=-1, keepdims=True))
         back_logits = low(jnp.sum(jnp.where(chosen, back_picked[:, :, None], 0.0), axis=1))
         router_change = dot_first(normed_expert, back_logits)

time: 638 us -> 724 us (1.13)
  waiting for transfers between devices: 10.1 us -> 151 us
  matrix products: 118 us -> 62.2 us
    reduce_scatter x4, waiting for transfers between devices: 0.02 us -> 91.6 us  [per_device(): lax.psum_scatter(change, 'fsdp', scatter_dimension=0, tiled=True)]
    reduce_scatter x1, waiting for transfers between devices: 0.02 us -> 51.2 us  [per_device(): above = lax.psum_scatter(packed, 'fsdp', scatter_dimension=0)]
    dot_general x18 -> x14, matrix products: 71.3 us -> 23.2 us  [dot_first(): lax.dot_general(left, right, contract_first, preferred_element_type=jnp.f...]
    all_to_all x2, starting transfers between devices: 18.7 us -> 26.2 us  [exchange(): return lax.all_to_all(values, 'dp', split_axis=0, concat_axis=0, tiled=True)]
    unnamed x139 -> x167, local copies, waits for them, and re-layouts: 25.5 us -> 25.5 us
  transfers between devices with their start and end apart: 11 -> 11, of which waited for: 3 -> 6; matrix products, arithmetic and copies ran while one was open for 24% -> 13% of each run, Pallas kernels for 45% -> 28%
where the time goes in v6:
time: 724 us; the launch traced here: 719 us
  Pallas kernels  378 us (52%)
  waiting for transfers between devices  151 us (21%)
  matrix products  62.2 us (9%)
  local copies, waits for them, and re-layouts  59.8 us (8%)
  starting transfers between devices  26.8 us (4%)
  other arithmetic  26.5 us (4%)
  between operations  15.3 us (2%)
    pallas_call x3, Pallas kernels, experts_in_kernel(): pl.pallas_call(functools.partial(run_experts, mode, 512), out_shape=tuple...  238 us
    reduce_scatter x4, waiting for transfers between devices, per_device(): lax.psum_scatter(change, 'fsdp', scatter_dimension=0, tiled=True)  91.6 us
    pallas_call x1, Pallas kernels, reduce_in_kernel(): pl.pallas_call(functools.partial(reduce_mixer, chunks), out_shape=(jax.Sh...  80 us
    reduce_scatter x1, waiting for transfers between devices, per_device(): above = lax.psum_scatter(packed, 'fsdp', scatter_dimension=0)  51.2 us
    pallas_call x2, Pallas kernels, attention_backward(): pl.pallas_call(functools.partial(attend_back, pair, size ** (-0.5)), grid...  34.6 us
    all_to_all x2, starting transfers between devices, exchange(): return lax.all_to_all(values, 'dp', split_axis=0, concat_axis=0, tiled=True)  26.2 us
    unnamed x167, local copies, waits for them, and re-layouts  25.5 us
    pallas_call x2, Pallas kernels, attention_forward(): pl.pallas_call(functools.partial(attend, pair, size ** (-0.5)), grid=(gro...  25 us
  transfers between devices with their start and end apart: 11, of which 6 were waited for; matrix products, arithmetic and copies ran while one was open for 13% of the time, Pallas kernels for 28%

profile of v6, /device:TPU:0, one launch (start us, length us, event | category | flops | bytes accessed | tf_op | source)
XLA Modules:
  0.0 718.8 jit_solution(14737559174750214587)
XLA Ops:
  20.6 2.3 convolution_convert_fusion.4
  22.9 7.3 %all-to-all-start = ((bf16[8,144,768]{2,1,0:T(8,128)(2,1)}), bf16[8,144,768]{2,1,0:T(8,128)(2,1)}, u32[]{:S(2)}, u32[]{:S(2)}) async-start(bf16[8,144,768]{2,1,0:T(8,128)(2,1)} %bitcast.9), calls=%async_computation | async-start | bytes 3538944 | tf_op jit(solution)/shard_map/all_to_all | solution.py:860
  32.6 8.4 %slice_bitcast_fusion.1 = (bf16[768,3072]{1,0:T(8,128)(2,1)}, bf16[768,3072]{1,0:T(8,128)(2,1)}) fusion(bf16[2,1,768,3072]{3,2,1,0:T(8,128)(2,1)} %param.22), kind=kLoop, calls=%fused_computation.3 | loop fusion | bytes 18874368 | tf_op jit(solution)/shard_map/squeeze | solution.py:959
  41.0 8.2 %slice_bitcast_fusion = (bf16[3072,768]{1,0:T(8,128)(2,1)}, bf16[3072,768]{1,0:T(8,128)(2,1)}) fusion(bf16[2,1,3072,768]{3,2,1,0:T(8,128)(2,1)} %param.23), kind=kLoop, calls=%fused_computation.2 | loop fusion | bytes 18874368 | tf_op jit(solution)/shard_map/squeeze | solution.py:959
  52.1 4.1 convolution_convert_fusion.1.q_ref.k_ref.v_ref
  56.2 12.5 %attend.2 = (bf16[512,768]{1,0:T(8,128)(2,1)S(1)}, f32[512,768]{1,0:T(8,128)S(1)}) custom-call(bf16[512,2304]{1,0:T(8,128)(2,1)S(1)} %convolution_convert_fusion.1.q_ref.k_ref.v_ref, bf16[512,2304]{1,0:T(8,128)(2,1)S(1)} %convolution_convert_fusion.1.q_ref.k_ref.v_ref, bf16[512,2304]{1,0:T(8,128)(2,1)S(1)} %convolution_convert_fusion.1.q_ref.k_ref.v_ref, ...), custom_call_target="tpu_custom_call" | custom-call | flops 805306368 | bytes 4718592 | tf_op jit(solution)/shard_map/attend/pallas_call | solution.py:196
  71.6 2.4 multiply_reduce_fusion.8
  77.1 75.5 %shard_map.220 = (bf16[8,144,768]{2,1,0:T(8,128)(2,1)}, bf16[8,144,768]{2,1,0:T(8,128)(2,1)}, bf16[4,288,3072]{2,1,0:T(8,128)(2,1)}, bf16[4,288,3072]{2,1,0:T(8,128)(2,1)}) custom-call(bf16[8,144,768]{2,1,0:T(8,128)(2,1)} %bitcast.225, bf16[768,3072]{1,0:T(8,128)(2,1)} %get-tuple-element.172.refs_1_, bf16[3072,768]{1,0:T(8,128)(2,1)} %get-tuple-element.170.refs_2_), custom_call_target="tpu_custom_call" | custom-call | flops 108716359680 | bytes 28311552 | tf_op jit(solution)/shard_map/pallas_call | solution.py:814
  154.0 3.9 fusion.14
  167.3 12.5 %attend.3 = (bf16[512,768]{1,0:T(8,128)(2,1)S(1)}, f32[512,768]{1,0:T(8,128)S(1)}) custom-call(bf16[512,2304]{1,0:T(8,128)(2,1)S(1)} %convolution_convert_fusion.q_ref.k_ref.v_ref, bf16[512,2304]{1,0:T(8,128)(2,1)S(1)} %convolution_convert_fusion.q_ref.k_ref.v_ref, bf16[512,2304]{1,0:T(8,128)(2,1)S(1)} %convolution_convert_fusion.q_ref.k_ref.v_ref, ...), custom_call_target="tpu_custom_call" | custom-call | flops 805306368 | bytes 4718592 | tf_op jit(solution)/shard_map/attend/pallas_call | solution.py:196
  183.1 2.3 convolution_convert_fusion.2
  188.0 86.2 %shard_map.221 = (bf16[8,144,768]{2,1,0:T(8,128)(2,1)}, bf16[8,144,768]{2,1,0:T(8,128)(2,1)}, bf16[8,144,768]{2,1,0:T(8,128)(2,1)}, f32[8,1,256]{2,1,0:T(1,128)}...) custom-call(bf16[8,144,768]{2,1,0:T(8,128)(2,1)} %bitcast.222, bf16[768,3072]{1,0:T(8,128)(2,1)} %get-tuple-element.171.refs_1_, ...), custom_call_target="tpu_custom_call" | custom-call | flops 108716359680 | bytes 28311552 | tf_op jit(solution)/shard_map/pallas_call | solution.py:814
  274.3 18.9 %all-to-all-start.1 = ((bf16[8,144,768]{2,1,0:T(8,128)(2,1)}), bf16[8,144,768]{2,1,0:T(8,128)(2,1)}, u32[]{:S(2)}, u32[]{:S(2)}) async-start(bf16[8,144,768]{2,1,0:T(8,128)(2,1)} %get-tuple-element.64), calls=%async_computation.1 | async-start | bytes 3538944 | tf_op jit(solution)/shard_map/all_to_all | solution.py:860
  294.0 3.3 fusion.106
  302.5 17.3 %attend_back.2 = (bf16[512,768]{1,0:T(8,128)(2,1)S(1)}, bf16[512,768]{1,0:T(8,128)(2,1)S(1)}, bf16[512,768]{1,0:T(8,128)(2,1)S(1)}, f32[6,2,1024]{2,1,0:T(2,128)S(1)}) custom-call(bf16[512,2304]{1,0:T(8,128)(2,1)S(1)} %convolution_convert_fusion.q_ref.k_ref.v_ref, bf16[512,2304]{1,0:T(8,128)(2,1)S(1)} %convolution_convert_fusion.q_ref.k_ref.v_ref, ...), custom_call_target="tpu_custom_call" | custom-call | flops 2013265920 | bytes 7864320 | tf_op jit(solution)/shard_map/attend_back/pallas_call | solution.py:220
  321.6 5.4 all-to-all-done.1
  327.0 9.7 %reduce-scatter.6.cloned.1.call-done = bf16[768,768]{1,0:T(8,128)(2,1)} async-done(((bf16[3072,768]{1,0:T(8,128)(2,1)}), bf16[768,768]{1,0:T(8,128)(2,1)}) %reduce-scatter.6.cloned.1.call-update) | async-done | bytes 1179664 | tf_op jit(solution)/shard_map/reduce_scatter | solution.py:1121
  336.7 2.4 fusion.42
  341.3 2.6 multiply_reduce_fusion.3
  345.9 3.4 fusion.6
  349.3 76.4 %shard_map.222 = (bf16[8,144,768]{2,1,0:T(8,128)(2,1)}, bf16[8,144,768]{2,1,0:T(8,128)(2,1)}, bf16[768,3072]{1,0:T(8,128)(2,1)}, bf16[3072,768]{1,0:T(8,128)(2,1)}) custom-call(bf16[8,144,768]{2,1,0:T(8,128)(2,1)} %bitcast.224, bf16[768,3072]{1,0:T(8,128)(2,1)} %get-tuple-element.172.refs_1_, bf16[3072,768]{1,0:T(8,128)(2,1)} %get-tuple-element.170.refs_2_, ...), custom_call_target="tpu_custom_call" | custom-call | flops 108716359680 | bytes 28311552 | tf_op jit(solution)/shard_map/pallas_call | solution.py:814
  428.0 3.3 convolution_convert_fusion.9
  441.9 4.0 fusion.15
  448.0 35.6 %reduce-scatter.14.cloned.1.call-done = bf16[768,768]{1,0:T(8,128)(2,1)} async-done(((bf16[3072,768]{1,0:T(8,128)(2,1)}), bf16[768,768]{1,0:T(8,128)(2,1)}) %reduce-scatter.14.cloned.1.call-update) | async-done | bytes 1179664 | tf_op jit(solution)/shard_map/reduce_scatter | solution.py:1121
  483.7 4.3 fusion.8
  488.0 46.2 %reduce-scatter.8.cloned.1.call-done = bf16[192,3072]{1,0:T(8,128)(2,1)} async-done(((bf16[768,3072]{1,0:T(8,128)(2,1)}), bf16[192,3072]{1,0:T(8,128)(2,1)}) %reduce-scatter.8.cloned.1.call-update) | async-done | bytes 1179664 | tf_op jit(solution)/shard_map/reduce_scatter | solution.py:1121
  534.2 51.2 %reduce-scatter.10.cloned.1.call-done = bf16[1,784,768]{2,1,0:T(8,128)(2,1)} async-done(((bf16[4,784,768]{2,1,0:T(8,128)(2,1)}), bf16[1,784,768]{2,1,0:T(8,128)(2,1)}) %reduce-scatter.10.cloned.1.call-update) | async-done | bytes 1204240 | tf_op jit(solution)/shard_map/reduce_scatter | solution.py:1180
  592.3 17.3 %attend_back.3 = (bf16[512,768]{1,0:T(8,128)(2,1)S(1)}, bf16[512,768]{1,0:T(8,128)(2,1)S(1)}, bf16[512,768]{1,0:T(8,128)(2,1)S(1)}, f32[6,2,1024]{2,1,0:T(2,128)S(1)}) custom-call(bf16[512,2304]{1,0:T(8,128)(2,1)S(1)} %copy-done.1, bf16[512,2304]{1,0:T(8,128)(2,1)S(1)} %copy-done.1, bf16[512,2304]{1,0:T(8,128)(2,1)S(1)} %copy-done.1, ...), custom_call_target="tpu_custom_call" | custom-call | flops 2013265920 | bytes 7864320 | tf_op jit(solution)/shard_map/attend_back/pallas_call | solution.py:220
  611.6 2.3 fusion.28
  619.3 80.0 %reduce_mixer.1 = (f32[4,2,192,768]{3,2,1,0:T(8,128)}, f32[2,16,768]{2,1,0:T(8,128)S(1)}) custom-call(bf16[4,192,768]{2,1,0:T(8,128)(2,1)S(1)} %bitcast.182, bf16[4,192,768]{2,1,0:T(8,128)(2,1)S(1)} %bitcast.183, bf16[4,192,768]{2,1,0:T(8,128)(2,1)S(1)} %bitcast.184, bf16[4,192,768]{2,1,0:T(8,128)(2,1)S(1)} %bitcast.180, bf16[4,16,768]{2,1,0:T(8,128)(2,1)S(1)} %bitcast.185, ...), custom_call_target="tpu_custom_call" | custom-call | tf_op jit(solution)/shard_map/reduce_mixer/pallas_call | solution.py:513
  701.6 4.6 slice_bitcast_fusion.4
  706.2 4.2 fusion.7
  (326 shorter events, 85.4 us)
Async XLA Ops:
  7.2 4.5 copy-start.54
  7.2 4.5 copy-start.55
  7.2 42.0 %all-gather.7.cloned.1.call-start = ((), (), s32[]{:S(2)}) async-start(), calls=%async_computation.7 | async-start | bytes 4669440 | tf_op jit(solution)/shard_map/all_gather | solution.py:934
  12.9 58.7 %all-gather.11.cloned.1.call-start = ((), (), s32[]{:S(2)}) async-start(), calls=%async_computation.14 | async-start | bytes 1474560 | tf_op jit(solution)/shard_map/all_gather | solution.py:935
  14.0 145.5 %all-gather.13.cloned.1.call-start = ((), (), s32[]{:S(2)}) async-start(), calls=%async_computation.15 | async-start | bytes 1474560 | tf_op jit(solution)/shard_map/all_gather | solution.py:935
  20.6 54.2 %copy-start.31 = (bf16[1152,512]{1,0:T(8,128)(2,1)}, bf16[1152,512]{1,0:T(8,128)(2,1)S(1)}, u32[]{:S(2)}) copy-start(bf16[1152,512]{1,0:T(8,128)(2,1)S(1)} %slice_add_fusion) | copy-start | bytes 3538948
  22.9 48.7 %all-to-all-start = ((bf16[8,144,768]{2,1,0:T(8,128)(2,1)}), bf16[8,144,768]{2,1,0:T(8,128)(2,1)}, u32[]{:S(2)}, u32[]{:S(2)}) async-start(bf16[8,144,768]{2,1,0:T(8,128)(2,1)} %bitcast.9), calls=%async_computation | async-start | bytes 3538944 | tf_op jit(solution)/shard_map/all_to_all | solution.py:860
  30.3 129.3 %all-gather.9.cloned.1.call-start = ((), (), s32[]{:S(2)}) async-start(), calls=%async_computation.8 | async-start | bytes 4669440 | tf_op jit(solution)/shard_map/all_gather | solution.py:934
  31.5 305.2 %reduce-scatter.6.cloned.1.call-start = ((), (), s32[]{:S(2)}) async-start(), calls=%async_computation.9 | async-start | bytes 5898240 | tf_op jit(solution)/shard_map/reduce_scatter | solution.py:1121
  31.7 135.4 %copy-start.59 = (s32[1024]{0:T(1024)}, s32[1024]{0:T(1024)S(1)}, u32[]{:S(2)}) copy-start(s32[1024]{0:T(1024)S(1)} %select_add_fusion) | copy-start | bytes 12292
  32.6 19.5 %copy-start.71 = (f32[512]{0:T(512)}, f32[512]{0:T(512)S(1)}, u32[]{:S(2)}) copy-start(f32[512]{0:T(512)S(1)} %get-tuple-element.196) | copy-start | bytes 6148
  50.7 5.5 copy-start.11
  52.1 4.1 copy-start.65
  52.1 22.5 %copy-start.61 = (f32[768]{0:T(1024)}, f32[768]{0:T(1024)S(1)}, u32[]{:S(2)}) copy-start(f32[768]{0:T(1024)S(1)} %get-tuple-element.154) | copy-start | bytes 9220
  74.0 84.0 %copy-start.23 = (f32[512,768]{1,0:T(8,128)}, f32[512,768]{1,0:T(8,128)S(1)}, u32[]{:S(2)}) copy-start(f32[512,768]{1,0:T(8,128)S(1)} %get-tuple-element.208) | copy-start | bytes 4718596
  74.8 77.7 %copy-start.36 = (bf16[512,768]{1,0:T(8,128)(2,1)}, bf16[512,768]{1,0:T(8,128)(2,1)S(1)}, u32[]{:S(2)}) copy-start(bf16[512,768]{1,0:T(8,128)(2,1)S(1)} %multiply_convert_fusion.4) | copy-start | bytes 2359300
  153.9 4.0 copy-start.57
  167.3 12.5 %copy-start.18 = (f32[512,768]{1,0:T(8,128)S(1)}, f32[512,768]{1,0:T(8,128)}, u32[]{:S(2)}) copy-start(f32[512,768]{1,0:T(8,128)} %copy-done.17) | copy-start | bytes 4718596
  167.3 12.5 %copy-start.47 = (bf16[1,768,768]{2,1,0:T(8,128)(2,1)S(1)}, bf16[1,768,768]{2,1,0:T(8,128)(2,1)}, u32[]{:S(2)}) copy-start(bf16[1,768,768]{2,1,0:T(8,128)(2,1)} %all-gather.13.cloned.1.call-done) | copy-start | bytes 3538948
  181.3 4.1 copy-start.20
  274.3 18.9 %copy-start.75 = (f32[8,1,256]{2,1,0:T(1,128)S(1)}, f32[8,1,256]{2,1,0:T(1,128)}, u32[]{:S(2)}) copy-start(f32[8,1,256]{2,1,0:T(1,128)} %get-tuple-element.62) | copy-start | bytes 24580
  274.3 52.7 %all-to-all-start.1 = ((bf16[8,144,768]{2,1,0:T(8,128)(2,1)}), bf16[8,144,768]{2,1,0:T(8,128)(2,1)}, u32[]{:S(2)}, u32[]{:S(2)}) async-start(bf16[8,144,768]{2,1,0:T(8,128)(2,1)} %get-tuple-element.64), calls=%async_computation.1 | async-start | bytes 3538944 | tf_op jit(solution)/shard_map/all_to_all | solution.py:860
  293.2 190.5 %reduce-scatter.14.cloned.1.call-start = ((), (), s32[]{:S(2)}) async-start(), calls=%async_computation.13 | async-start | bytes 5898240 | tf_op jit(solution)/shard_map/reduce_scatter | solution.py:1121
  425.8 108.4 %reduce-scatter.8.cloned.1.call-start = ((), (), s32[]{:S(2)}) async-start(), calls=%async_computation.10 | async-start | bytes 5898240 | tf_op jit(solution)/shard_map/reduce_scatter | solution.py:1121
  426.5 158.9 %reduce-scatter.10.cloned.1.call-start = ((), (), s32[]{:S(2)}) async-start(), calls=%async_computation.11 | async-start | bytes 6021120 | tf_op jit(solution)/shard_map/reduce_scatter | solution.py:1180
  441.2 265.1 %reduce-scatter.12.cloned.1.call-start = ((), (), s32[]{:S(2)}) async-start(), calls=%async_computation.12 | async-start | bytes 5898240 | tf_op jit(solution)/shard_map/reduce_scatter | solution.py:1121
  441.9 4.1 copy-start.22
  483.7 101.7 %copy-start.33 = (bf16[1152,512]{1,0:T(8,128)(2,1)S(1)}, bf16[1152,512]{1,0:T(8,128)(2,1)}, u32[]{:S(2)}) copy-start(bf16[1152,512]{1,0:T(8,128)(2,1)} %copy-done.31) | copy-start | bytes 3538948
  483.7 101.7 %copy-start.44 = (bf16[8,144,768]{2,1,0:T(8,128)(2,1)S(1)}, bf16[8,144,768]{2,1,0:T(8,128)(2,1)}, u32[]{:S(2)}) copy-start(bf16[8,144,768]{2,1,0:T(8,128)(2,1)} %get-tuple-element.79) | copy-start | bytes 5308420
  592.3 17.3 %copy-start.45 = (bf16[768,2432]{1,0:T(8,128)(2,1)S(1)}, bf16[768,2432]{1,0:T(8,128)(2,1)}, u32[]{:S(2)}) copy-start(bf16[768,2432]{1,0:T(8,128)(2,1)} %all-gather.7.cloned.1.call-done) | copy-start | bytes 11206660
  706.2 4.2 copy-start.40
  706.2 4.2 copy-start.73
  (56 other events, 99.5 us)
Sparse Core Ops, SparseCore 0:
  13.0 34.5 all-gather.6
  49.7 17.4 all-gather.10
  69.3 17.4 all-gather.12
  88.8 32.0 all-gather.8
  274.4 62.2 reduce-scatter.5
  425.9 57.7 reduce-scatter.13
  486.2 47.9 reduce-scatter.7
  536.7 48.5 reduce-scatter.9
  587.9 55.0 reduce-scatter.11
